TPU v7x, 256 devices: a whole 4x4x8 slice. The times are simulated.
256 devices in a mesh: section: 16 (over y, z_hi, core), dp: 16 (over x, z_lo).
Axes of the slice: x: 4, y: 4, z: 8 (z_hi: 2, z_lo: 4; z = z_hi * 4 + z_lo), core: 2. Of those that a mesh axis runs over, the one named last changes fastest.
Arguments:
- student_states: bfloat16 [16, 2048, 2048], P('section', 'dp'), may hold values from -6 to 6
- teacher_states: bfloat16 [64, 2048, 7168], P('section', 'dp'), may hold values from -18 to 18
- projector: bfloat16 [16, 2048, 7168], P('section', None, 'dp'), may hold values from -0.125 to 0.125
- layer_map: int32 [16], replicated, may hold values from 0 to 60, as said below
- boundaries: int32 [17], replicated, may hold values from 0 to 61, as said below
- valid_counts: int32 [16], P('dp'), may hold values from 32 to 128, as said below
Outputs:
- student_grads: bfloat16 [16, 2048, 2048], P('section', 'dp')
- projector_grads: bfloat16 [16, 2048, 7168], P('section', None, 'dp')
- layer_losses: float32 [16], P('section')
Inputs may be any that keep to these rules, and one draw needn't show every extreme that they name: Section k holds 4 or 3 teacher layers, three sections the smaller number; boundaries[0] is 0 and boundaries[16] is 61. Teacher layer layer_map[l] lies on a section from l - 2 to l + 2; student layers 0 and 15 pair with layers of sections 1 and 14, student layers 1 and 14 with layers of sections 3 and 12. `valid_counts`: the valid tokens stand first in their micro-batch; the last micro-batch is full.
All inputs are finite; a program needn't handle non-finite values.
Results may differ from a plain program's by a relative error of at most 0.015.
Values may be sent and summed in bfloat16 or wider, within the bound.
No kernel may reach another device: no remote copies, remote signals or barrier semaphores. Data moves between devices by JAX's collectives and lax.ppermute only.
A program may use at most 128 MiB of HBM per device.

v0:
```python
import jax
import jax.numpy as jnp
from jax import lax
from jax.experimental import pallas as pl
from jax.experimental.pallas import tpu as pltpu
from jax.sharding import Mesh
from jax.sharding import PartitionSpec as P

loss_scale = 128.0
norm_eps = 1e-06


SECTION = ("y", "zh", "core")
DP = ("x", "zl")
ROWS = 32


def rotate(block, axis, distance):
    n = lax.axis_size(axis)
    return lax.ppermute(block, axis, [(i, (i + distance) % n) for i in range(n)])


def exchange(block, axis, bit):
    n = lax.axis_size(axis)
    return lax.ppermute(block, axis, [(i, i ^ bit) for i in range(n)])


def prepare_body(places, order, limit, rows, out):
    wide = rows[0].astype(jnp.float32)
    scale = lax.rsqrt(jnp.mean(wide * wide, axis=1, keepdims=True) + norm_eps)
    token = pl.program_id(1) * wide.shape[0] + lax.broadcasted_iota(jnp.int32, scale.shape, 0)
    scale = jnp.where(token < limit[0], scale, 0.0)
    chunks, zs = out.shape[1], out.shape[2]
    group = wide.shape[1] // order.shape[0]
    width = group // zs
    for chunk in range(chunks):
        halves = []
        for half in range(2):
            start = pl.multiple_of(order[2 * chunk + half] * group, group)
            piece = rows[0, :, pl.ds(start, group)].astype(jnp.float32)
            halves.append((piece * scale).astype(jnp.bfloat16))
        for z in range(zs):
            cut = slice(z * width, (z + 1) * width)
            out[0, chunk, z] = jnp.concatenate([h[:, cut] for h in halves], axis=1)


def prepare(teacher, places, order, limit):
    _, tokens, features = teacher.shape
    pieces = places.shape[0]
    rows = min(ROWS, tokens)
    wide = features // 8
    return pl.pallas_call(
        prepare_body,
        out_shape=jax.ShapeDtypeStruct((pieces, 2, 4, tokens, wide), jnp.bfloat16),
        grid_spec=pltpu.PrefetchScalarGridSpec(
            num_scalar_prefetch=3,
            grid=(pieces, tokens // rows),
            in_specs=[pl.BlockSpec((1, rows, features), lambda k, i, places, order, limit: (places[k], i, 0))],
            out_specs=pl.BlockSpec((1, 2, 4, rows, wide), lambda k, i, places, order, limit: (k, 0, 0, i, 0)),
        ),
        compiler_params=pltpu.CompilerParams(dimension_semantics=("arbitrary", "arbitrary")),
    )(places, order, limit, teacher)


def dot(a, b, ca, cb):
    return lax.dot_general(a, b, (((ca,), (cb,)), ((), ())), preferred_element_type=jnp.float32)


def compute(student_states, teacher_states, projector, layer_map, boundaries, valid_counts):
    y, zh, core = (lax.axis_index(a) for a in SECTION)
    x, zl = (lax.axis_index(a) for a in DP)
    sections = lax.axis_size(SECTION)
    chip = 2 * y + zh
    here = 2 * chip + core
    weights = projector[0]
    tokens = student_states.shape[1]
    half = weights.shape[0] // 2
    width = weights.shape[1]

    valid = lax.broadcasted_iota(jnp.int32, (tokens, 1), 0) < valid_counts[0]
    student = jnp.where(valid, student_states[0], 0)
    students = [student]
    for k in (1, 2, 3):
        students.append(rotate(student, "zl", k))
    w_prev = rotate(weights, "x", 1)
    w_next = rotate(weights, "x", -1)

    owners = jnp.sum((boundaries[None, 1:sections] <= layer_map[:, None]).astype(jnp.int32), axis=1)
    layers = jnp.arange(sections, dtype=jnp.int32)
    across = 2 * (2 * y + 1 - zh) + core
    beyond = jnp.where(zh == 0, 2 * (chip - 1), 2 * (chip + 1)) + core
    aside = jnp.where(core == 1, 2 * (chip + 1), 2 * chip - 1)
    sibling = 2 * chip + 1 - core
    wanted = jnp.stack([sibling, aside, here, across, beyond])
    hit = layers[None, :] == wanted[:, None]
    owner_of = jnp.sum(jnp.where(hit, owners[None, :], 0), axis=1)
    first = jnp.sum(jnp.where(jnp.arange(sections + 1) == here, boundaries, 0))
    places = jnp.sum(jnp.where(hit, layer_map[None, :], 0), axis=1) - first
    places = jnp.clip(places, 0, teacher_states.shape[0] - 1)
    order = jnp.stack([(x + 2) & 3, (x + 1) & 3, (x + 3) & 3, x]).astype(jnp.int32)
    own_owner, across_owner, beyond_owner = owner_of[2], owner_of[3], owner_of[4]
    own_here = own_owner == here
    across_here = across_owner == here
    beyond_here = beyond_owner == here
    across_near = across_owner >> 1 == chip
    own_near = own_owner >> 1 == chip

    given = prepare(teacher_states, places[:2], order, valid_counts)
    from_sibling = exchange(given, "core", 1)
    kept = prepare(teacher_states, places[2:], order, valid_counts)

    y_route = [((i, 0), (i - 1, 0)) for i in range(1, 4)] + [((i, 1), (i + 1, 1)) for i in range(3)]
    y_route = [(a * 2 + b, c * 2 + d) for (a, b), (c, d) in y_route]
    relayed = []
    for chunk in range(2):
        moved = jnp.where(beyond_here, kept[2, chunk], from_sibling[1, chunk])
        relayed.append(lax.ppermute(moved, ("y", "zh"), y_route))

    def slab(array, index, axis=0):
        return lax.dynamic_index_in_dim(array, index, axis, keepdims=False)

    own = []
    for k in range(4):
        place = (zl + k) & 3
        both = jnp.where(own_here, slab(kept[0], place, 1), slab(from_sibling[0], place, 1))
        own.append(rotate(both, "zl", k) if k else both)
    crossed = []
    for chunk in range(2):
        for k in range(4):
            place = (zl + k) & 3
            cross = jnp.where(
                across_near,
                jnp.where(across_here, slab(kept[1, chunk], place), slab(from_sibling[1, chunk], place)),
                slab(relayed[chunk], place),
            )
            route = [(h * 4 + z, (1 - h) * 4 + (z + k) % 4) for h in range(2) for z in range(4)]
            crossed.append(lax.ppermute(cross, ("zh", "zl"), route))

    w_opp_top = rotate(w_prev[:half], "x", 1)
    w_opp_bot = rotate(w_next[half:], "x", -1)
    rows = jnp.concatenate(students, axis=0)

    w_first = jnp.concatenate([jnp.concatenate([w_opp_top, w_opp_bot], axis=0), w_next], axis=1)
    w_second = jnp.concatenate([w_prev, weights], axis=1)

    def residual_of(chunk, own, w):
        blocks = [jnp.where(own_near, own[k][chunk], crossed[4 * chunk + k]) for k in range(4)]
        target = jnp.concatenate(blocks, axis=0)
        residual = dot(rows, w, 1, 0) - target.astype(jnp.float32)
        return jnp.sum(residual * residual), residual.astype(jnp.bfloat16)

    squares_first, first_res = residual_of(0, own, w_first)
    own, first_res = lax.optimization_barrier((own, first_res))
    pair = dot(rows, first_res, 0, 0).astype(jnp.bfloat16)
    part_first = dot(first_res, w_first, 1, 1)
    up_top = rotate(pair[:half, :width], "x", 1)
    down_bot = rotate(pair[half:, :width], "x", -1)
    squares_second, second_res = residual_of(1, own, w_second)

    sums = jnp.stack([squares_first + squares_second, valid_counts[0].astype(jnp.float32)])
    copies = jnp.broadcast_to(sums, (lax.axis_size(DP), 2))
    sums = jnp.sum(lax.all_to_all(copies, DP, split_axis=0, concat_axis=0, tiled=True), axis=0)
    total = sums[1]
    loss = sums[:1] / (total * (width * lax.axis_size(DP)))
    factor = loss_scale / total

    next_part = pair[:, width:].astype(jnp.float32)
    next_part = jnp.concatenate([next_part[:half] + up_top.astype(jnp.float32), next_part[half:]], axis=0)
    next_part = lax.optimization_barrier((next_part.astype(jnp.bfloat16), sums))[0]
    from_prev = rotate(next_part, "x", 1)
    prev_part = dot(rows, second_res[:, :width], 0, 0)
    prev_part = jnp.concatenate([prev_part[:half], prev_part[half:] + down_bot.astype(jnp.float32)], axis=0)
    prev_part = lax.optimization_barrier((prev_part.astype(jnp.bfloat16), sums))[0]
    from_next = rotate(prev_part, "x", -1)

    student_part = (part_first + dot(second_res, w_second, 1, 1)).astype(jnp.bfloat16)
    student_part = lax.optimization_barrier((student_part, sums))[0]
    returned = []
    for k in (1, 2, 3):
        part = student_part[k * tokens : (k + 1) * tokens]
        returned.append(rotate(part, "zl", -k))

    student_grad = student_part[:tokens].astype(jnp.float32)
    for part in returned:
        student_grad = student_grad + part.astype(jnp.float32)
    student_grad = (student_grad * factor).astype(jnp.bfloat16)
    projector_grad = dot(rows, second_res[:, width:], 0, 0) + from_prev.astype(jnp.float32) + from_next.astype(jnp.float32)
    projector_grad = (projector_grad * factor).astype(jnp.bfloat16)
    return (student_grad[None], projector_grad[None], loss)


def solution(mesh):
    split = Mesh(mesh.devices.reshape(4, 2, 2, 4, 4), SECTION + DP)
    return jax.shard_map(
        compute,
        mesh=split,
        in_specs=(
            P(SECTION, DP, None),
            P(SECTION, DP, None),
            P(SECTION, None, DP),
            P(),
            P(),
            P(DP),
        ),
        out_specs=(P(SECTION, DP, None), P(SECTION, None, DP), P(SECTION)),
        check_vma=False,
    )
```

profile of v0, /device:TPU:47, one launch (start us, length us, event | category | flops | bytes accessed | tf_op | source)
XLA Modules:
  0.0 315.0 jit_solution(16863985663459604730)
XLA Ops:
  1.4 1.3 fusion.18
  6.9 8.3 %shard_map.86 = bf16[2,2,4,128,896]{4,3,2,1,0:T(8,128)(2,1)} custom-call(s32[2]{0:T(128)} %bitcast.119, s32[4]{0:T(128)} %pad_add_fusion.order, s32[1]{0:T(128)} %copy.27.limit, bf16[4,128,7168]{2,1,0:T(8,128)(2,1)} %rows.3), custom_call_target="tpu_custom_call" | custom-call | tf_op jit(solution)/shard_map/pallas_call | solution.py:52
  16.4 2.1 collective-permute-start.7
  19.1 11.3 %shard_map.85 = bf16[3,2,4,128,896]{4,3,2,1,0:T(8,128)(2,1)} custom-call(s32[3]{0:T(128)} %slice.145.places, s32[4]{0:T(128)} %pad_add_fusion.order, s32[1]{0:T(128)} %copy.27.limit, bf16[4,128,7168]{2,1,0:T(8,128)(2,1)} %rows.3), custom_call_target="tpu_custom_call" | custom-call | tf_op jit(solution)/shard_map/pallas_call | solution.py:52
  31.8 4.8 %fusion.23 = (bf16[1,1,4,128,896]{4,3,2,1,0:T(8,128)(2,1)}, bf16[1,1,4,128,896]{4,3,2,1,0:T(8,128)(2,1)S(1)}, bf16[4,128,896]{2,1,0:T(8,128)(2,1)}, bf16[4,128,8...) fusion(bf16[3,2,4,128,896]{4,3,2,1,0:T(8,128)(2,1)} %shard_map.85, ...), kind=kLoop, calls=%fused_computation.71 | loop fusion | flops 917504 | bytes 11010049 | tf_op jit(solution)/shard_map/slice | solution.py:133
  36.6 2.1 collective-permute-start.11
  38.7 1.9 collective-permute-start.16
  42.8 1.6 slice.183
  45.7 1.6 collective-permute-start.1
  47.4 12.8 %collective-permute-done.11 = bf16[4,128,896]{2,1,0:T(8,128)(2,1)} collective-permute-done((bf16[4,128,896]{2,1,0:T(8,128)(2,1)}, bf16[4,128,896]{2,1,0:T(8,128)(2,1)}, u32[]{:S(2)}, u32[]{:S(2)}) %collective-permute-start.11) | collective-permute-done | bytes 917536 | tf_op jit(solution)/shard_map/ppermute | solution.py:117
  60.2 3.0 collective-permute-start.2
  63.2 2.4 bitcast_select_fusion.16
  65.5 5.4 %collective-permute-start.15 = (bf16[128,896]{1,0:T(8,128)(2,1)}, bf16[128,896]{1,0:T(8,128)(2,1)S(1)}, u32[]{:S(2)}, u32[]{:S(2)}) collective-permute-start(bf16[128,896]{1,0:T(8,128)(2,1)} %get-tuple-element.41), channel_id=1, source_target_pairs={{0,35},{1,32},{2,33},{3,34},{32,3},{33,0},{34,1},{35,2},{4,39},{5,... | collective-permute-start | bytes 688136 | tf_op jit(solution)/shard_map/ppermute | solution.py:137
  72.5 1.3 slice.185
  75.1 4.7 %collective-permute-done.16 = bf16[4,128,896]{2,1,0:T(8,128)(2,1)} collective-permute-done((bf16[4,128,896]{2,1,0:T(8,128)(2,1)}, bf16[4,128,896]{2,1,0:T(8,128)(2,1)}, u32[]{:S(2)}, u32[]{:S(2)}) %collective-permute-start.16) | collective-permute-done | bytes 917536 | tf_op jit(solution)/shard_map/ppermute | solution.py:117
  79.8 1.4 bitcast_select_fusion.11
  81.3 2.8 collective-permute-start.8
  84.0 13.9 %collective-permute-done.2 = bf16[2,128,896]{2,1,0:T(8,128)(2,1)} collective-permute-done((bf16[2,128,896]{2,1,0:T(8,128)(2,1)}, bf16[2,128,896]{2,1,0:T(8,128)(2,1)}, u32[]{:S(2)}, u32[]{:S(2)}) %collective-permute-start.2) | collective-permute-done | bytes 458784 | tf_op jit(solution)/shard_map/ppermute | solution.py:20
  97.9 5.2 %collective-permute-start.14 = (bf16[128,896]{1,0:T(8,128)(2,1)S(1)}, bf16[128,896]{1,0:T(8,128)(2,1)S(1)}, u32[]{:S(2)}, u32[]{:S(2)}) collective-permute-start(bf16[128,896]{1,0:T(8,128)(2,1)S(1)} %copy-done.10), channel_id=1, source_target_pairs={{0,34},{1,35},{2,32},{3,33},{32,2},{33,3},{34,0},{35,1},{4,38},{5,... | collective-permute-start | bytes 688136 | tf_op jit(solution)/shard_map/ppermute | solution.py:137
  103.2 3.9 %collective-permute-start.12 = (bf16[128,896]{1,0:T(8,128)(2,1)S(1)}, bf16[128,896]{1,0:T(8,128)(2,1)S(1)}, u32[]{:S(2)}, u32[]{:S(2)}) collective-permute-start(bf16[128,896]{1,0:T(8,128)(2,1)S(1)} %copy-done.8), channel_id=1, source_target_pairs={{0,32},{1,33},{2,34},{3,35},{32,0},{33,1},{34,2},{35,3},{4,36},{5,... | collective-permute-start | bytes 688136 | tf_op jit(solution)/shard_map/ppermute | solution.py:137
  108.0 19.1 %collective-permute-done.14 = bf16[128,896]{1,0:T(8,128)(2,1)S(1)} collective-permute-done((bf16[128,896]{1,0:T(8,128)(2,1)S(1)}, bf16[128,896]{1,0:T(8,128)(2,1)S(1)}, u32[]{:S(2)}, u32[]{:S(2)}) %collective-permute-start.14) | collective-permute-done | bytes 229408 | tf_op jit(solution)/shard_map/ppermute | solution.py:137
  127.2 7.9 %collective-permute-done.13 = bf16[128,896]{1,0:T(8,128)(2,1)S(1)} collective-permute-done((bf16[128,896]{1,0:T(8,128)(2,1)S(1)}, bf16[128,896]{1,0:T(8,128)(2,1)S(1)}, u32[]{:S(2)}, u32[]{:S(2)}) %collective-permute-start.13) | collective-permute-done | bytes 229408 | tf_op jit(solution)/shard_map/ppermute | solution.py:137
  137.5 8.9 %collective-permute-done.6 = bf16[128,2048]{1,0:T(8,128)(2,1)S(1)} collective-permute-done((bf16[128,2048]{1,0:T(8,128)(2,1)S(1)}, bf16[128,2048]{1,0:T(8,128)(2,1)S(1)}, u32[]{:S(2)}, u32[]{:S(2)}) %collective-permute-start.6) | collective-permute-done | bytes 524320 | tf_op jit(solution)/shard_map/ppermute | solution.py:20
  146.4 18.4 %collective-permute-done.5 = bf16[128,2048]{1,0:T(8,128)(2,1)S(1)} collective-permute-done((bf16[128,2048]{1,0:T(8,128)(2,1)S(1)}, bf16[128,2048]{1,0:T(8,128)(2,1)S(1)}, u32[]{:S(2)}, u32[]{:S(2)}) %collective-permute-start.5) | collective-permute-done | bytes 524320 | tf_op jit(solution)/shard_map/ppermute | solution.py:20
  164.8 4.6 %collective-permute-start.19 = (bf16[128,896]{1,0:T(8,128)(2,1)S(1)}, bf16[128,896]{1,0:T(8,128)(2,1)S(1)}, u32[]{:S(2)}, u32[]{:S(2)}) collective-permute-start(bf16[128,896]{1,0:T(8,128)(2,1)S(1)} %get-tuple-element.38), channel_id=1, source_target_pairs={{0,34},{1,35},{2,32},{3,33},{32,2},{33,3},{34,0},{35,1},{4,38},{5,... | collective-permute-start | bytes 688136 | tf_op jit(solution)/shard_map/ppermute | solution.py:137
  169.3 6.7 %collective-permute-done.4 = bf16[128,2048]{1,0:T(8,128)(2,1)S(1)} collective-permute-done((bf16[128,2048]{1,0:T(8,128)(2,1)S(1)}, bf16[128,2048]{1,0:T(8,128)(2,1)S(1)}, u32[]{:S(2)}, u32[]{:S(2)}) %collective-permute-start.4) | collective-permute-done | bytes 524320 | tf_op jit(solution)/shard_map/ppermute | solution.py:20
  176.0 8.5 %collective-permute-start.18 = (bf16[128,896]{1,0:T(8,128)(2,1)S(1)}, bf16[128,896]{1,0:T(8,128)(2,1)S(1)}, u32[]{:S(2)}, u32[]{:S(2)}) collective-permute-start(bf16[128,896]{1,0:T(8,128)(2,1)S(1)} %get-tuple-element.39), channel_id=1, source_target_pairs={{0,33},{1,34},{2,35},{3,32},{32,1},{33,2},{34,3},{35,0},{4,37},{5,... | collective-permute-start | bytes 688136 | tf_op jit(solution)/shard_map/ppermute | solution.py:137
  184.5 4.1 %collective-permute-start.17 = (bf16[128,896]{1,0:T(8,128)(2,1)S(1)}, bf16[128,896]{1,0:T(8,128)(2,1)S(1)}, u32[]{:S(2)}, u32[]{:S(2)}) collective-permute-start(bf16[128,896]{1,0:T(8,128)(2,1)S(1)} %get-tuple-element.36), channel_id=1, source_target_pairs={{0,32},{1,33},{2,34},{3,35},{32,0},{33,1},{34,2},{35,3},{4,36},{5,... | collective-permute-start | bytes 688136 | tf_op jit(solution)/shard_map/ppermute | solution.py:137
  188.7 4.9 %multiply_reduce_fusion.1 = (f32[]{:T(128)}, bf16[512,896]{1,0:T(8,128)(2,1)S(1)}) fusion(bf16[128,896]{1,0:T(8,128)(2,1)S(1)} %fusion.14, bf16[128,896]{1,0:T(8,128)(2,1)S(1)} %fusion.15, bf16[128,896]{1,0:T(8,128)(2,1)S(1)} %fusion.16, bf16[128,896]{1,0:T(8,128)(2,1)S(1)} %fusion.17, bf16[2048,448]{0,1:T(8,128)(2,1)} %collective-permute-done.9, ...), kind=kOutput, calls=%fused_computation.16 | convolution fusion | flops 1903951872 | bytes 7602180 | tf_op jit(solution)/shard_map/dot_general | solution.py:66
  194.5 2.1 convolution_convert_fusion
  196.7 1.8 fusion.24
  200.4 17.8 %collective-permute-done.18 = bf16[128,896]{1,0:T(8,128)(2,1)S(1)} collective-permute-done((bf16[128,896]{1,0:T(8,128)(2,1)S(1)}, bf16[128,896]{1,0:T(8,128)(2,1)S(1)}, u32[]{:S(2)}, u32[]{:S(2)}) %collective-permute-start.18) | collective-permute-done | bytes 229408 | tf_op jit(solution)/shard_map/ppermute | solution.py:137
  219.3 6.0 %multiply_reduce_fusion = (f32[]{:T(128)}, bf16[512,896]{1,0:T(8,128)(2,1)}) fusion(bf16[128,896]{1,0:T(8,128)(2,1)S(1)} %bitcast_select_fusion.6, bf16[128,896]{1,0:T(8,128)(2,1)S(1)} %bitcast_select_fusion.8, bf16[128,896]{1,0:T(8,128)(2,1)S(1)} %bitcast_select_fusion.10, bf16[128,896]{1,0:T(8,128)(2,1)S(1)} %bitcast_select_fusion.12, ...), kind=kOutput, calls=%fused_computation.15 | convolution fusion | flops 1900281856 | bytes 7602180 | tf_op jit(solution)/shard_map/dot_general | solution.py:66
  227.3 4.9 %all-to-all-start = ((f32[16,1,2]{2,1,0:T(1,128)}), f32[16,1,2]{2,1,0:T(1,128)S(1)}, u32[]{:S(2)}, u32[]{:S(2)}) async-start(f32[16,1,2]{2,1,0:T(1,128)} %broadcast_in_dim.55), calls=%async_computation | async-start | bytes 16384 | tf_op jit(solution)/shard_map/all_to_all | solution.py:162
  232.4 6.8 %fusion.1 = f32[512,2048]{1,0:T(8,128)} fusion(bf16[512,896]{1,0:T(8,128)(2,1)} %get-tuple-element.48, bf16[2048,448]{0,1:T(8,128)(2,1)} %bitcast.16, bf16[2048,448]{0,1:T(8,128)(2,1)} %collective-permute-done.7), kind=kOutput, calls=%fused_computation.6 | convolution fusion | flops 1886388224 | bytes 8781824 | tf_op jit(solution)/shard_map/dot_general | solution.py:66
  240.4 1.8 copy-done.4
  242.4 1.8 fusion.3
  244.4 1.3 collective-permute-start.27
  245.7 7.8 %collective-permute-done.24 = bf16[1024,448]{0,1:T(8,128)(2,1)} collective-permute-done((bf16[1024,448]{0,1:T(8,128)(2,1)}, bf16[1024,448]{0,1:T(8,128)(2,1)}, u32[]{:S(2)}, u32[]{:S(2)}) %collective-permute-start.24) | collective-permute-done | bytes 917536 | tf_op jit(solution)/shard_map/ppermute | solution.py:20
  253.4 1.8 add_convert_fusion.1
  255.4 1.6 collective-permute-start.25
  257.0 3.9 %add_convert_fusion = bf16[512,2048]{1,0:T(8,128)(2,1)S(1)} fusion(f32[512,2048]{1,0:T(8,128)S(1)} %copy-done.24, bf16[512,896]{1,0:T(8,128)(2,1)S(1)} %copy-done.28, bf16[2048,448]{0,1:T(8,128)(2,1)} %collective-permute-done.9, bf16[1024,448]{0,1:T(8,128)(2,1)S(1)} %copy-done.13, bf16[1024,448]{0,1:T(8,128)(2,1)S(1)} %copy-done.15), kind=kOutput, calls=%fused_computation | convolution fusion | flops 1892155392 | bytes 10878976 | tf_op jit(solution)/shard_map/dot_general | solution.py:66
  261.1 1.2 collective-permute-start.23
  262.4 1.6 collective-permute-start.22
  267.3 5.2 %collective-permute-done.23 = bf16[128,2048]{1,0:T(8,128)(2,1)S(1)} collective-permute-done((bf16[128,2048]{1,0:T(8,128)(2,1)S(1)}, bf16[128,2048]{1,0:T(8,128)(2,1)S(1)}, u32[]{:S(2)}, u32[]{:S(2)}) %collective-permute-start.23) | collective-permute-done | bytes 524320 | tf_op jit(solution)/shard_map/ppermute | solution.py:20
  272.6 32.7 %collective-permute-done.22 = bf16[128,2048]{1,0:T(8,128)(2,1)S(1)} collective-permute-done((bf16[128,2048]{1,0:T(8,128)(2,1)S(1)}, bf16[128,2048]{1,0:T(8,128)(2,1)S(1)}, u32[]{:S(2)}, u32[]{:S(2)}) %collective-permute-start.22) | collective-permute-done | bytes 524320 | tf_op jit(solution)/shard_map/ppermute | solution.py:20
  305.2 4.6 %collective-permute-done.21 = bf16[128,2048]{1,0:T(8,128)(2,1)S(1)} collective-permute-done((bf16[128,2048]{1,0:T(8,128)(2,1)S(1)}, bf16[128,2048]{1,0:T(8,128)(2,1)S(1)}, u32[]{:S(2)}, u32[]{:S(2)}) %collective-permute-start.21) | collective-permute-done | bytes 524320 | tf_op jit(solution)/shard_map/ppermute | solution.py:20
  311.1 2.8 fusion
  (117 shorter events, 22.8 us)
Async XLA Ops:
  15.2 16.6 %collective-permute-start = (bf16[2,2,4,128,896]{4,3,2,1,0:T(8,128)(2,1)}, bf16[2,2,4,128,896]{4,3,2,1,0:T(8,128)(2,1)}, u32[]{:S(2)}, u32[]{:S(2)}) collective-permute-start(bf16[2,2,4,128,896]{4,3,2,1,0:T(8,128)(2,1)} %shard_map.86), channel_id=1, source_target_pairs={{0,16},{16,0},{1,17},{17,1},{2,18},{18,2},{3,19},{19,3},{4,20},{20... | collective-permute-start | bytes 11010056 | tf_op jit(solution)/shard_map/ppermute | solution.py:25
  15.9 49.7 %collective-permute-start.9 = (bf16[2048,448]{0,1:T(8,128)(2,1)}, bf16[2048,448]{0,1:T(8,128)(2,1)}, u32[]{:S(2)}, u32[]{:S(2)}) collective-permute-start(bf16[2048,448]{0,1:T(8,128)(2,1)} %bitcast.16), channel_id=1, source_target_pairs={{0,12},{4,0},{8,4},{12,8},{1,13},{5,1},{9,5},{13,9},{2,14},{6,2},{... | collective-permute-start | bytes 5505032 | tf_op jit(solution)/shard_map/ppermute | solution.py:20
  16.4 49.1 %collective-permute-start.7 = (bf16[2048,448]{0,1:T(8,128)(2,1)}, bf16[2048,448]{0,1:T(8,128)(2,1)}, u32[]{:S(2)}, u32[]{:S(2)}) collective-permute-start(bf16[2048,448]{0,1:T(8,128)(2,1)} %bitcast.16), channel_id=1, source_target_pairs={{0,4},{4,8},{8,12},{12,0},{1,5},{5,9},{9,13},{13,1},{2,6},{6,10},{... | collective-permute-start | bytes 5505032 | tf_op jit(solution)/shard_map/ppermute | solution.py:20
  36.6 23.5 %collective-permute-start.11 = (bf16[4,128,896]{2,1,0:T(8,128)(2,1)}, bf16[4,128,896]{2,1,0:T(8,128)(2,1)}, u32[]{:S(2)}, u32[]{:S(2)}) collective-permute-start(bf16[4,128,896]{2,1,0:T(8,128)(2,1)} %get-tuple-element.26), channel_id=1, source_target_pairs={{64,0},{128,64},{192,128},{32,96},{96,160},{160,224},{65,1},{129,6... | collective-permute-start | bytes 2752520 | tf_op jit(solution)/shard_map/ppermute | solution.py:117
  38.7 41.1 %collective-permute-start.16 = (bf16[4,128,896]{2,1,0:T(8,128)(2,1)}, bf16[4,128,896]{2,1,0:T(8,128)(2,1)}, u32[]{:S(2)}, u32[]{:S(2)}) collective-permute-start(bf16[4,128,896]{2,1,0:T(8,128)(2,1)} %get-tuple-element.25), channel_id=1, source_target_pairs={{64,0},{128,64},{192,128},{32,96},{96,160},{160,224},{65,1},{129,6... | collective-permute-start | bytes 2752520 | tf_op jit(solution)/shard_map/ppermute | solution.py:117
  44.5 18.7 %copy-start.2 = (bf16[1,1,4,128,896]{4,3,2,1,0:T(8,128)(2,1)S(1)}, bf16[1,1,4,128,896]{4,3,2,1,0:T(8,128)(2,1)}, u32[]{:S(2)}) copy-start(bf16[1,1,4,128,896]{4,3,2,1,0:T(8,128)(2,1)} %get-tuple-element.23) | copy-start | bytes 2752516
  44.5 18.7 %copy-start.3 = (bf16[1,1,4,128,896]{4,3,2,1,0:T(8,128)(2,1)S(1)}, bf16[1,1,4,128,896]{4,3,2,1,0:T(8,128)(2,1)}, u32[]{:S(2)}) copy-start(bf16[1,1,4,128,896]{4,3,2,1,0:T(8,128)(2,1)} %get-tuple-element.27) | copy-start | bytes 2752516
  44.5 26.4 %copy-start.5 = (bf16[1,128,2048]{2,1,0:T(8,128)(2,1)S(1)}, bf16[1,128,2048]{2,1,0:T(8,128)(2,1)}, u32[]{:S(2)}) copy-start(bf16[1,128,2048]{2,1,0:T(8,128)(2,1)} %param.6) | copy-start | bytes 1572868
  45.7 35.5 %collective-permute-start.1 = (bf16[2,128,896]{2,1,0:T(8,128)(2,1)}, bf16[2,128,896]{2,1,0:T(8,128)(2,1)}, u32[]{:S(2)}, u32[]{:S(2)}) collective-permute-start(bf16[2,128,896]{2,1,0:T(8,128)(2,1)} %get-tuple-element.34), channel_id=1, source_target_pairs={{0,1},{1,2},{2,3},{3,0},{4,5},{5,6},{6,7},{7,4},{8,9},{9,10},{10,1... | collective-permute-start | bytes 1376264 | tf_op jit(solution)/shard_map/ppermute | solution.py:20
  60.2 37.8 %collective-permute-start.2 = (bf16[2,128,896]{2,1,0:T(8,128)(2,1)}, bf16[2,128,896]{2,1,0:T(8,128)(2,1)}, u32[]{:S(2)}, u32[]{:S(2)}) collective-permute-start(bf16[2,128,896]{2,1,0:T(8,128)(2,1)} %get-tuple-element.33), channel_id=1, source_target_pairs={{0,2},{1,3},{2,0},{3,1},{4,6},{5,7},{6,4},{7,5},{8,10},{9,11},{10,... | collective-permute-start | bytes 1376264 | tf_op jit(solution)/shard_map/ppermute | solution.py:20
  63.2 16.7 %copy-start.1 = (bf16[1,1,4,128,896]{4,3,2,1,0:T(8,128)(2,1)S(1)}, bf16[1,1,4,128,896]{4,3,2,1,0:T(8,128)(2,1)}, u32[]{:S(2)}) copy-start(bf16[1,1,4,128,896]{4,3,2,1,0:T(8,128)(2,1)} %get-tuple-element.28) | copy-start | bytes 2752516
  65.5 37.6 %collective-permute-start.3 = (bf16[2,128,896]{2,1,0:T(8,128)(2,1)}, bf16[2,128,896]{2,1,0:T(8,128)(2,1)}, u32[]{:S(2)}, u32[]{:S(2)}) collective-permute-start(bf16[2,128,896]{2,1,0:T(8,128)(2,1)} %get-tuple-element.32), channel_id=1, source_target_pairs={{0,3},{1,0},{2,1},{3,2},{4,7},{5,4},{6,5},{7,6},{8,11},{9,8},{10,9... | collective-permute-start | bytes 1376264 | tf_op jit(solution)/shard_map/ppermute | solution.py:20
  65.5 37.6 %collective-permute-start.15 = (bf16[128,896]{1,0:T(8,128)(2,1)}, bf16[128,896]{1,0:T(8,128)(2,1)S(1)}, u32[]{:S(2)}, u32[]{:S(2)}) collective-permute-start(bf16[128,896]{1,0:T(8,128)(2,1)} %get-tuple-element.41), channel_id=1, source_target_pairs={{0,35},{1,32},{2,33},{3,34},{32,3},{33,0},{34,1},{35,2},{4,39},{5,... | collective-permute-start | bytes 688136 | tf_op jit(solution)/shard_map/ppermute | solution.py:137
  72.5 25.4 %copy-start.10 = (bf16[128,896]{1,0:T(8,128)(2,1)S(1)}, bf16[128,896]{1,0:T(8,128)(2,1)}, u32[]{:S(2)}) copy-start(bf16[128,896]{1,0:T(8,128)(2,1)} %get-tuple-element.42) | copy-start | bytes 688132
  72.5 30.6 %copy-start.9 = (bf16[128,896]{1,0:T(8,128)(2,1)S(1)}, bf16[128,896]{1,0:T(8,128)(2,1)}, u32[]{:S(2)}) copy-start(bf16[128,896]{1,0:T(8,128)(2,1)} %get-tuple-element.43) | copy-start | bytes 688132
  72.5 30.6 %copy-start.8 = (bf16[128,896]{1,0:T(8,128)(2,1)S(1)}, bf16[128,896]{1,0:T(8,128)(2,1)}, u32[]{:S(2)}) copy-start(bf16[128,896]{1,0:T(8,128)(2,1)} %get-tuple-element.40) | copy-start | bytes 688132
  72.5 54.6 %copy-start.6 = (bf16[128,2048]{1,0:T(8,128)(2,1)S(1)}, bf16[128,2048]{1,0:T(8,128)(2,1)}, u32[]{:S(2)}) copy-start(bf16[128,2048]{1,0:T(8,128)(2,1)} %bitcast_select_fusion) | copy-start | bytes 1572868
  79.8 104.7 %collective-permute-start.10 = (bf16[1024,448]{0,1:T(8,128)(2,1)S(1)}, bf16[1024,448]{0,1:T(8,128)(2,1)S(1)}, u32[]{:S(2)}, u32[]{:S(2)}) collective-permute-start(bf16[1024,448]{0,1:T(8,128)(2,1)S(1)} %slice.185), channel_id=1, source_target_pairs={{0,12},{4,0},{8,4},{12,8},{1,13},{5,1},{9,5},{13,9},{2,14},{6,2},{... | collective-permute-start | bytes 2752520 | tf_op jit(solution)/shard_map/ppermute | solution.py:20
  81.3 107.4 %collective-permute-start.8 = (bf16[1024,448]{0,1:T(8,128)(2,1)S(1)}, bf16[1024,448]{0,1:T(8,128)(2,1)S(1)}, u32[]{:S(2)}, u32[]{:S(2)}) collective-permute-start(bf16[1024,448]{0,1:T(8,128)(2,1)S(1)} %slice.184), channel_id=1, source_target_pairs={{0,4},{4,8},{8,12},{12,0},{1,5},{5,9},{9,13},{13,1},{2,6},{6,10},{... | collective-permute-start | bytes 2752520 | tf_op jit(solution)/shard_map/ppermute | solution.py:20
  97.9 29.2 %collective-permute-start.14 = (bf16[128,896]{1,0:T(8,128)(2,1)S(1)}, bf16[128,896]{1,0:T(8,128)(2,1)S(1)}, u32[]{:S(2)}, u32[]{:S(2)}) collective-permute-start(bf16[128,896]{1,0:T(8,128)(2,1)S(1)} %copy-done.10), channel_id=1, source_target_pairs={{0,34},{1,35},{2,32},{3,33},{32,2},{33,3},{34,0},{35,1},{4,38},{5,... | collective-permute-start | bytes 688136 | tf_op jit(solution)/shard_map/ppermute | solution.py:137
  103.1 31.9 %collective-permute-start.13 = (bf16[128,896]{1,0:T(8,128)(2,1)S(1)}, bf16[128,896]{1,0:T(8,128)(2,1)S(1)}, u32[]{:S(2)}, u32[]{:S(2)}) collective-permute-start(bf16[128,896]{1,0:T(8,128)(2,1)S(1)} %copy-done.9), channel_id=1, source_target_pairs={{0,33},{1,34},{2,35},{3,32},{32,1},{33,2},{34,3},{35,0},{4,37},{5,... | collective-permute-start | bytes 688136 | tf_op jit(solution)/shard_map/ppermute | solution.py:137
  103.2 31.9 %collective-permute-start.12 = (bf16[128,896]{1,0:T(8,128)(2,1)S(1)}, bf16[128,896]{1,0:T(8,128)(2,1)S(1)}, u32[]{:S(2)}, u32[]{:S(2)}) collective-permute-start(bf16[128,896]{1,0:T(8,128)(2,1)S(1)} %copy-done.8), channel_id=1, source_target_pairs={{0,32},{1,33},{2,34},{3,35},{32,0},{33,1},{34,2},{35,3},{4,36},{5,... | collective-permute-start | bytes 688136 | tf_op jit(solution)/shard_map/ppermute | solution.py:137
  127.2 19.2 %collective-permute-start.6 = (bf16[128,2048]{1,0:T(8,128)(2,1)S(1)}, bf16[128,2048]{1,0:T(8,128)(2,1)S(1)}, u32[]{:S(2)}, u32[]{:S(2)}) collective-permute-start(bf16[128,2048]{1,0:T(8,128)(2,1)S(1)} %copy-done.6), channel_id=1, source_target_pairs={{0,3},{1,0},{2,1},{3,2},{4,7},{5,4},{6,5},{7,6},{8,11},{9,8},{10,9... | collective-permute-start | bytes 1572872 | tf_op jit(solution)/shard_map/ppermute | solution.py:20
  135.0 29.7 %collective-permute-start.5 = (bf16[128,2048]{1,0:T(8,128)(2,1)S(1)}, bf16[128,2048]{1,0:T(8,128)(2,1)S(1)}, u32[]{:S(2)}, u32[]{:S(2)}) collective-permute-start(bf16[128,2048]{1,0:T(8,128)(2,1)S(1)} %copy-done.6), channel_id=1, source_target_pairs={{0,2},{1,3},{2,0},{3,1},{4,6},{5,7},{6,4},{7,5},{8,10},{9,11},{10,... | collective-permute-start | bytes 1572872 | tf_op jit(solution)/shard_map/ppermute | solution.py:20
  135.0 41.0 %collective-permute-start.4 = (bf16[128,2048]{1,0:T(8,128)(2,1)S(1)}, bf16[128,2048]{1,0:T(8,128)(2,1)S(1)}, u32[]{:S(2)}, u32[]{:S(2)}) collective-permute-start(bf16[128,2048]{1,0:T(8,128)(2,1)S(1)} %copy-done.6), channel_id=1, source_target_pairs={{0,1},{1,2},{2,3},{3,0},{4,5},{5,6},{6,7},{7,4},{8,9},{9,10},{10,1... | collective-permute-start | bytes 1572872 | tf_op jit(solution)/shard_map/ppermute | solution.py:20
  146.4 92.8 %copy-start.16 = (bf16[128,2048]{1,0:T(8,128)(2,1)}, bf16[128,2048]{1,0:T(8,128)(2,1)S(1)}, u32[]{:S(2)}) copy-start(bf16[128,2048]{1,0:T(8,128)(2,1)S(1)} %collective-permute-done.6) | copy-start | bytes 1572868
  146.4 52.1 %collective-permute-start.20 = (bf16[128,896]{1,0:T(8,128)(2,1)S(1)}, bf16[128,896]{1,0:T(8,128)(2,1)S(1)}, u32[]{:S(2)}, u32[]{:S(2)}) collective-permute-start(bf16[128,896]{1,0:T(8,128)(2,1)S(1)} %get-tuple-element.37), channel_id=1, source_target_pairs={{0,35},{1,32},{2,33},{3,34},{32,3},{33,0},{34,1},{35,2},{4,39},{5,... | collective-permute-start | bytes 688136 | tf_op jit(solution)/shard_map/ppermute | solution.py:137
  164.8 54.5 %copy-start.18 = (bf16[128,2048]{1,0:T(8,128)(2,1)}, bf16[128,2048]{1,0:T(8,128)(2,1)S(1)}, u32[]{:S(2)}) copy-start(bf16[128,2048]{1,0:T(8,128)(2,1)S(1)} %collective-permute-done.5) | copy-start | bytes 1572868
  164.8 34.7 %collective-permute-start.19 = (bf16[128,896]{1,0:T(8,128)(2,1)S(1)}, bf16[128,896]{1,0:T(8,128)(2,1)S(1)}, u32[]{:S(2)}, u32[]{:S(2)}) collective-permute-start(bf16[128,896]{1,0:T(8,128)(2,1)S(1)} %get-tuple-element.38), channel_id=1, source_target_pairs={{0,34},{1,35},{2,32},{3,33},{32,2},{33,3},{34,0},{35,1},{4,38},{5,... | collective-permute-start | bytes 688136 | tf_op jit(solution)/shard_map/ppermute | solution.py:137
  176.0 43.3 %copy-start.21 = (bf16[128,2048]{1,0:T(8,128)(2,1)}, bf16[128,2048]{1,0:T(8,128)(2,1)S(1)}, u32[]{:S(2)}) copy-start(bf16[128,2048]{1,0:T(8,128)(2,1)S(1)} %collective-permute-done.4) | copy-start | bytes 1572868
  176.0 42.3 %collective-permute-start.18 = (bf16[128,896]{1,0:T(8,128)(2,1)S(1)}, bf16[128,896]{1,0:T(8,128)(2,1)S(1)}, u32[]{:S(2)}, u32[]{:S(2)}) collective-permute-start(bf16[128,896]{1,0:T(8,128)(2,1)S(1)} %get-tuple-element.39), channel_id=1, source_target_pairs={{0,33},{1,34},{2,35},{3,32},{32,1},{33,2},{34,3},{35,0},{4,37},{5,... | collective-permute-start | bytes 688136 | tf_op jit(solution)/shard_map/ppermute | solution.py:137
  184.5 34.7 %collective-permute-start.17 = (bf16[128,896]{1,0:T(8,128)(2,1)S(1)}, bf16[128,896]{1,0:T(8,128)(2,1)S(1)}, u32[]{:S(2)}, u32[]{:S(2)}) collective-permute-start(bf16[128,896]{1,0:T(8,128)(2,1)S(1)} %get-tuple-element.36), channel_id=1, source_target_pairs={{0,32},{1,33},{2,34},{3,35},{32,0},{33,1},{34,2},{35,3},{4,36},{5,... | collective-permute-start | bytes 688136 | tf_op jit(solution)/shard_map/ppermute | solution.py:137
  196.7 22.6 %copy-start = (bf16[2048,896]{0,1:T(8,128)(2,1)}, bf16[2048,896]{0,1:T(8,128)(2,1)S(1)}, u32[]{:S(2)}) copy-start(bf16[2048,896]{0,1:T(8,128)(2,1)S(1)} %convolution_convert_fusion) | copy-start | bytes 11010052
  198.4 44.0 %collective-permute-start.26 = (bf16[1024,448]{0,1:T(8,128)(2,1)}, bf16[1024,448]{0,1:T(8,128)(2,1)S(1)}, u32[]{:S(2)}, u32[]{:S(2)}) collective-permute-start(bf16[1024,448]{0,1:T(8,128)(2,1)} %get-tuple-element.30), channel_id=1, source_target_pairs={{0,12},{4,0},{8,4},{12,8},{1,13},{5,1},{9,5},{13,9},{2,14},{6,2},{... | collective-permute-start | bytes 2752520 | tf_op jit(solution)/shard_map/ppermute | solution.py:20
  227.3 15.1 %all-to-all-start = ((f32[16,1,2]{2,1,0:T(1,128)}), f32[16,1,2]{2,1,0:T(1,128)S(1)}, u32[]{:S(2)}, u32[]{:S(2)}) async-start(f32[16,1,2]{2,1,0:T(1,128)} %broadcast_in_dim.55), calls=%async_computation | async-start | bytes 16384 | tf_op jit(solution)/shard_map/all_to_all | solution.py:162
  232.1 21.3 %collective-permute-start.24 = (bf16[1024,448]{0,1:T(8,128)(2,1)}, bf16[1024,448]{0,1:T(8,128)(2,1)}, u32[]{:S(2)}, u32[]{:S(2)}) collective-permute-start(bf16[1024,448]{0,1:T(8,128)(2,1)} %get-tuple-element.29), channel_id=1, source_target_pairs={{0,4},{4,8},{8,12},{12,0},{1,5},{5,9},{9,13},{13,1},{2,6},{6,10},{... | collective-permute-start | bytes 2752520 | tf_op jit(solution)/shard_map/ppermute | solution.py:20
  244.2 12.8 %copy-start.28 = (bf16[512,896]{1,0:T(8,128)(2,1)S(1)}, bf16[512,896]{1,0:T(8,128)(2,1)}, u32[]{:S(2)}) copy-start(bf16[512,896]{1,0:T(8,128)(2,1)} %copy-done.27) | copy-start | bytes 2752516
  244.4 12.6 %copy-start.13 = (bf16[1024,448]{0,1:T(8,128)(2,1)S(1)}, bf16[1024,448]{0,1:T(8,128)(2,1)}, u32[]{:S(2)}) copy-start(bf16[1024,448]{0,1:T(8,128)(2,1)} %copy-done.12) | copy-start | bytes 2752516
  244.4 12.6 %copy-start.15 = (bf16[1024,448]{0,1:T(8,128)(2,1)S(1)}, bf16[1024,448]{0,1:T(8,128)(2,1)}, u32[]{:S(2)}) copy-start(bf16[1024,448]{0,1:T(8,128)(2,1)} %copy-done.14) | copy-start | bytes 2752516
  244.4 66.6 %collective-permute-start.27 = (bf16[2048,448]{0,1:T(8,128)(2,1)S(1)}, bf16[2048,448]{0,1:T(8,128)(2,1)S(1)}, u32[]{:S(2)}, u32[]{:S(2)}) collective-permute-start(bf16[2048,448]{0,1:T(8,128)(2,1)S(1)} %pad_maximum_fusion.6), channel_id=1, source_target_pairs={{0,12},{4,0},{8,4},{12,8},{1,13},{5,1},{9,5},{13,9},{2,14},{6,2},{... | collective-permute-start | bytes 5505032 | tf_op jit(solution)/shard_map/ppermute | solution.py:20
  255.4 55.6 %collective-permute-start.25 = (bf16[2048,448]{0,1:T(8,128)(2,1)S(1)}, bf16[2048,448]{0,1:T(8,128)(2,1)S(1)}, u32[]{:S(2)}, u32[]{:S(2)}) collective-permute-start(bf16[2048,448]{0,1:T(8,128)(2,1)S(1)} %pad_maximum_fusion.5), channel_id=1, source_target_pairs={{0,4},{4,8},{8,12},{12,0},{1,5},{5,9},{9,13},{13,1},{2,6},{6,10},{... | collective-permute-start | bytes 5505032 | tf_op jit(solution)/shard_map/ppermute | solution.py:20
  260.9 50.1 %copy-start.17 = (bf16[128,2048]{1,0:T(8,128)(2,1)S(1)}, bf16[128,2048]{1,0:T(8,128)(2,1)}, u32[]{:S(2)}) copy-start(bf16[128,2048]{1,0:T(8,128)(2,1)} %copy-done.16) | copy-start | bytes 1572868
  260.9 50.1 %copy-start.20 = (bf16[128,2048]{1,0:T(8,128)(2,1)S(1)}, bf16[128,2048]{1,0:T(8,128)(2,1)}, u32[]{:S(2)}) copy-start(bf16[128,2048]{1,0:T(8,128)(2,1)} %copy-done.18) | copy-start | bytes 1572868
  260.9 50.1 %copy-start.23 = (bf16[128,2048]{1,0:T(8,128)(2,1)S(1)}, bf16[128,2048]{1,0:T(8,128)(2,1)}, u32[]{:S(2)}) copy-start(bf16[128,2048]{1,0:T(8,128)(2,1)} %copy-done.21) | copy-start | bytes 1572868
  260.9 50.1 %copy-start.26 = (bf16[512,896]{1,0:T(8,128)(2,1)S(1)}, bf16[512,896]{1,0:T(8,128)(2,1)}, u32[]{:S(2)}) copy-start(bf16[512,896]{1,0:T(8,128)(2,1)} %get-tuple-element.48) | copy-start | bytes 2752516
  261.1 11.4 %collective-permute-start.23 = (bf16[128,2048]{1,0:T(8,128)(2,1)S(1)}, bf16[128,2048]{1,0:T(8,128)(2,1)S(1)}, u32[]{:S(2)}, u32[]{:S(2)}) collective-permute-start(bf16[128,2048]{1,0:T(8,128)(2,1)S(1)} %get-tuple-element.45), channel_id=1, source_target_pairs={{0,1},{1,2},{2,3},{3,0},{4,5},{5,6},{6,7},{7,4},{8,9},{9,10},{10,1... | collective-permute-start | bytes 1572872 | tf_op jit(solution)/shard_map/ppermute | solution.py:20
  262.4 42.9 %collective-permute-start.22 = (bf16[128,2048]{1,0:T(8,128)(2,1)S(1)}, bf16[128,2048]{1,0:T(8,128)(2,1)S(1)}, u32[]{:S(2)}, u32[]{:S(2)}) collective-permute-start(bf16[128,2048]{1,0:T(8,128)(2,1)S(1)} %get-tuple-element.46), channel_id=1, source_target_pairs={{0,2},{1,3},{2,0},{3,1},{4,6},{5,7},{6,4},{7,5},{8,10},{9,11},{10,... | collective-permute-start | bytes 1572872 | tf_op jit(solution)/shard_map/ppermute | solution.py:20
  263.9 46.0 %collective-permute-start.21 = (bf16[128,2048]{1,0:T(8,128)(2,1)S(1)}, bf16[128,2048]{1,0:T(8,128)(2,1)S(1)}, u32[]{:S(2)}, u32[]{:S(2)}) collective-permute-start(bf16[128,2048]{1,0:T(8,128)(2,1)S(1)} %get-tuple-element.44), channel_id=1, source_target_pairs={{0,3},{1,0},{2,1},{3,2},{4,7},{5,4},{6,5},{7,6},{8,11},{9,8},{10,9... | collective-permute-start | bytes 1572872 | tf_op jit(solution)/shard_map/ppermute | solution.py:20
  (11 other events, 70.7 us)
where the time goes:
time: 316 us; the launch traced here: 315 us
  waiting for transfers between devices  161 us (51%)
  starting transfers between devices  58.4 us (18%)
  matrix products  27.7 us (9%)
  other arithmetic  26.5 us (8%)
  Pallas kernels  19.7 us (6%)
  local copies, waits for them, and re-layouts  12.4 us (4%)
  between operations  9.65 us (3%)
    ppermute x17, waiting for transfers between devices, rotate(): lax.ppermute(block, axis, [(i, (i + distance) % n) for i in range(n)])  98.3 us
    ppermute x8, waiting for transfers between devices, compute(): crossed.append(lax.ppermute(cross, ('zh', 'zl'), route))  44.9 us
    ppermute x8, starting transfers between devices, compute(): crossed.append(lax.ppermute(cross, ('zh', 'zl'), route))  31.7 us
    dot_general x7, matrix products, dot(): lax.dot_general(a, b, (((ca,), (cb,)), ((), ())), preferred_element_type=...  27.7 us
    pallas_call x2, Pallas kernels, prepare(): pl.pallas_call(prepare_body, out_shape=jax.ShapeDtypeStruct((pieces, 2, 4...  19.7 us
    ppermute x2, waiting for transfers between devices, compute(): relayed.append(lax.ppermute(moved, ('y', 'zh'), y_route))  17.5 us
    ppermute x17, starting transfers between devices, rotate(): lax.ppermute(block, axis, [(i, (i + distance) % n) for i in range(n)])  17.2 us
  transfers between devices with their start and end apart: 29, of which 13 were waited for; matrix products, arithmetic and copies ran while one was open for 18% of the time, Pallas kernels for 4%

commit v1 on v0

--- a/solution.py
+++ b/solution.py
@@ -62,6 +62,41 @@
     )(places, order, limit, teacher)
 
 
+def residual_body(near, projected, *refs):
+    own, cross, (out, squares) = refs[:4], refs[4:8], refs[8:]
+    rows = cross[0].shape[0]
+    total = jnp.zeros((), jnp.float32)
+    for k in range(4):
+        cut = slice(k * rows, (k + 1) * rows)
+        target = jnp.where(near[0] == 1, own[k][0].astype(jnp.float32), cross[k][...].astype(jnp.float32))
+        residual = projected[cut] - target
+        out[cut] = residual.astype(jnp.bfloat16)
+        total = total + jnp.sum(residual * residual)
+    squares[0] = total
+
+
+def residual_of(near, projected, own, chunk, cross):
+    tokens = projected.shape[0]
+    rows, wide = cross[0].shape
+
+    def whole(shape):
+        return pl.BlockSpec(shape, lambda i: (0, 0))
+
+    smem = pl.BlockSpec(memory_space=pltpu.SMEM)
+    return pl.pallas_call(
+        residual_body,
+        out_shape=(
+            jax.ShapeDtypeStruct((tokens, wide), jnp.bfloat16),
+            jax.ShapeDtypeStruct((1,), jnp.float32),
+        ),
+        grid=(1,),
+        in_specs=[smem, pl.BlockSpec((tokens, wide), lambda i: (0, chunk))]
+        + [pl.BlockSpec((1, rows, wide), lambda i: (chunk, 0, 0))] * 4
+        + [whole((rows, wide))] * 4,
+        out_specs=(whole((tokens, wide)), smem),
+    )(near, projected, *own, *cross)
+
+
 def dot(a, b, ca, cb):
     return lax.dot_general(a, b, (((ca,), (cb,)), ((), ())), preferred_element_type=jnp.float32)
 
@@ -84,6 +119,7 @@
         students.append(rotate(student, "zl", k))
     w_prev = rotate(weights, "x", 1)
     w_next = rotate(weights, "x", -1)
+    w_opp = rotate(weights, "x", 2)
 
     owners = jnp.sum((boundaries[None, 1:sections] <= layer_map[:, None]).astype(jnp.int32), axis=1)
     layers = jnp.arange(sections, dtype=jnp.int32)
@@ -111,10 +147,8 @@
 
     y_route = [((i, 0), (i - 1, 0)) for i in range(1, 4)] + [((i, 1), (i + 1, 1)) for i in range(3)]
     y_route = [(a * 2 + b, c * 2 + d) for (a, b), (c, d) in y_route]
-    relayed = []
-    for chunk in range(2):
-        moved = jnp.where(beyond_here, kept[2, chunk], from_sibling[1, chunk])
-        relayed.append(lax.ppermute(moved, ("y", "zh"), y_route))
+    moved = jnp.where(beyond_here, kept[2], from_sibling[1])
+    relayed = lax.ppermute(moved, ("y", "zh"), y_route)
 
     def slab(array, index, axis=0):
         return lax.dynamic_index_in_dim(array, index, axis, keepdims=False)
@@ -136,55 +170,56 @@
             route = [(h * 4 + z, (1 - h) * 4 + (z + k) % 4) for h in range(2) for z in range(4)]
             crossed.append(lax.ppermute(cross, ("zh", "zl"), route))
 
-    w_opp_top = rotate(w_prev[:half], "x", 1)
-    w_opp_bot = rotate(w_next[half:], "x", -1)
     rows = jnp.concatenate(students, axis=0)
-
-    w_first = jnp.concatenate([jnp.concatenate([w_opp_top, w_opp_bot], axis=0), w_next], axis=1)
-    w_second = jnp.concatenate([w_prev, weights], axis=1)
-
-    def residual_of(chunk, own, w):
-        blocks = [jnp.where(own_near, own[k][chunk], crossed[4 * chunk + k]) for k in range(4)]
-        target = jnp.concatenate(blocks, axis=0)
-        residual = dot(rows, w, 1, 0) - target.astype(jnp.float32)
-        return jnp.sum(residual * residual), residual.astype(jnp.bfloat16)
-
-    squares_first, first_res = residual_of(0, own, w_first)
-    own, first_res = lax.optimization_barrier((own, first_res))
-    pair = dot(rows, first_res, 0, 0).astype(jnp.bfloat16)
-    part_first = dot(first_res, w_first, 1, 1)
-    up_top = rotate(pair[:half, :width], "x", 1)
-    down_bot = rotate(pair[half:, :width], "x", -1)
-    squares_second, second_res = residual_of(1, own, w_second)
-
-    sums = jnp.stack([squares_first + squares_second, valid_counts[0].astype(jnp.float32)])
+    w_all = lax.optimization_barrier(jnp.concatenate([w_opp, w_next, w_prev, weights], axis=1))
+    projected = lax.optimization_barrier(dot(rows, w_all, 1, 0))
+    near = jnp.reshape(own_near.astype(jnp.int32), (1,))
+    top, bot = rows[:, :half], rows[:, half:]
+
+    def grad(part, residual):
+        return dot(part, residual, 0, 0)
+
+    first_res, squares_first = residual_of(near, projected, own, 0, crossed[:4])
+    opp_res, next_res = first_res[:, :width], first_res[:, width:]
+    opp_top = grad(top, opp_res).astype(jnp.bfloat16)
+    opp_bot = grad(bot, opp_res).astype(jnp.bfloat16)
+    next_bot = grad(bot, next_res).astype(jnp.bfloat16)
+    up_top = rotate(opp_top, "x", 1)
+    down_bot = rotate(opp_bot, "x", -1)
+    second_res, squares_second = residual_of(near, projected, own, 1, crossed[4:])
+
+    sums = jnp.stack([squares_first[0] + squares_second[0], valid_counts[0].astype(jnp.float32)])
     copies = jnp.broadcast_to(sums, (lax.axis_size(DP), 2))
     sums = jnp.sum(lax.all_to_all(copies, DP, split_axis=0, concat_axis=0, tiled=True), axis=0)
     total = sums[1]
     loss = sums[:1] / (total * (width * lax.axis_size(DP)))
     factor = loss_scale / total
 
-    next_part = pair[:, width:].astype(jnp.float32)
-    next_part = jnp.concatenate([next_part[:half] + up_top.astype(jnp.float32), next_part[half:]], axis=0)
-    next_part = lax.optimization_barrier((next_part.astype(jnp.bfloat16), sums))[0]
+    next_top = (grad(top, next_res) + up_top.astype(jnp.float32)).astype(jnp.bfloat16)
+    next_part = jnp.concatenate([next_top, next_bot], axis=0)
+    next_part = lax.optimization_barrier((next_part, sums))[0]
     from_prev = rotate(next_part, "x", 1)
-    prev_part = dot(rows, second_res[:, :width], 0, 0)
-    prev_part = jnp.concatenate([prev_part[:half], prev_part[half:] + down_bot.astype(jnp.float32)], axis=0)
-    prev_part = lax.optimization_barrier((prev_part.astype(jnp.bfloat16), sums))[0]
+    prev_res, own_res = second_res[:, :width], second_res[:, width:]
+    prev_top = grad(top, prev_res).astype(jnp.bfloat16)
+    prev_bot = (grad(bot, prev_res) + down_bot.astype(jnp.float32)).astype(jnp.bfloat16)
+    prev_part = jnp.concatenate([prev_top, prev_bot], axis=0)
+    prev_part = lax.optimization_barrier((prev_part, sums))[0]
     from_next = rotate(prev_part, "x", -1)
 
-    student_part = (part_first + dot(second_res, w_second, 1, 1)).astype(jnp.bfloat16)
+    residual = lax.optimization_barrier(jnp.concatenate([first_res, second_res], axis=1))
+    student_part = dot(residual, w_all, 1, 1).astype(jnp.bfloat16)
     student_part = lax.optimization_barrier((student_part, sums))[0]
     returned = []
     for k in (1, 2, 3):
         part = student_part[k * tokens : (k + 1) * tokens]
         returned.append(rotate(part, "zl", -k))
+    own_part = lax.optimization_barrier(grad(rows, own_res))
 
     student_grad = student_part[:tokens].astype(jnp.float32)
     for part in returned:
         student_grad = student_grad + part.astype(jnp.float32)
     student_grad = (student_grad * factor).astype(jnp.bfloat16)
-    projector_grad = dot(rows, second_res[:, width:], 0, 0) + from_prev.astype(jnp.float32) + from_next.astype(jnp.float32)
+    projector_grad = own_part + from_prev.astype(jnp.float32) + from_next.astype(jnp.float32)
     projector_grad = (projector_grad * factor).astype(jnp.bfloat16)
     return (student_grad[None], projector_grad[None], loss)
 

time: 316 us -> 314 us (level)
  the two profiles are of different devices: /device:TPU:47 before, /device:TPU:1 now
where the time goes in v1:
time: 314 us; the launch traced here: 311 us
  waiting for transfers between devices  151 us (48%)
  starting transfers between devices  63.7 us (20%)
  Pallas kernels  26.9 us (9%)
  matrix products  26.6 us (8%)
  other arithmetic  24.6 us (8%)
  between operations  9.33 us (3%)
  local copies, waits for them, and re-layouts  9.07 us (3%)
    ppermute x16, waiting for transfers between devices, rotate(): lax.ppermute(block, axis, [(i, (i + distance) % n) for i in range(n)])  124 us
    ppermute x8, starting transfers between devices, compute(): crossed.append(lax.ppermute(cross, ('zh', 'zl'), route))  29.4 us
    dot_general x9, matrix products, dot(): lax.dot_general(a, b, (((ca,), (cb,)), ((), ())), preferred_element_type=...  26.6 us
    ppermute x8, waiting for transfers between devices, compute(): crossed.append(lax.ppermute(cross, ('zh', 'zl'), route))  26.4 us
    pallas_call x2, Pallas kernels, prepare(): pl.pallas_call(prepare_body, out_shape=jax.ShapeDtypeStruct((pieces, 2, 4...  19.7 us
    ppermute x16, starting transfers between devices, rotate(): lax.ppermute(block, axis, [(i, (i + distance) % n) for i in range(n)])  19.6 us
    all_to_all x1, starting transfers between devices, compute(): lax.all_to_all(copies, DP, split_axis=0, concat_axis=0, tiled=True)  10.2 us
    pallas_call x2, Pallas kernels, residual_of(): pl.pallas_call(residual_body, out_shape=(jax.ShapeDtypeStruct((tokens, wi...  7.2 us
  transfers between devices with their start and end apart: 27, of which 12 were waited for; matrix products, arithmetic and copies ran while one was open for 17% of the time, Pallas kernels for 6%

profile of v1, /device:TPU:1, one launch (start us, length us, event | category | flops | bytes accessed | tf_op | source)
XLA Modules:
  0.0 311.1 jit_solution(15384776305117151492)
XLA Ops:
  1.4 1.4 fusion.17
  6.9 8.4 %shard_map.86 = bf16[2,2,4,128,896]{4,3,2,1,0:T(8,128)(2,1)} custom-call(s32[2]{0:T(128)} %bitcast.73, s32[4]{0:T(128)} %pad_add_fusion.order, s32[1]{0:T(128)} %copy.11.limit, bf16[4,128,7168]{2,1,0:T(8,128)(2,1)} %rows.3), custom_call_target="tpu_custom_call" | custom-call | tf_op jit(solution)/shard_map/pallas_call | solution.py:52
  15.3 3.2 %collective-permute-start.6 = (bf16[2,2,4,128,896]{4,3,2,1,0:T(8,128)(2,1)}, bf16[2,2,4,128,896]{4,3,2,1,0:T(8,128)(2,1)}, u32[]{:S(2)}, u32[]{:S(2)}) collective-permute-start(bf16[2,2,4,128,896]{4,3,2,1,0:T(8,128)(2,1)} %shard_map.86), channel_id=1, source_target_pairs={{0,16},{16,0},{1,17},{17,1},{2,18},{18,2},{3,19},{19,3},{4,20},{20... | collective-permute-start | bytes 11010056 | tf_op jit(solution)/shard_map/ppermute | solution.py:25
  21.1 1.7 collective-permute-start
  22.8 14.3 %collective-permute-done = bf16[128,2048]{1,0:T(8,128)(2,1)S(1)} collective-permute-done((bf16[128,2048]{1,0:T(8,128)(2,1)S(1)}, bf16[128,2048]{1,0:T(8,128)(2,1)S(1)}, u32[]{:S(2)}, u32[]{:S(2)}) %collective-permute-start) | collective-permute-done | bytes 524320 | tf_op jit(solution)/shard_map/ppermute | solution.py:20
  37.8 11.4 %shard_map.85 = bf16[3,2,4,128,896]{4,3,2,1,0:T(8,128)(2,1)} custom-call(s32[3]{0:T(128)} %slice.110.places, s32[4]{0:T(128)} %pad_add_fusion.order, s32[1]{0:T(128)} %copy.11.limit, bf16[4,128,7168]{2,1,0:T(8,128)(2,1)} %rows.3), custom_call_target="tpu_custom_call" | custom-call | tf_op jit(solution)/shard_map/pallas_call | solution.py:52
  51.7 5.5 %fusion.1 = (bf16[2,4,128,896]{3,2,1,0:T(8,128)(2,1)}, bf16[1,2,4,128,896]{4,3,2,1,0:T(8,128)(2,1)S(1)}, bf16[1,2,4,128,896]{4,3,2,1,0:T(8,128)(2,1)}) fusion(bf16[2,2,4,128,896]{4,3,2,1,0:T(8,128)(2,1)} %collective-permute-done.6, bf16[3,2,4,128,896]{4,3,2,1,0:T(8,128)(2,1)} %shard_map.85, pred[]{:T(512)S(6)} %eq.51), kind=kLoop, calls=%fused_computation.6 | loop fusion | flops 917504 | bytes 12845057 | tf_op jit(solution)/shard_map/jit(_where)/select_n | solution.py:150
  57.2 4.9 %collective-permute-done.1 = bf16[128,2048]{1,0:T(8,128)(2,1)S(1)} collective-permute-done((bf16[128,2048]{1,0:T(8,128)(2,1)S(1)}, bf16[128,2048]{1,0:T(8,128)(2,1)S(1)}, u32[]{:S(2)}, u32[]{:S(2)}) %collective-permute-start.1) | collective-permute-done | bytes 524320 | tf_op jit(solution)/shard_map/ppermute | solution.py:20
  62.0 1.3 collective-permute-start.10
  65.8 1.6 fusion.19
  67.5 5.8 %collective-permute-done.2 = bf16[128,2048]{1,0:T(8,128)(2,1)} collective-permute-done((bf16[128,2048]{1,0:T(8,128)(2,1)S(1)}, bf16[128,2048]{1,0:T(8,128)(2,1)}, u32[]{:S(2)}, u32[]{:S(2)}) %collective-permute-start.2) | collective-permute-done | bytes 524320 | tf_op jit(solution)/shard_map/ppermute | solution.py:20
  73.2 2.7 pad_maximum_fusion.1
  75.9 23.7 %collective-permute-done.4 = bf16[2048,448]{0,1:T(8,128)(2,1)} collective-permute-done((bf16[2048,448]{0,1:T(8,128)(2,1)}, bf16[2048,448]{0,1:T(8,128)(2,1)}, u32[]{:S(2)}, u32[]{:S(2)}) %collective-permute-start.4) | collective-permute-done | bytes 1835040 | tf_op jit(solution)/shard_map/ppermute | solution.py:20
  99.6 1.9 collective-permute-done.5
  101.6 4.1 %pad_maximum_fusion = bf16[2048,1792]{0,1:T(8,128)(2,1)S(1)} fusion(bf16[2048,448]{0,1:T(8,128)(2,1)} %bitcast.9, bf16[2048,448]{0,1:T(8,128)(2,1)} %collective-permute-done.5, bf16[2048,448]{0,1:T(8,128)(2,1)} %collective-permute-done.4, bf16[2048,448]{0,1:T(8,128)(2,1)} %collective-permute-done.3), kind=kLoop, calls=%fused_computation | loop fusion | flops 29360128 | bytes 14680064 | tf_op jit(solution)/shard_map/concatenate | solution.py:174
  105.6 1.3 select_bitcast_fusion
  107.0 2.9 collective-permute-start.8
  110.6 1.6 fusion.20
  112.3 1.6 fusion.22
  114.1 5.2 %collective-permute-start.11 = (bf16[128,896]{1,0:T(8,128)(2,1)S(1)}, bf16[128,896]{1,0:T(8,128)(2,1)S(1)}, u32[]{:S(2)}, u32[]{:S(2)}) collective-permute-start(bf16[128,896]{1,0:T(8,128)(2,1)S(1)} %get-tuple-element.33), channel_id=1, source_target_pairs={{0,32},{1,33},{2,34},{3,35},{32,0},{33,1},{34,2},{35,3},{4,36},{5,... | collective-permute-start | bytes 688136 | tf_op jit(solution)/shard_map/ppermute | solution.py:171
  119.3 2.5 collective-permute-start.12
  121.8 2.7 collective-permute-start.13
  124.5 25.6 %collective-permute-done.8.refs_2_ = bf16[2,128,896]{2,1,0:T(8,128)(2,1)S(1)} collective-permute-done((bf16[2,128,896]{2,1,0:T(8,128)(2,1)S(1)}, bf16[2,128,896]{2,1,0:T(8,128)(2,1)S(1)}, u32[]{:S(2)}, u32[]{:S(2)}) %collective-permute-start.8) | collective-permute-done | bytes 458784 | tf_op jit(solution)/shard_map/ppermute | solution.py:20
  150.1 12.0 %collective-permute-start.14 = (bf16[128,896]{1,0:T(8,128)(2,1)S(1)}, bf16[128,896]{1,0:T(8,128)(2,1)S(1)}, u32[]{:S(2)}, u32[]{:S(2)}) collective-permute-start(bf16[128,896]{1,0:T(8,128)(2,1)S(1)} %get-tuple-element.30), channel_id=1, source_target_pairs={{0,35},{1,32},{2,33},{3,34},{32,3},{33,0},{34,1},{35,2},{4,39},{5,... | collective-permute-start | bytes 688136 | tf_op jit(solution)/shard_map/ppermute | solution.py:171
  162.1 7.0 %fusion.18.projected = f32[512,1792]{1,0:T(8,128)} fusion(bf16[2048,1792]{0,1:T(8,128)(2,1)S(1)} %pad_maximum_fusion, bf16[128,2048]{1,0:T(8,128)(2,1)} %collective-permute-done.2, bf16[128,2048]{1,0:T(8,128)(2,1)S(1)} %collective-permute-done.1, bf16[128,2048]{1,0:T(8,128)(2,1)S(1)} %collective-permute-done, bf16[128,2048]{1,0:T(8,128)(2,1)S(1)} %bitcast_select_fusion), kind=kOutput, calls=%fused_computation.55 | convolution fusion | flops 3766484992 | bytes 13107200 | tf_op jit(solution)/shard_map/dot_general | solution.py:101
  170.3 5.3 %collective-permute-start.17 = (bf16[128,896]{1,0:T(8,128)(2,1)}, bf16[128,896]{1,0:T(8,128)(2,1)}, u32[]{:S(2)}, u32[]{:S(2)}) collective-permute-start(bf16[128,896]{1,0:T(8,128)(2,1)} %get-tuple-element.35), channel_id=1, source_target_pairs={{0,34},{1,35},{2,32},{3,33},{32,2},{33,3},{34,0},{35,1},{4,38},{5,... | collective-permute-start | bytes 688136 | tf_op jit(solution)/shard_map/ppermute | solution.py:171
  175.6 1.5 collective-permute-start.18
  177.1 21.5 %collective-permute-done.14.refs_7_ = bf16[128,896]{1,0:T(8,128)(2,1)S(1)} collective-permute-done((bf16[128,896]{1,0:T(8,128)(2,1)S(1)}, bf16[128,896]{1,0:T(8,128)(2,1)S(1)}, u32[]{:S(2)}, u32[]{:S(2)}) %collective-permute-start.14) | collective-permute-done | bytes 229408 | tf_op jit(solution)/shard_map/ppermute | solution.py:171
  199.3 3.7 %shard_map.87 = (bf16[512,896]{1,0:T(8,128)(2,1)}, f32[1]{0:T(128)}) custom-call(s32[1]{0:T(128)} %bitcast.6.near, f32[512,1792]{1,0:T(8,128)} %fusion.18.projected, bf16[2,128,896]{2,1,0:T(8,128)(2,1)} %get-tuple-element.29.refs_0_, bf16[2,128,896]{2,1,0:T(8,128)(2,1)} %copy-done.3, bf16[2,128,896]{2,1,0:T(8,128)(2,1)} %copy-done.4, ...), custom_call_target="tpu_custom_call" | custom-call | tf_op jit(solution)/shard_map/pallas_call | solution.py:86
  203.0 2.8 convolution_convert_fusion.4
  206.8 1.7 convolution_convert_fusion.1
  208.5 4.8 %collective-permute-done.18.refs_7_ = bf16[128,896]{1,0:T(8,128)(2,1)} collective-permute-done((bf16[128,896]{1,0:T(8,128)(2,1)S(1)}, bf16[128,896]{1,0:T(8,128)(2,1)}, u32[]{:S(2)}, u32[]{:S(2)}) %collective-permute-start.18) | collective-permute-done | bytes 229408 | tf_op jit(solution)/shard_map/ppermute | solution.py:171
  213.3 3.5 %shard_map.88 = (bf16[512,896]{1,0:T(8,128)(2,1)}, f32[1]{0:T(128)}) custom-call(s32[1]{0:T(128)} %bitcast.6.near, f32[512,1792]{1,0:T(8,128)} %fusion.18.projected, bf16[2,128,896]{2,1,0:T(8,128)(2,1)} %get-tuple-element.29.refs_0_, bf16[2,128,896]{2,1,0:T(8,128)(2,1)} %copy-done.3, bf16[2,128,896]{2,1,0:T(8,128)(2,1)} %copy-done.4, ...), custom_call_target="tpu_custom_call" | custom-call | tf_op jit(solution)/shard_map/pallas_call | solution.py:86
  219.0 10.2 %all-to-all-start = ((f32[16,1,2]{2,1,0:T(1,128)}), f32[16,1,2]{2,1,0:T(1,128)S(1)}, u32[]{:S(2)}, u32[]{:S(2)}) async-start(f32[16,1,2]{2,1,0:T(1,128)} %broadcast_in_dim.55), calls=%async_computation | async-start | bytes 16384 | tf_op jit(solution)/shard_map/all_to_all | solution.py:193
  229.1 2.6 collective-permute-start.24
  231.7 2.8 convolution_convert_fusion.3
  234.5 1.6 convolution_convert_fusion.2
  236.2 1.4 pad_maximum_fusion.2
  237.6 2.3 add_convert_fusion.1
  240.2 10.8 %collective-permute-done.24 = bf16[1024,448]{0,1:T(8,128)(2,1)} collective-permute-done((bf16[1024,448]{0,1:T(8,128)(2,1)}, bf16[1024,448]{0,1:T(8,128)(2,1)}, u32[]{:S(2)}, u32[]{:S(2)}) %collective-permute-start.24) | collective-permute-done | bytes 917536 | tf_op jit(solution)/shard_map/ppermute | solution.py:20
  251.0 1.9 add_convert_fusion
  253.0 3.3 %collective-permute-start.25 = (bf16[2048,448]{0,1:T(8,128)(2,1)S(1)}, bf16[2048,448]{0,1:T(8,128)(2,1)S(1)}, u32[]{:S(2)}, u32[]{:S(2)}) collective-permute-start(bf16[2048,448]{0,1:T(8,128)(2,1)S(1)} %pad_maximum_fusion.4), channel_id=1, source_target_pairs={{0,12},{4,0},{8,4},{12,8},{1,13},{5,1},{9,5},{13,9},{2,14},{6,2},{... | collective-permute-start | bytes 5505032 | tf_op jit(solution)/shard_map/ppermute | solution.py:20
  256.3 4.2 %convolution_convert_fusion = bf16[512,2048]{1,0:T(8,128)(2,1)S(1)} fusion(bf16[512,1792]{1,0:T(8,128)(2,1)S(1)} %copy-done.6, bf16[2048,1792]{0,1:T(8,128)(2,1)S(1)} %bitcast.72), kind=kOutput, calls=%fused_computation.2 | convolution fusion | flops 3759144960 | bytes 11272192 | tf_op jit(solution)/shard_map/dot_general | solution.py:101
  260.6 3.0 collective-permute-start.19
  264.2 2.4 fusion.9
  269.1 3.7 %collective-permute-done.19 = bf16[128,2048]{1,0:T(8,128)(2,1)S(1)} collective-permute-done((bf16[128,2048]{1,0:T(8,128)(2,1)S(1)}, bf16[128,2048]{1,0:T(8,128)(2,1)S(1)}, u32[]{:S(2)}, u32[]{:S(2)}) %collective-permute-start.19) | collective-permute-done | bytes 524320 | tf_op jit(solution)/shard_map/ppermute | solution.py:20
  272.9 33.7 %collective-permute-done.20 = bf16[128,2048]{1,0:T(8,128)(2,1)S(1)} collective-permute-done((bf16[128,2048]{1,0:T(8,128)(2,1)S(1)}, bf16[128,2048]{1,0:T(8,128)(2,1)S(1)}, u32[]{:S(2)}, u32[]{:S(2)}) %collective-permute-start.20) | collective-permute-done | bytes 524320 | tf_op jit(solution)/shard_map/ppermute | solution.py:20
  307.7 2.2 fusion
  (98 shorter events, 16.9 us)
Async XLA Ops:
  6.9 14.1 %copy-start.12 = (bf16[1,128,2048]{2,1,0:T(8,128)(2,1)S(1)}, bf16[1,128,2048]{2,1,0:T(8,128)(2,1)}, u32[]{:S(2)}) copy-start(bf16[1,128,2048]{2,1,0:T(8,128)(2,1)} %param.6) | copy-start | bytes 1572868
  6.9 30.2 %copy-start.21 = (s32[5]{0:T(128)S(1)}, s32[5]{0:T(128)}, u32[]{:S(2)}) copy-start(s32[5]{0:T(128)} %subtract_clamp_fusion) | copy-start | bytes 64
  15.3 35.1 %collective-permute-start.6 = (bf16[2,2,4,128,896]{4,3,2,1,0:T(8,128)(2,1)}, bf16[2,2,4,128,896]{4,3,2,1,0:T(8,128)(2,1)}, u32[]{:S(2)}, u32[]{:S(2)}) collective-permute-start(bf16[2,2,4,128,896]{4,3,2,1,0:T(8,128)(2,1)} %shard_map.86), channel_id=1, source_target_pairs={{0,16},{16,0},{1,17},{17,1},{2,18},{18,2},{3,19},{19,3},{4,20},{20... | collective-permute-start | bytes 11010056 | tf_op jit(solution)/shard_map/ppermute | solution.py:25
  18.5 57.4 %collective-permute-start.3 = (bf16[2048,448]{0,1:T(8,128)(2,1)}, bf16[2048,448]{0,1:T(8,128)(2,1)}, u32[]{:S(2)}, u32[]{:S(2)}) collective-permute-start(bf16[2048,448]{0,1:T(8,128)(2,1)} %bitcast.9), channel_id=1, source_target_pairs={{0,8},{4,12},{8,0},{12,4},{1,9},{5,13},{9,1},{13,5},{2,10},{6,14},... | collective-permute-start | bytes 5505032 | tf_op jit(solution)/shard_map/ppermute | solution.py:20
  19.5 80.1 %collective-permute-start.4 = (bf16[2048,448]{0,1:T(8,128)(2,1)}, bf16[2048,448]{0,1:T(8,128)(2,1)}, u32[]{:S(2)}, u32[]{:S(2)}) collective-permute-start(bf16[2048,448]{0,1:T(8,128)(2,1)} %bitcast.9), channel_id=1, source_target_pairs={{0,12},{4,0},{8,4},{12,8},{1,13},{5,1},{9,5},{13,9},{2,14},{6,2},{... | collective-permute-start | bytes 5505032 | tf_op jit(solution)/shard_map/ppermute | solution.py:20
  20.4 81.2 %collective-permute-start.5 = (bf16[2048,448]{0,1:T(8,128)(2,1)}, bf16[2048,448]{0,1:T(8,128)(2,1)}, u32[]{:S(2)}, u32[]{:S(2)}) collective-permute-start(bf16[2048,448]{0,1:T(8,128)(2,1)} %bitcast.9), channel_id=1, source_target_pairs={{0,4},{4,8},{8,12},{12,0},{1,5},{5,9},{9,13},{13,1},{2,6},{6,10},{... | collective-permute-start | bytes 5505032 | tf_op jit(solution)/shard_map/ppermute | solution.py:20
  21.1 16.0 %collective-permute-start = (bf16[128,2048]{1,0:T(8,128)(2,1)S(1)}, bf16[128,2048]{1,0:T(8,128)(2,1)S(1)}, u32[]{:S(2)}, u32[]{:S(2)}) collective-permute-start(bf16[128,2048]{1,0:T(8,128)(2,1)S(1)} %bitcast_select_fusion), channel_id=1, source_target_pairs={{0,1},{1,2},{2,3},{3,0},{4,5},{5,6},{6,7},{7,4},{8,9},{9,10},{10,1... | collective-permute-start | bytes 1572872 | tf_op jit(solution)/shard_map/ppermute | solution.py:20
  37.1 125.0 %copy-start.13 = (bf16[128,2048]{1,0:T(8,128)(2,1)}, bf16[128,2048]{1,0:T(8,128)(2,1)S(1)}, u32[]{:S(2)}) copy-start(bf16[128,2048]{1,0:T(8,128)(2,1)S(1)} %collective-permute-done) | copy-start | bytes 1572868
  37.1 24.9 %collective-permute-start.1 = (bf16[128,2048]{1,0:T(8,128)(2,1)S(1)}, bf16[128,2048]{1,0:T(8,128)(2,1)S(1)}, u32[]{:S(2)}, u32[]{:S(2)}) collective-permute-start(bf16[128,2048]{1,0:T(8,128)(2,1)S(1)} %bitcast_select_fusion), channel_id=1, source_target_pairs={{0,2},{1,3},{2,0},{3,1},{4,6},{5,7},{6,4},{7,5},{8,10},{9,11},{10,... | collective-permute-start | bytes 1572872 | tf_op jit(solution)/shard_map/ppermute | solution.py:20
  50.4 22.8 %collective-permute-start.2 = (bf16[128,2048]{1,0:T(8,128)(2,1)S(1)}, bf16[128,2048]{1,0:T(8,128)(2,1)}, u32[]{:S(2)}, u32[]{:S(2)}) collective-permute-start(bf16[128,2048]{1,0:T(8,128)(2,1)S(1)} %bitcast_select_fusion), channel_id=1, source_target_pairs={{0,3},{1,0},{2,1},{3,2},{4,7},{5,4},{6,5},{7,6},{8,11},{9,8},{10,9... | collective-permute-start | bytes 1572872 | tf_op jit(solution)/shard_map/ppermute | solution.py:20
  62.0 100.1 %copy-start.15 = (bf16[128,2048]{1,0:T(8,128)(2,1)}, bf16[128,2048]{1,0:T(8,128)(2,1)S(1)}, u32[]{:S(2)}) copy-start(bf16[128,2048]{1,0:T(8,128)(2,1)S(1)} %collective-permute-done.1) | copy-start | bytes 1572868
  62.0 50.2 %collective-permute-start.10 = (bf16[2,4,128,896]{3,2,1,0:T(8,128)(2,1)}, bf16[2,4,128,896]{3,2,1,0:T(8,128)(2,1)}, u32[]{:S(2)}, u32[]{:S(2)}) collective-permute-start(bf16[2,4,128,896]{3,2,1,0:T(8,128)(2,1)} %get-tuple-element.21), channel_id=1, source_target_pairs={{64,0},{128,64},{192,128},{32,96},{96,160},{160,224},{65,1},{129,6... | collective-permute-start | bytes 5505032 | tf_op jit(solution)/shard_map/ppermute | solution.py:151
  75.9 29.7 %copy-start.1 = (bf16[1,2,4,128,896]{4,3,2,1,0:T(8,128)(2,1)S(1)}, bf16[1,2,4,128,896]{4,3,2,1,0:T(8,128)(2,1)}, u32[]{:S(2)}) copy-start(bf16[1,2,4,128,896]{4,3,2,1,0:T(8,128)(2,1)} %get-tuple-element.25) | copy-start | bytes 5505028
  105.6 56.5 %copy-start = (bf16[2048,1792]{0,1:T(8,128)(2,1)}, bf16[2048,1792]{0,1:T(8,128)(2,1)S(1)}, u32[]{:S(2)}) copy-start(bf16[2048,1792]{0,1:T(8,128)(2,1)S(1)} %pad_maximum_fusion) | copy-start | bytes 22020100
  107.0 14.8 %collective-permute-start.7 = (bf16[2,128,896]{2,1,0:T(8,128)(2,1)S(1)}, bf16[2,128,896]{2,1,0:T(8,128)(2,1)S(1)}, u32[]{:S(2)}, u32[]{:S(2)}) collective-permute-start(bf16[2,128,896]{2,1,0:T(8,128)(2,1)S(1)} %get-tuple-element.28), channel_id=1, source_target_pairs={{0,1},{1,2},{2,3},{3,0},{4,5},{5,6},{6,7},{7,4},{8,9},{9,10},{10,1... | collective-permute-start | bytes 1376264 | tf_op jit(solution)/shard_map/ppermute | solution.py:20
  107.0 43.1 %collective-permute-start.8 = (bf16[2,128,896]{2,1,0:T(8,128)(2,1)S(1)}, bf16[2,128,896]{2,1,0:T(8,128)(2,1)S(1)}, u32[]{:S(2)}, u32[]{:S(2)}) collective-permute-start(bf16[2,128,896]{2,1,0:T(8,128)(2,1)S(1)} %get-tuple-element.27), channel_id=1, source_target_pairs={{0,2},{1,3},{2,0},{3,1},{4,6},{5,7},{6,4},{7,5},{8,10},{9,11},{10,... | collective-permute-start | bytes 1376264 | tf_op jit(solution)/shard_map/ppermute | solution.py:20
  109.9 60.2 %collective-permute-start.9 = (bf16[2,128,896]{2,1,0:T(8,128)(2,1)S(1)}, bf16[2,128,896]{2,1,0:T(8,128)(2,1)S(1)}, u32[]{:S(2)}, u32[]{:S(2)}) collective-permute-start(bf16[2,128,896]{2,1,0:T(8,128)(2,1)S(1)} %get-tuple-element.26), channel_id=1, source_target_pairs={{0,3},{1,0},{2,1},{3,2},{4,7},{5,4},{6,5},{7,6},{8,11},{9,8},{10,9... | collective-permute-start | bytes 1376264 | tf_op jit(solution)/shard_map/ppermute | solution.py:20
  114.1 56.2 %collective-permute-start.11 = (bf16[128,896]{1,0:T(8,128)(2,1)S(1)}, bf16[128,896]{1,0:T(8,128)(2,1)S(1)}, u32[]{:S(2)}, u32[]{:S(2)}) collective-permute-start(bf16[128,896]{1,0:T(8,128)(2,1)S(1)} %get-tuple-element.33), channel_id=1, source_target_pairs={{0,32},{1,33},{2,34},{3,35},{32,0},{33,1},{34,2},{35,3},{4,36},{5,... | collective-permute-start | bytes 688136 | tf_op jit(solution)/shard_map/ppermute | solution.py:171
  119.3 51.1 %collective-permute-start.12 = (bf16[128,896]{1,0:T(8,128)(2,1)S(1)}, bf16[128,896]{1,0:T(8,128)(2,1)S(1)}, u32[]{:S(2)}, u32[]{:S(2)}) collective-permute-start(bf16[128,896]{1,0:T(8,128)(2,1)S(1)} %get-tuple-element.32), channel_id=1, source_target_pairs={{0,33},{1,34},{2,35},{3,32},{32,1},{33,2},{34,3},{35,0},{4,37},{5,... | collective-permute-start | bytes 688136 | tf_op jit(solution)/shard_map/ppermute | solution.py:171
  121.7 47.4 %copy-start.3 = (bf16[2,128,896]{2,1,0:T(8,128)(2,1)}, bf16[2,128,896]{2,1,0:T(8,128)(2,1)S(1)}, u32[]{:S(2)}) copy-start(bf16[2,128,896]{2,1,0:T(8,128)(2,1)S(1)} %collective-permute-done.7.refs_1_) | copy-start | bytes 1376260
  121.8 53.9 %collective-permute-start.13 = (bf16[128,896]{1,0:T(8,128)(2,1)S(1)}, bf16[128,896]{1,0:T(8,128)(2,1)S(1)}, u32[]{:S(2)}, u32[]{:S(2)}) collective-permute-start(bf16[128,896]{1,0:T(8,128)(2,1)S(1)} %get-tuple-element.31), channel_id=1, source_target_pairs={{0,34},{1,35},{2,32},{3,33},{32,2},{33,3},{34,0},{35,1},{4,38},{5,... | collective-permute-start | bytes 688136 | tf_op jit(solution)/shard_map/ppermute | solution.py:171
  150.1 19.0 %copy-start.4 = (bf16[2,128,896]{2,1,0:T(8,128)(2,1)}, bf16[2,128,896]{2,1,0:T(8,128)(2,1)S(1)}, u32[]{:S(2)}) copy-start(bf16[2,128,896]{2,1,0:T(8,128)(2,1)S(1)} %collective-permute-done.8.refs_2_) | copy-start | bytes 1376260
  150.1 48.5 %collective-permute-start.14 = (bf16[128,896]{1,0:T(8,128)(2,1)S(1)}, bf16[128,896]{1,0:T(8,128)(2,1)S(1)}, u32[]{:S(2)}, u32[]{:S(2)}) collective-permute-start(bf16[128,896]{1,0:T(8,128)(2,1)S(1)} %get-tuple-element.30), channel_id=1, source_target_pairs={{0,35},{1,32},{2,33},{3,34},{32,3},{33,0},{34,1},{35,2},{4,39},{5,... | collective-permute-start | bytes 688136 | tf_op jit(solution)/shard_map/ppermute | solution.py:171
  170.0 28.5 %copy-start.5 = (bf16[2,128,896]{2,1,0:T(8,128)(2,1)}, bf16[2,128,896]{2,1,0:T(8,128)(2,1)S(1)}, u32[]{:S(2)}) copy-start(bf16[2,128,896]{2,1,0:T(8,128)(2,1)S(1)} %collective-permute-done.9.refs_3_) | copy-start | bytes 1376260
  170.0 38.4 %collective-permute-start.15 = (bf16[128,896]{1,0:T(8,128)(2,1)}, bf16[128,896]{1,0:T(8,128)(2,1)}, u32[]{:S(2)}, u32[]{:S(2)}) collective-permute-start(bf16[128,896]{1,0:T(8,128)(2,1)} %get-tuple-element.37), channel_id=1, source_target_pairs={{0,32},{1,33},{2,34},{3,35},{32,0},{33,1},{34,2},{35,3},{4,36},{5,... | collective-permute-start | bytes 688136 | tf_op jit(solution)/shard_map/ppermute | solution.py:171
  170.3 29.0 %copy-start.17 = (bf16[128,896]{1,0:T(8,128)(2,1)}, bf16[128,896]{1,0:T(8,128)(2,1)S(1)}, u32[]{:S(2)}) copy-start(bf16[128,896]{1,0:T(8,128)(2,1)S(1)} %collective-permute-done.11.refs_4_) | copy-start | bytes 688132
  170.3 38.1 %collective-permute-start.16 = (bf16[128,896]{1,0:T(8,128)(2,1)}, bf16[128,896]{1,0:T(8,128)(2,1)}, u32[]{:S(2)}, u32[]{:S(2)}) collective-permute-start(bf16[128,896]{1,0:T(8,128)(2,1)} %get-tuple-element.36), channel_id=1, source_target_pairs={{0,33},{1,34},{2,35},{3,32},{32,1},{33,2},{34,3},{35,0},{4,37},{5,... | collective-permute-start | bytes 688136 | tf_op jit(solution)/shard_map/ppermute | solution.py:171
  170.3 29.0 %copy-start.18 = (bf16[128,896]{1,0:T(8,128)(2,1)}, bf16[128,896]{1,0:T(8,128)(2,1)S(1)}, u32[]{:S(2)}) copy-start(bf16[128,896]{1,0:T(8,128)(2,1)S(1)} %collective-permute-done.12.refs_5_) | copy-start | bytes 688132
  170.3 38.2 %collective-permute-start.17 = (bf16[128,896]{1,0:T(8,128)(2,1)}, bf16[128,896]{1,0:T(8,128)(2,1)}, u32[]{:S(2)}, u32[]{:S(2)}) collective-permute-start(bf16[128,896]{1,0:T(8,128)(2,1)} %get-tuple-element.35), channel_id=1, source_target_pairs={{0,34},{1,35},{2,32},{3,33},{32,2},{33,3},{34,0},{35,1},{4,38},{5,... | collective-permute-start | bytes 688136 | tf_op jit(solution)/shard_map/ppermute | solution.py:171
  175.6 23.0 %copy-start.19 = (bf16[128,896]{1,0:T(8,128)(2,1)}, bf16[128,896]{1,0:T(8,128)(2,1)S(1)}, u32[]{:S(2)}) copy-start(bf16[128,896]{1,0:T(8,128)(2,1)S(1)} %collective-permute-done.13.refs_6_) | copy-start | bytes 688132
  175.6 37.7 %collective-permute-start.18 = (bf16[128,896]{1,0:T(8,128)(2,1)S(1)}, bf16[128,896]{1,0:T(8,128)(2,1)}, u32[]{:S(2)}, u32[]{:S(2)}) collective-permute-start(bf16[128,896]{1,0:T(8,128)(2,1)S(1)} %get-tuple-element.34), channel_id=1, source_target_pairs={{0,35},{1,32},{2,33},{3,34},{32,3},{33,0},{34,1},{35,2},{4,39},{5,... | collective-permute-start | bytes 688136 | tf_op jit(solution)/shard_map/ppermute | solution.py:171
  199.3 3.7 %copy-start.2 = (bf16[512,2048]{1,0:T(8,128)(2,1)S(1)}, bf16[512,2048]{1,0:T(8,128)(2,1)}, u32[]{:S(2)}) copy-start(bf16[512,2048]{1,0:T(8,128)(2,1)} %pad_maximum_fusion.1) | copy-start | bytes 6291460
  203.0 3.8 %copy-start.8 = (bf16[512,896]{1,0:T(8,128)(2,1)S(1)}, bf16[512,896]{1,0:T(8,128)(2,1)}, u32[]{:S(2)}) copy-start(bf16[512,896]{1,0:T(8,128)(2,1)} %get-tuple-element.10) | copy-start | bytes 2752516
  205.7 31.8 %collective-permute-start.22 = (bf16[1024,448]{0,1:T(8,128)(2,1)}, bf16[1024,448]{0,1:T(8,128)(2,1)}, u32[]{:S(2)}, u32[]{:S(2)}) collective-permute-start(bf16[1024,448]{0,1:T(8,128)(2,1)} %convolution_convert_fusion.4), channel_id=1, source_target_pairs={{0,4},{4,8},{8,12},{12,0},{1,5},{5,9},{9,13},{13,1},{2,6},{6,10},{... | collective-permute-start | bytes 2752520 | tf_op jit(solution)/shard_map/ppermute | solution.py:20
  216.9 17.7 %copy-start.7 = (bf16[512,896]{1,0:T(8,128)(2,1)S(1)}, bf16[512,896]{1,0:T(8,128)(2,1)}, u32[]{:S(2)}) copy-start(bf16[512,896]{1,0:T(8,128)(2,1)} %get-tuple-element.11) | copy-start | bytes 2752516
  219.0 18.6 %all-to-all-start = ((f32[16,1,2]{2,1,0:T(1,128)}), f32[16,1,2]{2,1,0:T(1,128)S(1)}, u32[]{:S(2)}, u32[]{:S(2)}) async-start(f32[16,1,2]{2,1,0:T(1,128)} %broadcast_in_dim.55), calls=%async_computation | async-start | bytes 16384 | tf_op jit(solution)/shard_map/all_to_all | solution.py:193
  229.1 21.8 %collective-permute-start.24 = (bf16[1024,448]{0,1:T(8,128)(2,1)}, bf16[1024,448]{0,1:T(8,128)(2,1)}, u32[]{:S(2)}, u32[]{:S(2)}) collective-permute-start(bf16[1024,448]{0,1:T(8,128)(2,1)} %convolution_convert_fusion.1), channel_id=1, source_target_pairs={{0,12},{4,0},{8,4},{12,8},{1,13},{5,1},{9,5},{13,9},{2,14},{6,2},{... | collective-permute-start | bytes 2752520 | tf_op jit(solution)/shard_map/ppermute | solution.py:20
  237.6 18.7 %slice-start = ((s8[7340032]{0:T(1024)(128)(4,1)}), s8[4194304]{0:T(1024)(128)(4,1)S(1)}, s32[]{:S(2)}) async-start(s8[7340032]{0:T(1024)(128)(4,1)} %bitcast.71), calls=%async_computation.1 | async-start | bytes 8388608
  240.1 12.8 %copy-start.10 = (bf16[1024,448]{0,1:T(8,128)(2,1)S(1)}, bf16[1024,448]{0,1:T(8,128)(2,1)}, u32[]{:S(2)}) copy-start(bf16[1024,448]{0,1:T(8,128)(2,1)} %convolution_convert_fusion.2) | copy-start | bytes 2752516
  240.1 16.2 %slice-start.1 = ((s8[7340032]{0:T(1024)(128)(4,1)}), s8[3145728]{0:T(1024)(128)(4,1)S(1)}, s32[]{:S(2)}) async-start(s8[7340032]{0:T(1024)(128)(4,1)} %bitcast.71), calls=%async_computation.2 | async-start | bytes 6291456
  240.1 67.6 %collective-permute-start.23 = (bf16[2048,448]{0,1:T(8,128)(2,1)S(1)}, bf16[2048,448]{0,1:T(8,128)(2,1)S(1)}, u32[]{:S(2)}, u32[]{:S(2)}) collective-permute-start(bf16[2048,448]{0,1:T(8,128)(2,1)S(1)} %pad_maximum_fusion.3), channel_id=1, source_target_pairs={{0,4},{4,8},{8,12},{12,0},{1,5},{5,9},{9,13},{13,1},{2,6},{6,10},{... | collective-permute-start | bytes 5505032 | tf_op jit(solution)/shard_map/ppermute | solution.py:20
  252.9 3.5 %copy-start.6 = (bf16[512,1792]{1,0:T(8,128)(2,1)S(1)}, bf16[512,1792]{1,0:T(8,128)(2,1)}, u32[]{:S(2)}) copy-start(bf16[512,1792]{1,0:T(8,128)(2,1)} %pad_maximum_fusion.2) | copy-start | bytes 5505028
  253.0 54.7 %collective-permute-start.25 = (bf16[2048,448]{0,1:T(8,128)(2,1)S(1)}, bf16[2048,448]{0,1:T(8,128)(2,1)S(1)}, u32[]{:S(2)}, u32[]{:S(2)}) collective-permute-start(bf16[2048,448]{0,1:T(8,128)(2,1)S(1)} %pad_maximum_fusion.4), channel_id=1, source_target_pairs={{0,12},{4,0},{8,4},{12,8},{1,13},{5,1},{9,5},{13,9},{2,14},{6,2},{... | collective-permute-start | bytes 5505032 | tf_op jit(solution)/shard_map/ppermute | solution.py:20
  260.5 3.7 %copy-start.14 = (bf16[128,2048]{1,0:T(8,128)(2,1)S(1)}, bf16[128,2048]{1,0:T(8,128)(2,1)}, u32[]{:S(2)}) copy-start(bf16[128,2048]{1,0:T(8,128)(2,1)} %copy-done.13) | copy-start | bytes 1572868
  260.5 3.7 %copy-start.16 = (bf16[128,2048]{1,0:T(8,128)(2,1)S(1)}, bf16[128,2048]{1,0:T(8,128)(2,1)}, u32[]{:S(2)}) copy-start(bf16[128,2048]{1,0:T(8,128)(2,1)} %copy-done.15) | copy-start | bytes 1572868
  260.6 12.2 %collective-permute-start.19 = (bf16[128,2048]{1,0:T(8,128)(2,1)S(1)}, bf16[128,2048]{1,0:T(8,128)(2,1)S(1)}, u32[]{:S(2)}, u32[]{:S(2)}) collective-permute-start(bf16[128,2048]{1,0:T(8,128)(2,1)S(1)} %get-tuple-element.38), channel_id=1, source_target_pairs={{0,3},{1,0},{2,1},{3,2},{4,7},{5,4},{6,5},{7,6},{8,11},{9,8},{10,9... | collective-permute-start | bytes 1572872 | tf_op jit(solution)/shard_map/ppermute | solution.py:20
  263.6 43.0 %collective-permute-start.20 = (bf16[128,2048]{1,0:T(8,128)(2,1)S(1)}, bf16[128,2048]{1,0:T(8,128)(2,1)S(1)}, u32[]{:S(2)}, u32[]{:S(2)}) collective-permute-start(bf16[128,2048]{1,0:T(8,128)(2,1)S(1)} %get-tuple-element.40), channel_id=1, source_target_pairs={{0,2},{1,3},{2,0},{3,1},{4,6},{5,7},{6,4},{7,5},{8,10},{9,11},{10,... | collective-permute-start | bytes 1572872 | tf_op jit(solution)/shard_map/ppermute | solution.py:20
  263.6 43.0 %collective-permute-start.21 = (bf16[128,2048]{1,0:T(8,128)(2,1)S(1)}, bf16[128,2048]{1,0:T(8,128)(2,1)S(1)}, u32[]{:S(2)}, u32[]{:S(2)}) collective-permute-start(bf16[128,2048]{1,0:T(8,128)(2,1)S(1)} %get-tuple-element.39), channel_id=1, source_target_pairs={{0,1},{1,2},{2,3},{3,0},{4,5},{5,6},{6,7},{7,4},{8,9},{9,10},{10,1... | collective-permute-start | bytes 1572872 | tf_op jit(solution)/shard_map/ppermute | solution.py:20
  (3 other events, 4.7 us)

commit v2 on v1

v2 whole, which is shorter than its diff:
```python
import functools

import jax
import jax.numpy as jnp
from jax import lax
from jax.experimental import pallas as pl
from jax.experimental.pallas import tpu as pltpu
from jax.sharding import Mesh
from jax.sharding import PartitionSpec as P

loss_scale = 128.0
norm_eps = 1e-06


SECTION = ("y", "zh", "core")
DP = ("x", "zl")
ROWS = 32


def rotate(block, axis, distance):
    n = lax.axis_size(axis)
    return lax.ppermute(block, axis, [(i, (i + distance) % n) for i in range(n)])


def exchange(block, axis, bit):
    n = lax.axis_size(axis)
    return lax.ppermute(block, axis, [(i, i ^ bit) for i in range(n)])


PIECES = ("beyond", "across", "here")
ORDER, ZL, LIMIT = 6, 10, 11


def prepare_body(piece, info, mine, theirs, *refs):
    outs, spread = refs[:-1], refs[-1]
    local = info[3 + piece] == 1
    wide = jnp.where(local, mine[0], theirs[0]).astype(jnp.float32)
    scale = lax.rsqrt(jnp.mean(wide * wide, axis=1, keepdims=True) + norm_eps)
    token = pl.program_id(0) * wide.shape[0] + lax.broadcasted_iota(jnp.int32, scale.shape, 0)
    scale = jnp.where(token < info[LIMIT], scale, 0.0)
    group = wide.shape[1] // 4
    width = group // 4
    for chunk in range(2):
        halves = []
        for half in range(2):
            start = pl.multiple_of(info[ORDER + 2 * chunk + half] * group, group)
            cut = pl.ds(start, group)
            part = jnp.where(local, mine[0, :, cut], theirs[0, :, cut]).astype(jnp.float32)
            halves.append((part * scale).astype(jnp.bfloat16))
        for z in range(4):
            cut = slice(z * width, (z + 1) * width)
            spread[chunk, (z - info[ZL]) & 3] = jnp.concatenate([h[:, cut] for h in halves], axis=1)
    for index, out in enumerate(outs):
        out[...] = spread[:, index] if PIECES[piece] == "here" else spread[index]


def prepare(mine, theirs, info, name):
    _, tokens, features = mine.shape
    piece = PIECES.index(name)
    rows = min(ROWS, tokens)
    wide = features // 8
    lead = [(2,)] * 4 if name == "here" else [(4,)] * 2

    def taken(kept):
        def index(i, info):
            on = info[3 + piece] if kept else 1 - info[3 + piece]
            return (info[piece] * on, i * on, 0)

        return pl.BlockSpec((1, rows, features), index)

    def written(dims):
        return pl.BlockSpec((*dims, rows, wide), lambda i, info: (0,) * len(dims) + (i, 0))

    return pl.pallas_call(
        functools.partial(prepare_body, piece),
        out_shape=[jax.ShapeDtypeStruct((*dims, tokens, wide), jnp.bfloat16) for dims in lead],
        grid_spec=pltpu.PrefetchScalarGridSpec(
            num_scalar_prefetch=1,
            grid=(tokens // rows,),
            in_specs=[taken(True), taken(False)],
            out_specs=[written(dims) for dims in lead],
            scratch_shapes=[pltpu.VMEM((2, 4, rows, wide), jnp.bfloat16)],
        ),
        compiler_params=pltpu.CompilerParams(dimension_semantics=("arbitrary",)),
    )(info, mine, theirs)


def residual_body(near, projected, *refs):
    own, cross, (out, squares) = refs[:4], refs[4:8], refs[8:]
    rows = cross[0].shape[0]
    total = jnp.zeros((), jnp.float32)
    for k in range(4):
        cut = slice(k * rows, (k + 1) * rows)
        target = jnp.where(near[0] == 1, own[k][0].astype(jnp.float32), cross[k][...].astype(jnp.float32))
        residual = projected[cut] - target
        out[cut] = residual.astype(jnp.bfloat16)
        total = total + jnp.sum(residual * residual)
    squares[0] = total


def residual_of(near, projected, own, chunk, cross):
    tokens = projected.shape[0]
    rows, wide = cross[0].shape

    def whole(shape):
        return pl.BlockSpec(shape, lambda i: (0, 0))

    smem = pl.BlockSpec(memory_space=pltpu.SMEM)
    return pl.pallas_call(
        residual_body,
        out_shape=(
            jax.ShapeDtypeStruct((tokens, wide), jnp.bfloat16),
            jax.ShapeDtypeStruct((1,), jnp.float32),
        ),
        grid=(1,),
        in_specs=[smem, pl.BlockSpec((tokens, wide), lambda i: (0, chunk))]
        + [pl.BlockSpec((1, rows, wide), lambda i: (chunk, 0, 0))] * 4
        + [whole((rows, wide))] * 4,
        out_specs=(whole((tokens, wide)), smem),
    )(near, projected, *own, *cross)


def dot(a, b, ca, cb):
    return lax.dot_general(a, b, (((ca,), (cb,)), ((), ())), preferred_element_type=jnp.float32)


def compute(student_states, teacher_states, projector, layer_map, boundaries, valid_counts):
    y, zh, core = (lax.axis_index(a) for a in SECTION)
    x, zl = (lax.axis_index(a) for a in DP)
    sections = lax.axis_size(SECTION)
    chip = 2 * y + zh
    here = 2 * chip + core
    weights = projector[0]
    tokens = student_states.shape[1]
    half = weights.shape[0] // 2
    width = weights.shape[1]

    theirs = exchange(teacher_states, "core", 1)

    valid = lax.broadcasted_iota(jnp.int32, (tokens, 1), 0) < valid_counts[0]
    student = jnp.where(valid, student_states[0], 0)
    students = [student]
    for k in (1, 2, 3):
        students.append(rotate(student, "zl", k))
    w_prev = rotate(weights, "x", 1)
    w_next = rotate(weights, "x", -1)
    w_opp = rotate(weights, "x", 2)

    owners = jnp.sum((boundaries[None, 1:sections] <= layer_map[:, None]).astype(jnp.int32), axis=1)
    layers = jnp.arange(sections, dtype=jnp.int32)
    across = 2 * (2 * y + 1 - zh) + core
    beyond = jnp.where(zh == 0, 2 * (chip - 1), 2 * (chip + 1)) + core
    wanted = jnp.stack([beyond, across, here])
    hit = layers[None, :] == wanted[:, None]
    owner_of = jnp.sum(jnp.where(hit, owners[None, :], 0), axis=1)
    layer_of = jnp.sum(jnp.where(hit, layer_map[None, :], 0), axis=1)
    first_of = jnp.sum(jnp.where(layers[None, :] == owner_of[:, None], boundaries[None, :sections], 0), axis=1)
    places = jnp.clip(layer_of - first_of, 0, teacher_states.shape[0] - 1)
    local = (owner_of == here).astype(jnp.int32)
    rest = jnp.stack([(x + 2) & 3, (x + 1) & 3, (x + 3) & 3, x, zl, valid_counts[0]]).astype(jnp.int32)
    info = jnp.concatenate([places, local, rest])
    near = (owner_of >> 1 == chip).astype(jnp.int32)
    across_near = near[1] == 1

    beyond_slabs = prepare(teacher_states, theirs, info, "beyond")
    y_route = [((i, 0), (i - 1, 0)) for i in range(1, 4)] + [((i, 1), (i + 1, 1)) for i in range(3)]
    y_route = [(a * 2 + b, c * 2 + d) for (a, b), (c, d) in y_route]
    relayed = []
    for chunk in range(2):
        relayed.append(lax.ppermute(beyond_slabs[chunk], ("y", "zh"), y_route))
    across_slabs = prepare(teacher_states, theirs, info, "across")

    def send_across(chunk):
        sent = []
        for k in range(4):
            route = [(h * 4 + z, (1 - h) * 4 + (z + k) % 4) for h in range(2) for z in range(4)]
            slab = jnp.where(across_near, across_slabs[chunk][k], relayed[chunk][k])
            sent.append(lax.ppermute(slab, ("zh", "zl"), route))
        return sent

    crossed = send_across(0)
    here_slabs = prepare(teacher_states, theirs, info, "here")
    own = [here_slabs[0]] + [rotate(here_slabs[k], "zl", k) for k in (1, 2, 3)]
    crossed = crossed + send_across(1)

    rows = jnp.concatenate(students, axis=0)
    w_all = lax.optimization_barrier(jnp.concatenate([w_opp, w_next, w_prev, weights], axis=1))
    projected = lax.optimization_barrier(dot(rows, w_all, 1, 0))
    near = near[2:]
    top, bot = rows[:, :half], rows[:, half:]

    def grad(part, residual):
        return dot(part, residual, 0, 0)

    first_res, squares_first = residual_of(near, projected, own, 0, crossed[:4])
    opp_res, next_res = first_res[:, :width], first_res[:, width:]
    opp_top = grad(top, opp_res).astype(jnp.bfloat16)
    opp_bot = grad(bot, opp_res).astype(jnp.bfloat16)
    next_bot = grad(bot, next_res).astype(jnp.bfloat16)
    up_top = rotate(opp_top, "x", 1)
    down_bot = rotate(opp_bot, "x", -1)
    second_res, squares_second = residual_of(near, projected, own, 1, crossed[4:])

    next_top = (grad(top, next_res) + up_top.astype(jnp.float32)).astype(jnp.bfloat16)
    next_part = jnp.concatenate([next_top, next_bot], axis=0)
    from_prev = rotate(next_part, "x", 1)
    prev_res, own_res = second_res[:, :width], second_res[:, width:]
    prev_top = grad(top, prev_res).astype(jnp.bfloat16)
    prev_bot = (grad(bot, prev_res) + down_bot.astype(jnp.float32)).astype(jnp.bfloat16)
    prev_part = jnp.concatenate([prev_top, prev_bot], axis=0)
    from_next = rotate(prev_part, "x", -1)

    residual = lax.optimization_barrier(jnp.concatenate([first_res, second_res], axis=1))
    student_part = dot(residual, w_all, 1, 1).astype(jnp.bfloat16)
    returned = []
    for k in (1, 2, 3):
        part = student_part[k * tokens : (k + 1) * tokens]
        returned.append(rotate(part, "zl", -k))
    own_part = grad(rows, own_res)

    sums = jnp.stack([squares_first[0] + squares_second[0], valid_counts[0].astype(jnp.float32)])
    copies = jnp.broadcast_to(sums, (lax.axis_size(DP), 2))
    copies, own_part = lax.optimization_barrier((copies, own_part))
    sums = jnp.sum(lax.all_to_all(copies, DP, split_axis=0, concat_axis=0, tiled=True), axis=0)
    total = sums[1]
    loss = sums[:1] / (total * (width * lax.axis_size(DP)))
    factor = loss_scale / total

    student_grad = student_part[:tokens].astype(jnp.float32)
    for part in returned:
        student_grad = student_grad + part.astype(jnp.float32)
    student_grad = (student_grad * factor).astype(jnp.bfloat16)
    projector_grad = own_part + from_prev.astype(jnp.float32) + from_next.astype(jnp.float32)
    projector_grad = (projector_grad * factor).astype(jnp.bfloat16)
    return (student_grad[None], projector_grad[None], loss)


def solution(mesh):
    split = Mesh(mesh.devices.reshape(4, 2, 2, 4, 4), SECTION + DP)
    return jax.shard_map(
        compute,
        mesh=split,
        in_specs=(
            P(SECTION, DP, None),
            P(SECTION, DP, None),
            P(SECTION, None, DP),
            P(),
            P(),
            P(DP),
        ),
        out_specs=(P(SECTION, DP, None), P(SECTION, None, DP), P(SECTION)),
        check_vma=False,
    )
```

time: 314 us -> 320 us (1.019)
  waiting for transfers between devices: 151 us -> 89.8 us
  starting transfers between devices: 63.7 us -> 101 us
  blocking collectives: 0 us -> 36.9 us
  local copies, waits for them, and re-layouts: 9.07 us -> 4.99 us
    ppermute x16, waiting for transfers between devices: 124 us -> 81.3 us  [rotate(): lax.ppermute(block, axis, [(i, (i + distance) % n) for i in range(n)])]
    all_to_all x0 -> x1, blocking collectives: none -> 36.9 us  [compute(): lax.all_to_all(copies, DP, split_axis=0, concat_axis=0, tiled=True)]
    ppermute x9 -> x10, starting transfers between devices: 30.7 us -> 67.1 us  [the longest x8 64.5 us: send_across(): sent.append(lax.ppermute(slab, ('zh', 'zl'), route))]
    ppermute x9 -> x10, waiting for transfers between devices: 26.4 us -> 8.56 us  [the longest x8 8.56 us: send_across(): sent.append(lax.ppermute(slab, ('zh', 'zl'), route))]
    ppermute x16, starting transfers between devices: 19.6 us -> 30.8 us  [rotate(): lax.ppermute(block, axis, [(i, (i + distance) % n) for i in range(n)])]
    all_to_all x1 -> x0, starting transfers between devices: 10.2 us -> none  [compute(): lax.all_to_all(copies, DP, split_axis=0, concat_axis=0, tiled=True)]
    slice x5 -> x1, local copies, waits for them, and re-layouts: 6.15 us -> 0.61 us  [compute(): across_near = near[1] == 1]
    broadcast_in_dim x2, other arithmetic: 3.35 us -> 7.7 us  [compute(): return (student_grad[None], projector_grad[None], loss)]
  transfers between devices with their start and end apart: 27 -> 27, of which waited for: 12 -> 9; matrix products, arithmetic and copies ran while one was open for 17% -> 16% of each run, Pallas kernels for 6% -> 6%
where the time goes in v2:
time: 320 us; the launch traced here: 317 us
  starting transfers between devices  101 us (32%)
  waiting for transfers between devices  89.8 us (28%)
  blocking collectives  36.9 us (12%)
  matrix products  27.7 us (9%)
  other arithmetic  26 us (8%)
  Pallas kernels  24.2 us (8%)
  between operations  6.52 us (2%)
  local copies, waits for them, and re-layouts  4.99 us (2%)
    ppermute x16, waiting for transfers between devices, rotate(): lax.ppermute(block, axis, [(i, (i + distance) % n) for i in range(n)])  81.3 us
    ppermute x8, starting transfers between devices, send_across(): sent.append(lax.ppermute(slab, ('zh', 'zl'), route))  64.5 us
    all_to_all x1, blocking collectives, compute(): lax.all_to_all(copies, DP, split_axis=0, concat_axis=0, tiled=True)  36.9 us
    ppermute x16, starting transfers between devices, rotate(): lax.ppermute(block, axis, [(i, (i + distance) % n) for i in range(n)])  30.8 us
    dot_general x9, matrix products, dot(): lax.dot_general(a, b, (((ca,), (cb,)), ((), ())), preferred_element_type=...  27.7 us
    pallas_call x3, Pallas kernels, prepare(): pl.pallas_call(functools.partial(prepare_body, piece), out_shape=[jax.Sha...  15.8 us
    ppermute x8, waiting for transfers between devices, send_across(): sent.append(lax.ppermute(slab, ('zh', 'zl'), route))  8.56 us
    pallas_call x2, Pallas kernels, residual_of(): pl.pallas_call(residual_body, out_shape=(jax.ShapeDtypeStruct((tokens, wi...  8.33 us
  transfers between devices with their start and end apart: 27, of which 9 were waited for; matrix products, arithmetic and copies ran while one was open for 16% of the time, Pallas kernels for 6%

profile of v2, /device:TPU:1, one launch (start us, length us, event | category | flops | bytes accessed | tf_op | source)
XLA Modules:
  0.0 317.3 jit_solution(1241094743186056299)
XLA Ops:
  0.6 3.3 %collective-permute-start.6 = (bf16[4,128,7168]{2,1,0:T(8,128)(2,1)}, bf16[4,128,7168]{2,1,0:T(8,128)(2,1)}, u32[]{:S(2)}, u32[]{:S(2)}) collective-permute-start(bf16[4,128,7168]{2,1,0:T(8,128)(2,1)} %mine.5), channel_id=1, source_target_pairs={{0,16},{16,0},{1,17},{17,1},{2,18},{18,2},{3,19},{19,3},{4,20},{20... | collective-permute-start | bytes 22020104 | tf_op jit(solution)/shard_map/ppermute | solution.py:27
  5.8 2.7 collective-permute-start.3
  10.0 11.2 %collective-permute-done = bf16[128,2048]{1,0:T(8,128)(2,1)S(1)} collective-permute-done((bf16[128,2048]{1,0:T(8,128)(2,1)S(1)}, bf16[128,2048]{1,0:T(8,128)(2,1)S(1)}, u32[]{:S(2)}, u32[]{:S(2)}) %collective-permute-start) | collective-permute-done | bytes 524320 | tf_op jit(solution)/shard_map/ppermute | solution.py:22
  23.7 22.0 %collective-permute-done.1 = bf16[128,2048]{1,0:T(8,128)(2,1)S(1)} collective-permute-done((bf16[128,2048]{1,0:T(8,128)(2,1)S(1)}, bf16[128,2048]{1,0:T(8,128)(2,1)S(1)}, u32[]{:S(2)}, u32[]{:S(2)}) %collective-permute-start.1) | collective-permute-done | bytes 524320 | tf_op jit(solution)/shard_map/ppermute | solution.py:22
  45.8 2.3 collective-permute-start.2
  50.8 8.2 %collective-permute-done.2 = bf16[128,2048]{1,0:T(8,128)(2,1)} collective-permute-done((bf16[128,2048]{1,0:T(8,128)(2,1)S(1)}, bf16[128,2048]{1,0:T(8,128)(2,1)}, u32[]{:S(2)}, u32[]{:S(2)}) %collective-permute-start.2) | collective-permute-done | bytes 524320 | tf_op jit(solution)/shard_map/ppermute | solution.py:22
  59.0 1.4 pad_maximum_fusion.1
  60.3 28.0 %collective-permute-done.4 = bf16[2048,448]{0,1:T(8,128)(2,1)} collective-permute-done((bf16[2048,448]{0,1:T(8,128)(2,1)}, bf16[2048,448]{0,1:T(8,128)(2,1)}, u32[]{:S(2)}, u32[]{:S(2)}) %collective-permute-start.4) | collective-permute-done | bytes 1835040 | tf_op jit(solution)/shard_map/ppermute | solution.py:22
  89.0 6.0 %pad_maximum_fusion = bf16[2048,1792]{0,1:T(8,128)(2,1)} fusion(bf16[2048,448]{0,1:T(8,128)(2,1)S(1)} %bitcast.47, bf16[2048,448]{0,1:T(8,128)(2,1)} %collective-permute-done.5, bf16[2048,448]{0,1:T(8,128)(2,1)} %collective-permute-done.4, bf16[2048,448]{0,1:T(8,128)(2,1)} %collective-permute-done.3), kind=kLoop, calls=%fused_computation | loop fusion | flops 29360128 | bytes 14680064 | tf_op jit(solution)/shard_map/concatenate | solution.py:187
  95.0 5.2 %shard_map.87 = (bf16[4,128,896]{2,1,0:T(8,128)(2,1)}, bf16[4,128,896]{2,1,0:T(8,128)(2,1)}) custom-call(s32[12]{0:T(128)} %concatenate.20.info, bf16[4,128,7168]{2,1,0:T(8,128)(2,1)} %mine.5, bf16[4,128,7168]{2,1,0:T(8,128)(2,1)} %collective-permute-done.6.theirs), custom_call_target="tpu_custom_call" | custom-call | tf_op jit(solution)/shard_map/pallas_call | solution.py:74
  100.3 1.3 collective-permute-start.10
  101.6 5.3 %shard_map.85 = (bf16[2,128,896]{2,1,0:T(8,128)(2,1)}, bf16[2,128,896]{2,1,0:T(8,128)(2,1)}, bf16[2,128,896]{2,1,0:T(8,128)(2,1)}, bf16[2,128,896]{2,1,0:T(8,128)(2,1)}) custom-call(s32[12]{0:T(128)} %concatenate.20.info, bf16[4,128,7168]{2,1,0:T(8,128)(2,1)} %mine.5, bf16[4,128,7168]{2,1,0:T(8,128)(2,1)} %collective-permute-done.6.theirs), custom_call_target="tpu_custom_call" | custom-call | tf_op jit(solution)/shard_map/pallas_call | solution.py:74
  106.9 1.5 collective-permute-start.7
  108.3 2.0 collective-permute-start.8
  111.6 9.4 %fusion.24.projected = f32[512,1792]{1,0:T(8,128)} fusion(bf16[2048,1792]{0,1:T(8,128)(2,1)} %pad_maximum_fusion, bf16[128,2048]{1,0:T(8,128)(2,1)} %collective-permute-done.2, bf16[128,2048]{1,0:T(8,128)(2,1)} %copy-done.8, bf16[128,2048]{1,0:T(8,128)(2,1)} %copy-done.6, bf16[128,2048]{1,0:T(8,128)(2,1)S(1)} %bitcast_select_fusion), kind=kOutput, calls=%fused_computation.59 | convolution fusion | flops 3766484992 | bytes 13107200 | tf_op jit(solution)/shard_map/dot_general | solution.py:124
  121.0 1.7 collective-permute-start.9
  122.7 5.3 %shard_map.86 = (bf16[4,128,896]{2,1,0:T(8,128)(2,1)}, bf16[4,128,896]{2,1,0:T(8,128)(2,1)}) custom-call(s32[12]{0:T(128)} %concatenate.20.info, bf16[4,128,7168]{2,1,0:T(8,128)(2,1)} %mine.5, bf16[4,128,7168]{2,1,0:T(8,128)(2,1)} %collective-permute-done.6.theirs), custom_call_target="tpu_custom_call" | custom-call | tf_op jit(solution)/shard_map/pallas_call | solution.py:74
  128.0 1.7 fusion.20
  129.8 9.1 %collective-permute-start.11 = (bf16[128,896]{1,0:T(8,128)(2,1)S(1)}, bf16[128,896]{1,0:T(8,128)(2,1)S(1)}, u32[]{:S(2)}, u32[]{:S(2)}) collective-permute-start(bf16[128,896]{1,0:T(8,128)(2,1)S(1)} %get-tuple-element.39), channel_id=1, source_target_pairs={{0,32},{1,33},{2,34},{3,35},{32,0},{33,1},{34,2},{35,3},{4,36},{5,... | collective-permute-start | bytes 688136 | tf_op jit(solution)/shard_map/ppermute | solution.py:178
  138.9 2.3 collective-permute-done.8.refs_2_
  141.2 9.2 %collective-permute-start.13 = (bf16[128,896]{1,0:T(8,128)(2,1)S(1)}, bf16[128,896]{1,0:T(8,128)(2,1)S(1)}, u32[]{:S(2)}, u32[]{:S(2)}) collective-permute-start(bf16[128,896]{1,0:T(8,128)(2,1)S(1)} %get-tuple-element.37), channel_id=1, source_target_pairs={{0,34},{1,35},{2,32},{3,33},{32,2},{33,3},{34,0},{35,1},{4,38},{5,... | collective-permute-start | bytes 688136 | tf_op jit(solution)/shard_map/ppermute | solution.py:178
  150.4 15.1 %collective-permute-start.14 = (bf16[128,896]{1,0:T(8,128)(2,1)S(1)}, bf16[128,896]{1,0:T(8,128)(2,1)S(1)}, u32[]{:S(2)}, u32[]{:S(2)}) collective-permute-start(bf16[128,896]{1,0:T(8,128)(2,1)S(1)} %get-tuple-element.36), channel_id=1, source_target_pairs={{0,35},{1,32},{2,33},{3,34},{32,3},{33,0},{34,1},{35,2},{4,39},{5,... | collective-permute-start | bytes 688136 | tf_op jit(solution)/shard_map/ppermute | solution.py:178
  165.5 2.3 fusion.16
  167.7 2.6 collective-permute-start.16
  170.3 2.7 collective-permute-start.17
  173.1 7.9 %collective-permute-start.18 = (bf16[128,896]{1,0:T(8,128)(2,1)}, bf16[128,896]{1,0:T(8,128)(2,1)}, u32[]{:S(2)}, u32[]{:S(2)}) collective-permute-start(bf16[128,896]{1,0:T(8,128)(2,1)} %get-tuple-element.41), channel_id=1, source_target_pairs={{0,34},{1,35},{2,32},{3,33},{32,2},{33,3},{34,0},{35,1},{4,38},{5,... | collective-permute-start | bytes 688136 | tf_op jit(solution)/shard_map/ppermute | solution.py:178
  181.0 18.0 %collective-permute-start.19 = (bf16[128,896]{1,0:T(8,128)(2,1)}, bf16[128,896]{1,0:T(8,128)(2,1)}, u32[]{:S(2)}, u32[]{:S(2)}) collective-permute-start(bf16[128,896]{1,0:T(8,128)(2,1)} %get-tuple-element.40), channel_id=1, source_target_pairs={{0,35},{1,32},{2,33},{3,34},{32,3},{33,0},{34,1},{35,2},{4,39},{5,... | collective-permute-start | bytes 688136 | tf_op jit(solution)/shard_map/ppermute | solution.py:178
  198.9 5.0 %collective-permute-done.14.refs_7_ = bf16[128,896]{1,0:T(8,128)(2,1)S(1)} collective-permute-done((bf16[128,896]{1,0:T(8,128)(2,1)S(1)}, bf16[128,896]{1,0:T(8,128)(2,1)S(1)}, u32[]{:S(2)}, u32[]{:S(2)}) %collective-permute-start.14) | collective-permute-done | bytes 229408 | tf_op jit(solution)/shard_map/ppermute | solution.py:178
  204.6 4.2 %shard_map.88 = (bf16[512,896]{1,0:T(8,128)(2,1)}, f32[1]{0:T(128)}) custom-call(s32[1]{0:T(128)} %get-tuple-element.47.near, f32[512,1792]{1,0:T(8,128)} %fusion.24.projected, bf16[2,128,896]{2,1,0:T(8,128)(2,1)} %get-tuple-element.17.refs_0_, bf16[2,128,896]{2,1,0:T(8,128)(2,1)} %copy-done, bf16[2,128,896]{2,1,0:T(8,128)(2,1)} %copy-done.1, ...), custom_call_target="tpu_custom_call" | custom-call | tf_op jit(solution)/shard_map/pallas_call | solution.py:109
  208.8 2.8 convolution_convert_fusion.4
  212.6 1.6 convolution_convert_fusion.1
  214.2 1.6 collective-permute-start.25
  215.9 3.6 %collective-permute-done.17.refs_5_ = bf16[128,896]{1,0:T(8,128)(2,1)} collective-permute-done((bf16[128,896]{1,0:T(8,128)(2,1)}, bf16[128,896]{1,0:T(8,128)(2,1)}, u32[]{:S(2)}, u32[]{:S(2)}) %collective-permute-start.17) | collective-permute-done | bytes 229408 | tf_op jit(solution)/shard_map/ppermute | solution.py:178
  219.4 4.2 %shard_map.89 = (bf16[512,896]{1,0:T(8,128)(2,1)}, f32[1]{0:T(128)}) custom-call(s32[1]{0:T(128)} %get-tuple-element.47.near, f32[512,1792]{1,0:T(8,128)} %fusion.24.projected, bf16[2,128,896]{2,1,0:T(8,128)(2,1)} %get-tuple-element.17.refs_0_, bf16[2,128,896]{2,1,0:T(8,128)(2,1)} %copy-done, bf16[2,128,896]{2,1,0:T(8,128)(2,1)} %copy-done.1, ...), custom_call_target="tpu_custom_call" | custom-call | tf_op jit(solution)/shard_map/pallas_call | solution.py:109
  225.6 8.8 %collective-permute-done.23 = bf16[1024,448]{0,1:T(8,128)(2,1)} collective-permute-done((bf16[1024,448]{0,1:T(8,128)(2,1)}, bf16[1024,448]{0,1:T(8,128)(2,1)}, u32[]{:S(2)}, u32[]{:S(2)}) %collective-permute-start.23) | collective-permute-done | bytes 917536 | tf_op jit(solution)/shard_map/ppermute | solution.py:22
  234.4 2.1 add_convert_fusion.1
  236.5 1.5 pad_maximum_fusion.3
  238.1 2.0 add_convert_fusion
  240.1 1.4 pad_maximum_fusion.4
  241.5 2.5 collective-permute-start.26
  244.0 4.1 %convolution_convert_fusion = bf16[512,2048]{1,0:T(8,128)(2,1)S(1)} fusion(bf16[512,1792]{1,0:T(8,128)(2,1)S(1)} %pad_maximum_fusion.2, bf16[2048,1792]{0,1:T(8,128)(2,1)S(1)} %bitcast.43), kind=kOutput, calls=%fused_computation.2 | convolution fusion | flops 3759144960 | bytes 11272192 | tf_op jit(solution)/shard_map/dot_general | solution.py:124
  249.4 4.3 %collective-permute-start.20 = (bf16[128,2048]{1,0:T(8,128)(2,1)}, bf16[128,2048]{1,0:T(8,128)(2,1)S(1)}, u32[]{:S(2)}, u32[]{:S(2)}) collective-permute-start(bf16[128,2048]{1,0:T(8,128)(2,1)} %get-tuple-element.33), channel_id=1, source_target_pairs={{0,3},{1,0},{2,1},{3,2},{4,7},{5,4},{6,5},{7,6},{8,11},{9,8},{10,9... | collective-permute-start | bytes 1572872 | tf_op jit(solution)/shard_map/ppermute | solution.py:22
  253.7 8.1 %collective-permute-start.21 = (bf16[128,2048]{1,0:T(8,128)(2,1)}, bf16[128,2048]{1,0:T(8,128)(2,1)}, u32[]{:S(2)}, u32[]{:S(2)}) collective-permute-start(bf16[128,2048]{1,0:T(8,128)(2,1)} %get-tuple-element.35), channel_id=1, source_target_pairs={{0,2},{1,3},{2,0},{3,1},{4,6},{5,7},{6,4},{7,5},{8,10},{9,11},{10,... | collective-permute-start | bytes 1572872 | tf_op jit(solution)/shard_map/ppermute | solution.py:22
  261.8 1.5 collective-permute-start.22
  264.6 4.1 %fusion.8 = f32[2048,448]{0,1:T(8,128)} fusion(bf16[512,896]{1,0:T(8,128)(2,1)S(1)} %copy-done.3, bf16[128,2048]{1,0:T(8,128)(2,1)} %collective-permute-done.2, bf16[128,2048]{1,0:T(8,128)(2,1)S(1)} %copy-done.9, bf16[128,2048]{1,0:T(8,128)(2,1)S(1)} %copy-done.7, bf16[128,2048]{1,0:T(8,128)(2,1)S(1)} %bitcast_select_fusion), kind=kOutput, calls=%fused_computation.23 | convolution fusion | flops 947912704 | bytes 6291456 | tf_op jit(solution)/shard_map/dot_general | solution.py:124
  268.9 36.9 %all_to_all.9 = f32[16,1,2]{2,1,0:T(1,128)S(1)} all-to-all(f32[16,1,2]{2,1,0:T(1,128)S(1)} %copy.10), channel_id=1, replica_groups=mesh['y'=4,'zh'=2,'core'=2,'x'=4,'zl'=4] {'x','zl'}, dimensions={0} | all-to-all | bytes 256 | tf_op jit(solution)/shard_map/all_to_all | solution.py:224
  308.4 2.3 fusion.7
  310.8 5.4 %fusion = bf16[1,2048,448]{1,2,0:T(8,128)(2,1)} fusion(bf16[2048,448]{0,1:T(8,128)(2,1)} %collective-permute-done.26, f32[2048,448]{0,1:T(8,128)} %fusion.8, bf16[2048,448]{0,1:T(8,128)(2,1)} %collective-permute-done.24, f32[]{:T(128)} %bitcast.22), kind=kLoop, calls=%fused_computation.4 | loop fusion | flops 5505024 | bytes 9175044 | tf_op jit(solution)/shard_map/broadcast_in_dim | solution.py:235
  (80 shorter events, 15.1 us)
Async XLA Ops:
  0.6 94.4 %collective-permute-start.6 = (bf16[4,128,7168]{2,1,0:T(8,128)(2,1)}, bf16[4,128,7168]{2,1,0:T(8,128)(2,1)}, u32[]{:S(2)}, u32[]{:S(2)}) collective-permute-start(bf16[4,128,7168]{2,1,0:T(8,128)(2,1)} %mine.5), channel_id=1, source_target_pairs={{0,16},{16,0},{1,17},{17,1},{2,18},{18,2},{3,19},{19,3},{4,20},{20... | collective-permute-start | bytes 22020104 | tf_op jit(solution)/shard_map/ppermute | solution.py:27
  5.7 15.5 %collective-permute-start = (bf16[128,2048]{1,0:T(8,128)(2,1)S(1)}, bf16[128,2048]{1,0:T(8,128)(2,1)S(1)}, u32[]{:S(2)}, u32[]{:S(2)}) collective-permute-start(bf16[128,2048]{1,0:T(8,128)(2,1)S(1)} %bitcast_select_fusion), channel_id=1, source_target_pairs={{0,1},{1,2},{2,3},{3,0},{4,5},{5,6},{6,7},{7,4},{8,9},{9,10},{10,1... | collective-permute-start | bytes 1572872 | tf_op jit(solution)/shard_map/ppermute | solution.py:22
  5.8 54.5 %collective-permute-start.3 = (bf16[2048,448]{0,1:T(8,128)(2,1)}, bf16[2048,448]{0,1:T(8,128)(2,1)}, u32[]{:S(2)}, u32[]{:S(2)}) collective-permute-start(bf16[2048,448]{0,1:T(8,128)(2,1)} %bitcast.44), channel_id=1, source_target_pairs={{0,8},{4,12},{8,0},{12,4},{1,9},{5,13},{9,1},{13,5},{2,10},{6,14},... | collective-permute-start | bytes 5505032 | tf_op jit(solution)/shard_map/ppermute | solution.py:22
  8.5 79.8 %collective-permute-start.4 = (bf16[2048,448]{0,1:T(8,128)(2,1)}, bf16[2048,448]{0,1:T(8,128)(2,1)}, u32[]{:S(2)}, u32[]{:S(2)}) collective-permute-start(bf16[2048,448]{0,1:T(8,128)(2,1)} %bitcast.45), channel_id=1, source_target_pairs={{0,12},{4,0},{8,4},{12,8},{1,13},{5,1},{9,5},{13,9},{2,14},{6,2},{... | collective-permute-start | bytes 5505032 | tf_op jit(solution)/shard_map/ppermute | solution.py:22
  9.3 79.6 %collective-permute-start.5 = (bf16[2048,448]{0,1:T(8,128)(2,1)}, bf16[2048,448]{0,1:T(8,128)(2,1)}, u32[]{:S(2)}, u32[]{:S(2)}) collective-permute-start(bf16[2048,448]{0,1:T(8,128)(2,1)} %bitcast.46), channel_id=1, source_target_pairs={{0,4},{4,8},{8,12},{12,0},{1,5},{5,9},{9,13},{13,1},{2,6},{6,10},{... | collective-permute-start | bytes 5505032 | tf_op jit(solution)/shard_map/ppermute | solution.py:22
  21.2 39.1 %copy-start.6 = (bf16[128,2048]{1,0:T(8,128)(2,1)}, bf16[128,2048]{1,0:T(8,128)(2,1)S(1)}, u32[]{:S(2)}) copy-start(bf16[128,2048]{1,0:T(8,128)(2,1)S(1)} %collective-permute-done) | copy-start | bytes 1572868
  21.2 24.6 %collective-permute-start.1 = (bf16[128,2048]{1,0:T(8,128)(2,1)S(1)}, bf16[128,2048]{1,0:T(8,128)(2,1)S(1)}, u32[]{:S(2)}, u32[]{:S(2)}) collective-permute-start(bf16[128,2048]{1,0:T(8,128)(2,1)S(1)} %bitcast_select_fusion), channel_id=1, source_target_pairs={{0,2},{1,3},{2,0},{3,1},{4,6},{5,7},{6,4},{7,5},{8,10},{9,11},{10,... | collective-permute-start | bytes 1572872 | tf_op jit(solution)/shard_map/ppermute | solution.py:22
  45.8 5.0 %copy-start.8 = (bf16[128,2048]{1,0:T(8,128)(2,1)}, bf16[128,2048]{1,0:T(8,128)(2,1)S(1)}, u32[]{:S(2)}) copy-start(bf16[128,2048]{1,0:T(8,128)(2,1)S(1)} %collective-permute-done.1) | copy-start | bytes 1572868
  45.8 13.2 %collective-permute-start.2 = (bf16[128,2048]{1,0:T(8,128)(2,1)S(1)}, bf16[128,2048]{1,0:T(8,128)(2,1)}, u32[]{:S(2)}, u32[]{:S(2)}) collective-permute-start(bf16[128,2048]{1,0:T(8,128)(2,1)S(1)} %bitcast_select_fusion), channel_id=1, source_target_pairs={{0,3},{1,0},{2,1},{3,2},{4,7},{5,4},{6,5},{7,6},{8,11},{9,8},{10,9... | collective-permute-start | bytes 1572872 | tf_op jit(solution)/shard_map/ppermute | solution.py:22
  50.8 38.2 %copy-start.2 = (bf16[1,2048,448]{1,2,0:T(8,128)(2,1)S(1)}, bf16[1,2048,448]{1,2,0:T(8,128)(2,1)}, u32[]{:S(2)}) copy-start(bf16[1,2048,448]{1,2,0:T(8,128)(2,1)} %param.8) | copy-start | bytes 5505028
  100.3 27.8 %collective-permute-start.10 = (bf16[4,128,896]{2,1,0:T(8,128)(2,1)}, bf16[4,128,896]{2,1,0:T(8,128)(2,1)}, u32[]{:S(2)}, u32[]{:S(2)}) collective-permute-start(bf16[4,128,896]{2,1,0:T(8,128)(2,1)} %get-tuple-element.22), channel_id=1, source_target_pairs={{64,0},{128,64},{192,128},{32,96},{96,160},{160,224},{65,1},{129,6... | collective-permute-start | bytes 2752520 | tf_op jit(solution)/shard_map/ppermute | solution.py:170
  106.9 32.0 %collective-permute-start.7 = (bf16[2,128,896]{2,1,0:T(8,128)(2,1)}, bf16[2,128,896]{2,1,0:T(8,128)(2,1)S(1)}, u32[]{:S(2)}, u32[]{:S(2)}) collective-permute-start(bf16[2,128,896]{2,1,0:T(8,128)(2,1)} %get-tuple-element.18), channel_id=1, source_target_pairs={{0,1},{1,2},{2,3},{3,0},{4,5},{5,6},{6,7},{7,4},{8,9},{9,10},{10,1... | collective-permute-start | bytes 1376264 | tf_op jit(solution)/shard_map/ppermute | solution.py:22
  108.3 32.9 %collective-permute-start.8 = (bf16[2,128,896]{2,1,0:T(8,128)(2,1)}, bf16[2,128,896]{2,1,0:T(8,128)(2,1)S(1)}, u32[]{:S(2)}, u32[]{:S(2)}) collective-permute-start(bf16[2,128,896]{2,1,0:T(8,128)(2,1)} %get-tuple-element.19), channel_id=1, source_target_pairs={{0,2},{1,3},{2,0},{3,1},{4,6},{5,7},{6,4},{7,5},{8,10},{9,11},{10,... | collective-permute-start | bytes 1376264 | tf_op jit(solution)/shard_map/ppermute | solution.py:22
  110.3 40.1 %collective-permute-start.15 = (bf16[4,128,896]{2,1,0:T(8,128)(2,1)}, bf16[4,128,896]{2,1,0:T(8,128)(2,1)}, u32[]{:S(2)}, u32[]{:S(2)}) collective-permute-start(bf16[4,128,896]{2,1,0:T(8,128)(2,1)} %get-tuple-element.25), channel_id=1, source_target_pairs={{64,0},{128,64},{192,128},{32,96},{96,160},{160,224},{65,1},{129,6... | collective-permute-start | bytes 2752520 | tf_op jit(solution)/shard_map/ppermute | solution.py:170
  121.0 46.7 %collective-permute-start.9 = (bf16[2,128,896]{2,1,0:T(8,128)(2,1)}, bf16[2,128,896]{2,1,0:T(8,128)(2,1)}, u32[]{:S(2)}, u32[]{:S(2)}) collective-permute-start(bf16[2,128,896]{2,1,0:T(8,128)(2,1)} %get-tuple-element.20), channel_id=1, source_target_pairs={{0,3},{1,0},{2,1},{3,2},{4,7},{5,4},{6,5},{7,6},{8,11},{9,8},{10,9... | collective-permute-start | bytes 1376264 | tf_op jit(solution)/shard_map/ppermute | solution.py:22
  128.0 37.5 %copy-start.5 = (bf16[4,128,896]{2,1,0:T(8,128)(2,1)S(1)}, bf16[4,128,896]{2,1,0:T(8,128)(2,1)}, u32[]{:S(2)}) copy-start(bf16[4,128,896]{2,1,0:T(8,128)(2,1)} %get-tuple-element.24) | copy-start | bytes 2752516
  129.8 40.6 %collective-permute-start.11 = (bf16[128,896]{1,0:T(8,128)(2,1)S(1)}, bf16[128,896]{1,0:T(8,128)(2,1)S(1)}, u32[]{:S(2)}, u32[]{:S(2)}) collective-permute-start(bf16[128,896]{1,0:T(8,128)(2,1)S(1)} %get-tuple-element.39), channel_id=1, source_target_pairs={{0,32},{1,33},{2,34},{3,35},{32,0},{33,1},{34,2},{35,3},{4,36},{5,... | collective-permute-start | bytes 688136 | tf_op jit(solution)/shard_map/ppermute | solution.py:178
  138.8 65.8 %copy-start = (bf16[2,128,896]{2,1,0:T(8,128)(2,1)}, bf16[2,128,896]{2,1,0:T(8,128)(2,1)S(1)}, u32[]{:S(2)}) copy-start(bf16[2,128,896]{2,1,0:T(8,128)(2,1)S(1)} %collective-permute-done.7.refs_1_) | copy-start | bytes 1376260
  138.9 34.2 %collective-permute-start.12 = (bf16[128,896]{1,0:T(8,128)(2,1)S(1)}, bf16[128,896]{1,0:T(8,128)(2,1)S(1)}, u32[]{:S(2)}, u32[]{:S(2)}) collective-permute-start(bf16[128,896]{1,0:T(8,128)(2,1)S(1)} %get-tuple-element.38), channel_id=1, source_target_pairs={{0,33},{1,34},{2,35},{3,32},{32,1},{33,2},{34,3},{35,0},{4,37},{5,... | collective-permute-start | bytes 688136 | tf_op jit(solution)/shard_map/ppermute | solution.py:178
  141.2 63.4 %copy-start.1 = (bf16[2,128,896]{2,1,0:T(8,128)(2,1)}, bf16[2,128,896]{2,1,0:T(8,128)(2,1)S(1)}, u32[]{:S(2)}) copy-start(bf16[2,128,896]{2,1,0:T(8,128)(2,1)S(1)} %collective-permute-done.8.refs_2_) | copy-start | bytes 1376260
  141.2 39.7 %collective-permute-start.13 = (bf16[128,896]{1,0:T(8,128)(2,1)S(1)}, bf16[128,896]{1,0:T(8,128)(2,1)S(1)}, u32[]{:S(2)}, u32[]{:S(2)}) collective-permute-start(bf16[128,896]{1,0:T(8,128)(2,1)S(1)} %get-tuple-element.37), channel_id=1, source_target_pairs={{0,34},{1,35},{2,32},{3,33},{32,2},{33,3},{34,0},{35,1},{4,38},{5,... | collective-permute-start | bytes 688136 | tf_op jit(solution)/shard_map/ppermute | solution.py:178
  150.4 53.5 %collective-permute-start.14 = (bf16[128,896]{1,0:T(8,128)(2,1)S(1)}, bf16[128,896]{1,0:T(8,128)(2,1)S(1)}, u32[]{:S(2)}, u32[]{:S(2)}) collective-permute-start(bf16[128,896]{1,0:T(8,128)(2,1)S(1)} %get-tuple-element.36), channel_id=1, source_target_pairs={{0,35},{1,32},{2,33},{3,34},{32,3},{33,0},{34,1},{35,2},{4,39},{5,... | collective-permute-start | bytes 688136 | tf_op jit(solution)/shard_map/ppermute | solution.py:178
  167.7 46.5 %collective-permute-start.16 = (bf16[128,896]{1,0:T(8,128)(2,1)}, bf16[128,896]{1,0:T(8,128)(2,1)}, u32[]{:S(2)}, u32[]{:S(2)}) collective-permute-start(bf16[128,896]{1,0:T(8,128)(2,1)} %get-tuple-element.43), channel_id=1, source_target_pairs={{0,32},{1,33},{2,34},{3,35},{32,0},{33,1},{34,2},{35,3},{4,36},{5,... | collective-permute-start | bytes 688136 | tf_op jit(solution)/shard_map/ppermute | solution.py:178
  170.3 33.6 %copy-start.10 = (bf16[128,896]{1,0:T(8,128)(2,1)}, bf16[128,896]{1,0:T(8,128)(2,1)S(1)}, u32[]{:S(2)}) copy-start(bf16[128,896]{1,0:T(8,128)(2,1)S(1)} %collective-permute-done.11.refs_4_) | copy-start | bytes 688132
  170.3 49.1 %collective-permute-start.17 = (bf16[128,896]{1,0:T(8,128)(2,1)}, bf16[128,896]{1,0:T(8,128)(2,1)}, u32[]{:S(2)}, u32[]{:S(2)}) collective-permute-start(bf16[128,896]{1,0:T(8,128)(2,1)} %get-tuple-element.42), channel_id=1, source_target_pairs={{0,33},{1,34},{2,35},{3,32},{32,1},{33,2},{34,3},{35,0},{4,37},{5,... | collective-permute-start | bytes 688136 | tf_op jit(solution)/shard_map/ppermute | solution.py:178
  173.1 30.8 %copy-start.11 = (bf16[128,896]{1,0:T(8,128)(2,1)}, bf16[128,896]{1,0:T(8,128)(2,1)S(1)}, u32[]{:S(2)}) copy-start(bf16[128,896]{1,0:T(8,128)(2,1)S(1)} %collective-permute-done.12.refs_5_) | copy-start | bytes 688132
  173.1 46.4 %collective-permute-start.18 = (bf16[128,896]{1,0:T(8,128)(2,1)}, bf16[128,896]{1,0:T(8,128)(2,1)}, u32[]{:S(2)}, u32[]{:S(2)}) collective-permute-start(bf16[128,896]{1,0:T(8,128)(2,1)} %get-tuple-element.41), channel_id=1, source_target_pairs={{0,34},{1,35},{2,32},{3,33},{32,2},{33,3},{34,0},{35,1},{4,38},{5,... | collective-permute-start | bytes 688136 | tf_op jit(solution)/shard_map/ppermute | solution.py:178
  180.9 23.0 %copy-start.12 = (bf16[128,896]{1,0:T(8,128)(2,1)}, bf16[128,896]{1,0:T(8,128)(2,1)S(1)}, u32[]{:S(2)}) copy-start(bf16[128,896]{1,0:T(8,128)(2,1)S(1)} %collective-permute-done.13.refs_6_) | copy-start | bytes 688132
  181.0 38.5 %collective-permute-start.19 = (bf16[128,896]{1,0:T(8,128)(2,1)}, bf16[128,896]{1,0:T(8,128)(2,1)}, u32[]{:S(2)}, u32[]{:S(2)}) collective-permute-start(bf16[128,896]{1,0:T(8,128)(2,1)} %get-tuple-element.40), channel_id=1, source_target_pairs={{0,35},{1,32},{2,33},{3,34},{32,3},{33,0},{34,1},{35,2},{4,39},{5,... | collective-permute-start | bytes 688136 | tf_op jit(solution)/shard_map/ppermute | solution.py:178
  203.9 0.7 copy-start.13
  208.8 3.8 %copy-start.4 = (bf16[512,896]{1,0:T(8,128)(2,1)S(1)}, bf16[512,896]{1,0:T(8,128)(2,1)}, u32[]{:S(2)}) copy-start(bf16[512,896]{1,0:T(8,128)(2,1)} %get-tuple-element.23) | copy-start | bytes 2752516
  211.5 22.8 %collective-permute-start.23 = (bf16[1024,448]{0,1:T(8,128)(2,1)}, bf16[1024,448]{0,1:T(8,128)(2,1)}, u32[]{:S(2)}, u32[]{:S(2)}) collective-permute-start(bf16[1024,448]{0,1:T(8,128)(2,1)} %convolution_convert_fusion.4), channel_id=1, source_target_pairs={{0,4},{4,8},{8,12},{12,0},{1,5},{5,9},{9,13},{13,1},{2,6},{6,10},{... | collective-permute-start | bytes 2752520 | tf_op jit(solution)/shard_map/ppermute | solution.py:22
  214.2 23.8 %collective-permute-start.25 = (bf16[1024,448]{0,1:T(8,128)(2,1)}, bf16[1024,448]{0,1:T(8,128)(2,1)}, u32[]{:S(2)}, u32[]{:S(2)}) collective-permute-start(bf16[1024,448]{0,1:T(8,128)(2,1)} %convolution_convert_fusion.1), channel_id=1, source_target_pairs={{0,12},{4,0},{8,4},{12,8},{1,13},{5,1},{9,5},{13,9},{2,14},{6,2},{... | collective-permute-start | bytes 2752520 | tf_op jit(solution)/shard_map/ppermute | solution.py:22
  223.6 1.2 copy-start.3
  234.4 9.6 %slice-start = ((s8[7340032]{0:T(1024)(128)(4,1)}), s8[4194304]{0:T(1024)(128)(4,1)S(1)}, s32[]{:S(2)}) async-start(s8[7340032]{0:T(1024)(128)(4,1)} %bitcast.42), calls=%async_computation.1 | async-start | bytes 8388608
  238.1 5.9 %slice-start.1 = ((s8[7340032]{0:T(1024)(128)(4,1)}), s8[3145728]{0:T(1024)(128)(4,1)S(1)}, s32[]{:S(2)}) async-start(s8[7340032]{0:T(1024)(128)(4,1)} %bitcast.42), calls=%async_computation.2 | async-start | bytes 6291456
  238.1 72.7 %collective-permute-start.24 = (bf16[2048,448]{0,1:T(8,128)(2,1)}, bf16[2048,448]{0,1:T(8,128)(2,1)}, u32[]{:S(2)}, u32[]{:S(2)}) collective-permute-start(bf16[2048,448]{0,1:T(8,128)(2,1)} %pad_maximum_fusion.3), channel_id=1, source_target_pairs={{0,4},{4,8},{8,12},{12,0},{1,5},{5,9},{9,13},{13,1},{2,6},{6,10},{... | collective-permute-start | bytes 5505032 | tf_op jit(solution)/shard_map/ppermute | solution.py:22
  241.5 69.3 %collective-permute-start.26 = (bf16[2048,448]{0,1:T(8,128)(2,1)}, bf16[2048,448]{0,1:T(8,128)(2,1)}, u32[]{:S(2)}, u32[]{:S(2)}) collective-permute-start(bf16[2048,448]{0,1:T(8,128)(2,1)} %pad_maximum_fusion.4), channel_id=1, source_target_pairs={{0,12},{4,0},{8,4},{12,8},{1,13},{5,1},{9,5},{13,9},{2,14},{6,2},{... | collective-permute-start | bytes 5505032 | tf_op jit(solution)/shard_map/ppermute | solution.py:22
  248.2 16.4 %copy-start.7 = (bf16[128,2048]{1,0:T(8,128)(2,1)S(1)}, bf16[128,2048]{1,0:T(8,128)(2,1)}, u32[]{:S(2)}) copy-start(bf16[128,2048]{1,0:T(8,128)(2,1)} %copy-done.6) | copy-start | bytes 1572868
  248.2 16.4 %copy-start.9 = (bf16[128,2048]{1,0:T(8,128)(2,1)S(1)}, bf16[128,2048]{1,0:T(8,128)(2,1)}, u32[]{:S(2)}) copy-start(bf16[128,2048]{1,0:T(8,128)(2,1)} %copy-done.8) | copy-start | bytes 1572868
  249.4 59.0 %collective-permute-start.20 = (bf16[128,2048]{1,0:T(8,128)(2,1)}, bf16[128,2048]{1,0:T(8,128)(2,1)S(1)}, u32[]{:S(2)}, u32[]{:S(2)}) collective-permute-start(bf16[128,2048]{1,0:T(8,128)(2,1)} %get-tuple-element.33), channel_id=1, source_target_pairs={{0,3},{1,0},{2,1},{3,2},{4,7},{5,4},{6,5},{7,6},{8,11},{9,8},{10,9... | collective-permute-start | bytes 1572872 | tf_op jit(solution)/shard_map/ppermute | solution.py:22
  253.7 54.7 %collective-permute-start.21 = (bf16[128,2048]{1,0:T(8,128)(2,1)}, bf16[128,2048]{1,0:T(8,128)(2,1)}, u32[]{:S(2)}, u32[]{:S(2)}) collective-permute-start(bf16[128,2048]{1,0:T(8,128)(2,1)} %get-tuple-element.35), channel_id=1, source_target_pairs={{0,2},{1,3},{2,0},{3,1},{4,6},{5,7},{6,4},{7,5},{8,10},{9,11},{10,... | collective-permute-start | bytes 1572872 | tf_op jit(solution)/shard_map/ppermute | solution.py:22
  261.8 46.6 %collective-permute-start.22 = (bf16[128,2048]{1,0:T(8,128)(2,1)}, bf16[128,2048]{1,0:T(8,128)(2,1)}, u32[]{:S(2)}, u32[]{:S(2)}) collective-permute-start(bf16[128,2048]{1,0:T(8,128)(2,1)} %get-tuple-element.34), channel_id=1, source_target_pairs={{0,1},{1,2},{2,3},{3,0},{4,5},{5,6},{6,7},{7,4},{8,9},{9,10},{10,1... | collective-permute-start | bytes 1572872 | tf_op jit(solution)/shard_map/ppermute | solution.py:22

commit v3 on v2

--- a/solution.py
+++ b/solution.py
@@ -51,7 +51,7 @@
             cut = slice(z * width, (z + 1) * width)
             spread[chunk, (z - info[ZL]) & 3] = jnp.concatenate([h[:, cut] for h in halves], axis=1)
     for index, out in enumerate(outs):
-        out[...] = spread[:, index] if PIECES[piece] == "here" else spread[index]
+        out[...] = spread[index // 4, index % 4] if PIECES[piece] == "here" else spread[index]
 
 
 def prepare(mine, theirs, info, name):
@@ -59,7 +59,7 @@
     piece = PIECES.index(name)
     rows = min(ROWS, tokens)
     wide = features // 8
-    lead = [(2,)] * 4 if name == "here" else [(4,)] * 2
+    lead = [()] * 8 if name == "here" else [(4,)] * 2
 
     def taken(kept):
         def index(i, info):
@@ -81,7 +81,7 @@
             out_specs=[written(dims) for dims in lead],
             scratch_shapes=[pltpu.VMEM((2, 4, rows, wide), jnp.bfloat16)],
         ),
-        compiler_params=pltpu.CompilerParams(dimension_semantics=("arbitrary",)),
+        compiler_params=pltpu.CompilerParams(dimension_semantics=("arbitrary",), vmem_limit_bytes=12 << 20),
     )(info, mine, theirs)
 
 
@@ -91,7 +91,7 @@
     total = jnp.zeros((), jnp.float32)
     for k in range(4):
         cut = slice(k * rows, (k + 1) * rows)
-        target = jnp.where(near[0] == 1, own[k][0].astype(jnp.float32), cross[k][...].astype(jnp.float32))
+        target = jnp.where(near[0] == 1, own[k][...].astype(jnp.float32), cross[k][...].astype(jnp.float32))
         residual = projected[cut] - target
         out[cut] = residual.astype(jnp.bfloat16)
         total = total + jnp.sum(residual * residual)
@@ -114,9 +114,9 @@
         ),
         grid=(1,),
         in_specs=[smem, pl.BlockSpec((tokens, wide), lambda i: (0, chunk))]
-        + [pl.BlockSpec((1, rows, wide), lambda i: (chunk, 0, 0))] * 4
-        + [whole((rows, wide))] * 4,
+        + [whole((rows, wide))] * 8,
         out_specs=(whole((tokens, wide)), smem),
+        compiler_params=pltpu.CompilerParams(vmem_limit_bytes=16 << 20),
     )(near, projected, *own, *cross)
 
 
@@ -178,10 +178,15 @@
             sent.append(lax.ppermute(slab, ("zh", "zl"), route))
         return sent
 
-    crossed = send_across(0)
+    def send_own(chunk):
+        slabs = here_slabs[4 * chunk : 4 * chunk + 4]
+        return [slabs[0]] + [rotate(slabs[k], "zl", k) for k in (1, 2, 3)]
+
+    crossed_first = send_across(0)
     here_slabs = prepare(teacher_states, theirs, info, "here")
-    own = [here_slabs[0]] + [rotate(here_slabs[k], "zl", k) for k in (1, 2, 3)]
-    crossed = crossed + send_across(1)
+    own_first = send_own(0)
+    crossed_second = send_across(1)
+    own_second = send_own(1)
 
     rows = jnp.concatenate(students, axis=0)
     w_all = lax.optimization_barrier(jnp.concatenate([w_opp, w_next, w_prev, weights], axis=1))
@@ -192,39 +197,39 @@
     def grad(part, residual):
         return dot(part, residual, 0, 0)
 
-    first_res, squares_first = residual_of(near, projected, own, 0, crossed[:4])
+    first_res, squares_first = residual_of(near, projected, own_first, 0, crossed_first)
     opp_res, next_res = first_res[:, :width], first_res[:, width:]
     opp_top = grad(top, opp_res).astype(jnp.bfloat16)
     opp_bot = grad(bot, opp_res).astype(jnp.bfloat16)
     next_bot = grad(bot, next_res).astype(jnp.bfloat16)
     up_top = rotate(opp_top, "x", 1)
     down_bot = rotate(opp_bot, "x", -1)
-    second_res, squares_second = residual_of(near, projected, own, 1, crossed[4:])
+    second_res, squares_second = residual_of(near, projected, own_second, 1, crossed_second)
+
+    sums = jnp.stack([squares_first[0] + squares_second[0], valid_counts[0].astype(jnp.float32)])
+    copies = jnp.broadcast_to(sums, (lax.axis_size(DP), 2))
+    sums = jnp.sum(lax.all_to_all(copies, DP, split_axis=0, concat_axis=0, tiled=True), axis=0)
+    total = sums[1]
+    loss = sums[:1] / (total * (width * lax.axis_size(DP)))
+    factor = loss_scale / total
 
     next_top = (grad(top, next_res) + up_top.astype(jnp.float32)).astype(jnp.bfloat16)
-    next_part = jnp.concatenate([next_top, next_bot], axis=0)
+    next_part = lax.optimization_barrier((jnp.concatenate([next_top, next_bot], axis=0), sums))[0]
     from_prev = rotate(next_part, "x", 1)
     prev_res, own_res = second_res[:, :width], second_res[:, width:]
     prev_top = grad(top, prev_res).astype(jnp.bfloat16)
     prev_bot = (grad(bot, prev_res) + down_bot.astype(jnp.float32)).astype(jnp.bfloat16)
-    prev_part = jnp.concatenate([prev_top, prev_bot], axis=0)
+    prev_part = lax.optimization_barrier((jnp.concatenate([prev_top, prev_bot], axis=0), sums))[0]
     from_next = rotate(prev_part, "x", -1)
 
     residual = lax.optimization_barrier(jnp.concatenate([first_res, second_res], axis=1))
     student_part = dot(residual, w_all, 1, 1).astype(jnp.bfloat16)
+    student_part = lax.optimization_barrier((student_part, sums))[0]
     returned = []
     for k in (1, 2, 3):
         part = student_part[k * tokens : (k + 1) * tokens]
         returned.append(rotate(part, "zl", -k))
-    own_part = grad(rows, own_res)
-
-    sums = jnp.stack([squares_first[0] + squares_second[0], valid_counts[0].astype(jnp.float32)])
-    copies = jnp.broadcast_to(sums, (lax.axis_size(DP), 2))
-    copies, own_part = lax.optimization_barrier((copies, own_part))
-    sums = jnp.sum(lax.all_to_all(copies, DP, split_axis=0, concat_axis=0, tiled=True), axis=0)
-    total = sums[1]
-    loss = sums[:1] / (total * (width * lax.axis_size(DP)))
-    factor = loss_scale / total
+    own_part = lax.optimization_barrier(grad(rows, own_res))
 
     student_grad = student_part[:tokens].astype(jnp.float32)
     for part in returned:

time: 320 us -> 305 us (0.953)
  waiting for transfers between devices: 89.8 us -> 148 us
  blocking collectives: 36.9 us -> 0 us
  starting transfers between devices: 101 us -> 88.9 us
  other arithmetic: 26 us -> 16.9 us
  Pallas kernels: 24.2 us -> 15.6 us
  matrix products: 27.7 us -> 23.2 us
    ppermute x16 -> x19, waiting for transfers between devices: 81.3 us -> 123 us  [rotate(): lax.ppermute(block, axis, [(i, (i + distance) % n) for i in range(n)])]
    all_to_all x1 -> x0, blocking collectives: 36.9 us -> none  [compute(): lax.all_to_all(copies, DP, split_axis=0, concat_axis=0, tiled=True)]
    ppermute x8, starting transfers between devices: 64.5 us -> 35.2 us  [send_across(): sent.append(lax.ppermute(slab, ('zh', 'zl'), route))]
    ppermute x8, waiting for transfers between devices: 8.56 us -> 22.2 us  [send_across(): sent.append(lax.ppermute(slab, ('zh', 'zl'), route))]
    ppermute x16 -> x19, starting transfers between devices: 30.8 us -> 40.1 us  [rotate(): lax.ppermute(block, axis, [(i, (i + distance) % n) for i in range(n)])]
    all_to_all x0 -> x1, starting transfers between devices: none -> 7.76 us  [compute(): lax.all_to_all(copies, DP, split_axis=0, concat_axis=0, tiled=True)]
    pallas_call x2, Pallas kernels: 8.33 us -> 3.48 us  [residual_of(): pl.pallas_call(residual_body, out_shape=(jax.ShapeDtypeStruct((tokens, wi...]
    dot_general x9, matrix products: 27.7 us -> 23.2 us  [dot(): lax.dot_general(a, b, (((ca,), (cb,)), ((), ())), preferred_element_type=...]
  transfers between devices with their start and end apart: 27 -> 31, of which waited for: 9 -> 16; matrix products, arithmetic and copies ran while one was open for 16% -> 13% of each run, Pallas kernels for 6% -> 4%
where the time goes in v3:
time: 305 us; the launch traced here: 302 us
  waiting for transfers between devices  148 us (49%)
  starting transfers between devices  88.9 us (29%)
  matrix products  23.2 us (8%)
  other arithmetic  16.9 us (6%)
  Pallas kernels  15.6 us (5%)
  between operations  6.77 us (2%)
    ppermute x19, waiting for transfers between devices, rotate(): lax.ppermute(block, axis, [(i, (i + distance) % n) for i in range(n)])  123 us
    ppermute x19, starting transfers between devices, rotate(): lax.ppermute(block, axis, [(i, (i + distance) % n) for i in range(n)])  40.1 us
    ppermute x8, starting transfers between devices, send_across(): sent.append(lax.ppermute(slab, ('zh', 'zl'), route))  35.2 us
    dot_general x9, matrix products, dot(): lax.dot_general(a, b, (((ca,), (cb,)), ((), ())), preferred_element_type=...  23.2 us
    ppermute x8, waiting for transfers between devices, send_across(): sent.append(lax.ppermute(slab, ('zh', 'zl'), route))  22.2 us
    pallas_call x3, Pallas kernels, prepare(): pl.pallas_call(functools.partial(prepare_body, piece), out_shape=[jax.Sha...  12.1 us
    all_to_all x1, starting transfers between devices, compute(): lax.all_to_all(copies, DP, split_axis=0, concat_axis=0, tiled=True)  7.76 us
  transfers between devices with their start and end apart: 31, of which 16 were waited for; matrix products, arithmetic and copies ran while one was open for 13% of the time, Pallas kernels for 4%

profile of v3, /device:TPU:1, one launch (start us, length us, event | category | flops | bytes accessed | tf_op | source)
XLA Modules:
  0.0 302.3 jit_solution(8969138502886696673)
XLA Ops:
  0.6 3.3 %collective-permute-start.6 = (bf16[4,128,7168]{2,1,0:T(8,128)(2,1)}, bf16[4,128,7168]{2,1,0:T(8,128)(2,1)}, u32[]{:S(2)}, u32[]{:S(2)}) collective-permute-start(bf16[4,128,7168]{2,1,0:T(8,128)(2,1)} %mine.5), channel_id=1, source_target_pairs={{0,16},{16,0},{1,17},{17,1},{2,18},{18,2},{3,19},{19,3},{4,20},{20... | collective-permute-start | bytes 22020104 | tf_op jit(solution)/shard_map/ppermute | solution.py:27
  5.8 2.7 collective-permute-start.3
  10.0 11.2 %collective-permute-done = bf16[128,2048]{1,0:T(8,128)(2,1)S(1)} collective-permute-done((bf16[128,2048]{1,0:T(8,128)(2,1)S(1)}, bf16[128,2048]{1,0:T(8,128)(2,1)S(1)}, u32[]{:S(2)}, u32[]{:S(2)}) %collective-permute-start) | collective-permute-done | bytes 524320 | tf_op jit(solution)/shard_map/ppermute | solution.py:22
  23.7 22.0 %collective-permute-done.1 = bf16[128,2048]{1,0:T(8,128)(2,1)} collective-permute-done((bf16[128,2048]{1,0:T(8,128)(2,1)S(1)}, bf16[128,2048]{1,0:T(8,128)(2,1)}, u32[]{:S(2)}, u32[]{:S(2)}) %collective-permute-start.1) | collective-permute-done | bytes 524320 | tf_op jit(solution)/shard_map/ppermute | solution.py:22
  45.8 2.3 collective-permute-start.2
  50.2 8.6 %collective-permute-done.2 = bf16[128,2048]{1,0:T(8,128)(2,1)} collective-permute-done((bf16[128,2048]{1,0:T(8,128)(2,1)S(1)}, bf16[128,2048]{1,0:T(8,128)(2,1)}, u32[]{:S(2)}, u32[]{:S(2)}) %collective-permute-start.2) | collective-permute-done | bytes 524320 | tf_op jit(solution)/shard_map/ppermute | solution.py:22
  58.9 1.5 pad_maximum_fusion.1
  60.4 27.9 %collective-permute-done.4 = bf16[2048,448]{0,1:T(8,128)(2,1)} collective-permute-done((bf16[2048,448]{0,1:T(8,128)(2,1)}, bf16[2048,448]{0,1:T(8,128)(2,1)}, u32[]{:S(2)}, u32[]{:S(2)}) %collective-permute-start.4) | collective-permute-done | bytes 1835040 | tf_op jit(solution)/shard_map/ppermute | solution.py:22
  89.0 3.7 %pad_maximum_fusion = bf16[2048,1792]{0,1:T(8,128)(2,1)S(1)} fusion(bf16[2048,448]{0,1:T(8,128)(2,1)S(1)} %bitcast.48, bf16[2048,448]{0,1:T(8,128)(2,1)} %collective-permute-done.5, bf16[2048,448]{0,1:T(8,128)(2,1)} %collective-permute-done.4, bf16[2048,448]{0,1:T(8,128)(2,1)} %collective-permute-done.3), kind=kLoop, calls=%fused_computation | loop fusion | flops 29360128 | bytes 14680064 | tf_op jit(solution)/shard_map/concatenate | solution.py:192
  92.7 4.7 %shard_map.87 = (bf16[4,128,896]{2,1,0:T(8,128)(2,1)S(1)}, bf16[4,128,896]{2,1,0:T(8,128)(2,1)S(1)}) custom-call(s32[12]{0:T(128)S(1)} %concatenate.20.info, bf16[4,128,7168]{2,1,0:T(8,128)(2,1)S(1)} %bitcast.42, bf16[4,128,7168]{2,1,0:T(8,128)(2,1)} %collective-permute-done.6.theirs), custom_call_target="tpu_custom_call" | custom-call | tf_op jit(solution)/shard_map/pallas_call | solution.py:74
  100.1 5.3 %fusion.24.projected = f32[512,1792]{1,0:T(8,128)S(1)} fusion(bf16[2048,1792]{0,1:T(8,128)(2,1)S(1)} %pad_maximum_fusion, bf16[128,2048]{1,0:T(8,128)(2,1)} %collective-permute-done.2, bf16[128,2048]{1,0:T(8,128)(2,1)} %collective-permute-done.1, bf16[128,2048]{1,0:T(8,128)(2,1)S(1)} %collective-permute-done, bf16[128,2048]{1,0:T(8,128)(2,1)S(1)} %bitcast_select_fusion), kind=kOutput, calls=%fused_computation.59 | convolution fusion | flops 3766484992 | bytes 13107200 | tf_op jit(solution)/shard_map/dot_general | solution.py:124
  105.3 3.9 %shard_map.85 = (bf16[128,896]{1,0:T(8,128)(2,1)S(1)}, bf16[128,896]{1,0:T(8,128)(2,1)S(1)}, bf16[128,896]{1,0:T(8,128)(2,1)S(1)}, bf16[128,896]{1,0:T(8,128)(2,...) custom-call(s32[12]{0:T(128)S(1)} %concatenate.20.info, ...), custom_call_target="tpu_custom_call" | custom-call | tf_op jit(solution)/shard_map/pallas_call | solution.py:74
  109.3 1.5 collective-permute-start.7
  110.8 2.0 collective-permute-start.8
  112.8 1.7 collective-permute-start.9
  114.5 3.5 %shard_map.86 = (bf16[4,128,896]{2,1,0:T(8,128)(2,1)S(1)}, bf16[4,128,896]{2,1,0:T(8,128)(2,1)S(1)}) custom-call(s32[12]{0:T(128)S(1)} %concatenate.20.info, bf16[4,128,7168]{2,1,0:T(8,128)(2,1)S(1)} %bitcast.42, bf16[4,128,7168]{2,1,0:T(8,128)(2,1)} %collective-permute-done.6.theirs), custom_call_target="tpu_custom_call" | custom-call | tf_op jit(solution)/shard_map/pallas_call | solution.py:74
  118.0 3.3 %collective-permute-done.10 = bf16[4,128,896]{2,1,0:T(8,128)(2,1)} collective-permute-done((bf16[4,128,896]{2,1,0:T(8,128)(2,1)S(1)}, bf16[4,128,896]{2,1,0:T(8,128)(2,1)}, u32[]{:S(2)}, u32[]{:S(2)}) %collective-permute-start.10) | collective-permute-done | bytes 917536 | tf_op jit(solution)/shard_map/ppermute | solution.py:170
  121.3 1.4 fusion.20
  122.7 5.7 %collective-permute-start.11 = (bf16[128,896]{1,0:T(8,128)(2,1)S(1)}, bf16[128,896]{1,0:T(8,128)(2,1)S(1)}, u32[]{:S(2)}, u32[]{:S(2)}) collective-permute-start(bf16[128,896]{1,0:T(8,128)(2,1)S(1)} %get-tuple-element.49), channel_id=1, source_target_pairs={{0,32},{1,33},{2,34},{3,35},{32,0},{33,1},{34,2},{35,3},{4,36},{5,... | collective-permute-start | bytes 688136 | tf_op jit(solution)/shard_map/ppermute | solution.py:178
  128.6 12.5 %collective-permute-start.13 = (bf16[128,896]{1,0:T(8,128)(2,1)S(1)}, bf16[128,896]{1,0:T(8,128)(2,1)S(1)}, u32[]{:S(2)}, u32[]{:S(2)}) collective-permute-start(bf16[128,896]{1,0:T(8,128)(2,1)S(1)} %get-tuple-element.47), channel_id=1, source_target_pairs={{0,34},{1,35},{2,32},{3,33},{32,2},{33,3},{34,0},{35,1},{4,38},{5,... | collective-permute-start | bytes 688136 | tf_op jit(solution)/shard_map/ppermute | solution.py:178
  141.1 9.2 %collective-permute-start.14 = (bf16[128,896]{1,0:T(8,128)(2,1)S(1)}, bf16[128,896]{1,0:T(8,128)(2,1)S(1)}, u32[]{:S(2)}, u32[]{:S(2)}) collective-permute-start(bf16[128,896]{1,0:T(8,128)(2,1)S(1)} %get-tuple-element.46), channel_id=1, source_target_pairs={{0,35},{1,32},{2,33},{3,34},{32,3},{33,0},{34,1},{35,2},{4,39},{5,... | collective-permute-start | bytes 688136 | tf_op jit(solution)/shard_map/ppermute | solution.py:178
  150.2 1.4 fusion.16
  152.9 14.6 %collective-permute-start.17 = (bf16[128,896]{1,0:T(8,128)(2,1)S(1)}, bf16[128,896]{1,0:T(8,128)(2,1)S(1)}, u32[]{:S(2)}, u32[]{:S(2)}) collective-permute-start(bf16[128,896]{1,0:T(8,128)(2,1)S(1)} %get-tuple-element.32), channel_id=1, source_target_pairs={{0,3},{1,0},{2,1},{3,2},{4,7},{5,4},{6,5},{7,6},{8,11},{9,8},{10,9... | collective-permute-start | bytes 688136 | tf_op jit(solution)/shard_map/ppermute | solution.py:22
  167.5 6.1 %collective-permute-start.20 = (bf16[128,896]{1,0:T(8,128)(2,1)S(1)}, bf16[128,896]{1,0:T(8,128)(2,1)S(1)}, u32[]{:S(2)}, u32[]{:S(2)}) collective-permute-start(bf16[128,896]{1,0:T(8,128)(2,1)S(1)} %get-tuple-element.52), channel_id=1, source_target_pairs={{0,33},{1,34},{2,35},{3,32},{32,1},{33,2},{34,3},{35,0},{4,37},{5,... | collective-permute-start | bytes 688136 | tf_op jit(solution)/shard_map/ppermute | solution.py:178
  173.6 1.7 shard_map.88
  175.4 1.6 convolution_convert_fusion.4
  177.0 1.7 collective-permute-start.21
  180.0 1.6 convolution_convert_fusion.1
  181.7 4.8 %collective-permute-done.17.refs_3_ = bf16[128,896]{1,0:T(8,128)(2,1)S(1)} collective-permute-done((bf16[128,896]{1,0:T(8,128)(2,1)S(1)}, bf16[128,896]{1,0:T(8,128)(2,1)S(1)}, u32[]{:S(2)}, u32[]{:S(2)}) %collective-permute-start.17) | collective-permute-done | bytes 229408 | tf_op jit(solution)/shard_map/ppermute | solution.py:22
  186.5 2.4 collective-permute-start.26
  188.9 4.0 %collective-permute-done.19.refs_4_ = bf16[128,896]{1,0:T(8,128)(2,1)S(1)} collective-permute-done((bf16[128,896]{1,0:T(8,128)(2,1)S(1)}, bf16[128,896]{1,0:T(8,128)(2,1)S(1)}, u32[]{:S(2)}, u32[]{:S(2)}) %collective-permute-start.19) | collective-permute-done | bytes 229408 | tf_op jit(solution)/shard_map/ppermute | solution.py:178
  192.9 8.4 %collective-permute-done.20.refs_5_ = bf16[128,896]{1,0:T(8,128)(2,1)S(1)} collective-permute-done((bf16[128,896]{1,0:T(8,128)(2,1)S(1)}, bf16[128,896]{1,0:T(8,128)(2,1)S(1)}, u32[]{:S(2)}, u32[]{:S(2)}) %collective-permute-start.20) | collective-permute-done | bytes 229408 | tf_op jit(solution)/shard_map/ppermute | solution.py:178
  201.3 4.9 %collective-permute-done.21.refs_6_ = bf16[128,896]{1,0:T(8,128)(2,1)S(1)} collective-permute-done((bf16[128,896]{1,0:T(8,128)(2,1)S(1)}, bf16[128,896]{1,0:T(8,128)(2,1)S(1)}, u32[]{:S(2)}, u32[]{:S(2)}) %collective-permute-start.21) | collective-permute-done | bytes 229408 | tf_op jit(solution)/shard_map/ppermute | solution.py:178
  206.2 4.9 %collective-permute-done.22.refs_7_ = bf16[128,896]{1,0:T(8,128)(2,1)S(1)} collective-permute-done((bf16[128,896]{1,0:T(8,128)(2,1)S(1)}, bf16[128,896]{1,0:T(8,128)(2,1)S(1)}, u32[]{:S(2)}, u32[]{:S(2)}) %collective-permute-start.22) | collective-permute-done | bytes 229408 | tf_op jit(solution)/shard_map/ppermute | solution.py:178
  211.2 1.7 shard_map.89
  214.9 7.8 %all-to-all-start = ((f32[16,1,2]{2,1,0:T(1,128)}), f32[16,1,2]{2,1,0:T(1,128)S(1)}, u32[]{:S(2)}, u32[]{:S(2)}) async-start(f32[16,1,2]{2,1,0:T(1,128)} %broadcast_in_dim.60), calls=%async_computation | async-start | bytes 16384 | tf_op jit(solution)/shard_map/all_to_all | solution.py:211
  222.7 2.9 collective-permute-start.28
  225.5 3.0 convolution_convert_fusion.3
  230.6 2.5 add_convert_fusion.1
  233.4 9.9 %collective-permute-done.28 = bf16[1024,448]{0,1:T(8,128)(2,1)} collective-permute-done((bf16[1024,448]{0,1:T(8,128)(2,1)}, bf16[1024,448]{0,1:T(8,128)(2,1)}, u32[]{:S(2)}, u32[]{:S(2)}) %collective-permute-start.28) | collective-permute-done | bytes 917536 | tf_op jit(solution)/shard_map/ppermute | solution.py:22
  243.2 1.9 add_convert_fusion
  245.3 3.5 %collective-permute-start.29 = (bf16[2048,448]{0,1:T(8,128)(2,1)S(1)}, bf16[2048,448]{0,1:T(8,128)(2,1)S(1)}, u32[]{:S(2)}, u32[]{:S(2)}) collective-permute-start(bf16[2048,448]{0,1:T(8,128)(2,1)S(1)} %pad_maximum_fusion.4), channel_id=1, source_target_pairs={{0,12},{4,0},{8,4},{12,8},{1,13},{5,1},{9,5},{13,9},{2,14},{6,2},{... | collective-permute-start | bytes 5505032 | tf_op jit(solution)/shard_map/ppermute | solution.py:22
  248.8 4.2 %convolution_convert_fusion = bf16[512,2048]{1,0:T(8,128)(2,1)S(1)} fusion(bf16[512,1792]{1,0:T(8,128)(2,1)S(1)} %copy-done.5, bf16[2048,1792]{0,1:T(8,128)(2,1)S(1)} %bitcast.44), kind=kOutput, calls=%fused_computation.2 | convolution fusion | flops 3759144960 | bytes 11272192 | tf_op jit(solution)/shard_map/dot_general | solution.py:124
  253.1 3.0 collective-permute-start.23
  256.7 2.5 fusion.8
  261.8 2.2 collective-permute-done.23
  264.0 33.7 %collective-permute-done.24 = bf16[128,2048]{1,0:T(8,128)(2,1)S(1)} collective-permute-done((bf16[128,2048]{1,0:T(8,128)(2,1)S(1)}, bf16[128,2048]{1,0:T(8,128)(2,1)S(1)}, u32[]{:S(2)}, u32[]{:S(2)}) %collective-permute-start.24) | collective-permute-done | bytes 524320 | tf_op jit(solution)/shard_map/ppermute | solution.py:22
  298.9 2.3 fusion
  (81 shorter events, 18.4 us)
Async XLA Ops:
  0.6 92.1 %collective-permute-start.6 = (bf16[4,128,7168]{2,1,0:T(8,128)(2,1)}, bf16[4,128,7168]{2,1,0:T(8,128)(2,1)}, u32[]{:S(2)}, u32[]{:S(2)}) collective-permute-start(bf16[4,128,7168]{2,1,0:T(8,128)(2,1)} %mine.5), channel_id=1, source_target_pairs={{0,16},{16,0},{1,17},{17,1},{2,18},{18,2},{3,19},{19,3},{4,20},{20... | collective-permute-start | bytes 22020104 | tf_op jit(solution)/shard_map/ppermute | solution.py:27
  5.7 15.5 %collective-permute-start = (bf16[128,2048]{1,0:T(8,128)(2,1)S(1)}, bf16[128,2048]{1,0:T(8,128)(2,1)S(1)}, u32[]{:S(2)}, u32[]{:S(2)}) collective-permute-start(bf16[128,2048]{1,0:T(8,128)(2,1)S(1)} %bitcast_select_fusion), channel_id=1, source_target_pairs={{0,1},{1,2},{2,3},{3,0},{4,5},{5,6},{6,7},{7,4},{8,9},{9,10},{10,1... | collective-permute-start | bytes 1572872 | tf_op jit(solution)/shard_map/ppermute | solution.py:22
  5.8 54.6 %collective-permute-start.3 = (bf16[2048,448]{0,1:T(8,128)(2,1)}, bf16[2048,448]{0,1:T(8,128)(2,1)}, u32[]{:S(2)}, u32[]{:S(2)}) collective-permute-start(bf16[2048,448]{0,1:T(8,128)(2,1)} %bitcast.45), channel_id=1, source_target_pairs={{0,8},{4,12},{8,0},{12,4},{1,9},{5,13},{9,1},{13,5},{2,10},{6,14},... | collective-permute-start | bytes 5505032 | tf_op jit(solution)/shard_map/ppermute | solution.py:22
  8.5 79.8 %collective-permute-start.4 = (bf16[2048,448]{0,1:T(8,128)(2,1)}, bf16[2048,448]{0,1:T(8,128)(2,1)}, u32[]{:S(2)}, u32[]{:S(2)}) collective-permute-start(bf16[2048,448]{0,1:T(8,128)(2,1)} %bitcast.46), channel_id=1, source_target_pairs={{0,12},{4,0},{8,4},{12,8},{1,13},{5,1},{9,5},{13,9},{2,14},{6,2},{... | collective-permute-start | bytes 5505032 | tf_op jit(solution)/shard_map/ppermute | solution.py:22
  9.3 79.6 %collective-permute-start.5 = (bf16[2048,448]{0,1:T(8,128)(2,1)}, bf16[2048,448]{0,1:T(8,128)(2,1)}, u32[]{:S(2)}, u32[]{:S(2)}) collective-permute-start(bf16[2048,448]{0,1:T(8,128)(2,1)} %bitcast.47), channel_id=1, source_target_pairs={{0,4},{4,8},{8,12},{12,0},{1,5},{5,9},{9,13},{13,1},{2,6},{6,10},{... | collective-permute-start | bytes 5505032 | tf_op jit(solution)/shard_map/ppermute | solution.py:22
  21.2 78.9 %copy-start.7 = (bf16[128,2048]{1,0:T(8,128)(2,1)}, bf16[128,2048]{1,0:T(8,128)(2,1)S(1)}, u32[]{:S(2)}) copy-start(bf16[128,2048]{1,0:T(8,128)(2,1)S(1)} %collective-permute-done) | copy-start | bytes 1572868
  21.2 24.6 %collective-permute-start.1 = (bf16[128,2048]{1,0:T(8,128)(2,1)S(1)}, bf16[128,2048]{1,0:T(8,128)(2,1)}, u32[]{:S(2)}, u32[]{:S(2)}) collective-permute-start(bf16[128,2048]{1,0:T(8,128)(2,1)S(1)} %bitcast_select_fusion), channel_id=1, source_target_pairs={{0,2},{1,3},{2,0},{3,1},{4,6},{5,7},{6,4},{7,5},{8,10},{9,11},{10,... | collective-permute-start | bytes 1572872 | tf_op jit(solution)/shard_map/ppermute | solution.py:22
  45.8 13.1 %collective-permute-start.2 = (bf16[128,2048]{1,0:T(8,128)(2,1)S(1)}, bf16[128,2048]{1,0:T(8,128)(2,1)}, u32[]{:S(2)}, u32[]{:S(2)}) collective-permute-start(bf16[128,2048]{1,0:T(8,128)(2,1)S(1)} %bitcast_select_fusion), channel_id=1, source_target_pairs={{0,3},{1,0},{2,1},{3,2},{4,7},{5,4},{6,5},{7,6},{8,11},{9,8},{10,9... | collective-permute-start | bytes 1572872 | tf_op jit(solution)/shard_map/ppermute | solution.py:22
  50.2 38.8 %copy-start.4 = (bf16[1,2048,448]{1,2,0:T(8,128)(2,1)S(1)}, bf16[1,2048,448]{1,2,0:T(8,128)(2,1)}, u32[]{:S(2)}) copy-start(bf16[1,2048,448]{1,2,0:T(8,128)(2,1)} %param.8) | copy-start | bytes 5505028
  58.8 33.9 %slice-start = ((s8[7340032]{0:T(1024)(128)(4,1)}), s8[4194304]{0:T(1024)(128)(4,1)S(1)}, s32[]{:S(2)}) async-start(s8[7340032]{0:T(1024)(128)(4,1)} %bitcast.41), calls=%async_computation.1 | async-start | bytes 8388608
  60.4 119.7 %copy-start.1 = (bf16[512,2048]{1,0:T(8,128)(2,1)}, bf16[512,2048]{1,0:T(8,128)(2,1)S(1)}, u32[]{:S(2)}) copy-start(bf16[512,2048]{1,0:T(8,128)(2,1)S(1)} %pad_maximum_fusion.1) | copy-start | bytes 6291460
  60.4 32.3 %slice-start.1 = ((s8[7340032]{0:T(1024)(128)(4,1)}), s8[3145728]{0:T(1024)(128)(4,1)S(1)}, s32[]{:S(2)}) async-start(s8[7340032]{0:T(1024)(128)(4,1)} %bitcast.41), calls=%async_computation.2 | async-start | bytes 6291456
  92.7 7.4 %copy-start = (bf16[2048,1792]{0,1:T(8,128)(2,1)}, bf16[2048,1792]{0,1:T(8,128)(2,1)S(1)}, u32[]{:S(2)}) copy-start(bf16[2048,1792]{0,1:T(8,128)(2,1)S(1)} %pad_maximum_fusion) | copy-start | bytes 22020100
  97.5 23.9 %collective-permute-start.10 = (bf16[4,128,896]{2,1,0:T(8,128)(2,1)S(1)}, bf16[4,128,896]{2,1,0:T(8,128)(2,1)}, u32[]{:S(2)}, u32[]{:S(2)}) collective-permute-start(bf16[4,128,896]{2,1,0:T(8,128)(2,1)S(1)} %get-tuple-element.27), channel_id=1, source_target_pairs={{64,0},{128,64},{192,128},{32,96},{96,160},{160,224},{65,1},{129,6... | collective-permute-start | bytes 2752520 | tf_op jit(solution)/shard_map/ppermute | solution.py:170
  98.8 42.3 %collective-permute-start.18 = (bf16[4,128,896]{2,1,0:T(8,128)(2,1)S(1)}, bf16[4,128,896]{2,1,0:T(8,128)(2,1)}, u32[]{:S(2)}, u32[]{:S(2)}) collective-permute-start(bf16[4,128,896]{2,1,0:T(8,128)(2,1)S(1)} %get-tuple-element.34), channel_id=1, source_target_pairs={{64,0},{128,64},{192,128},{32,96},{96,160},{160,224},{65,1},{129,6... | collective-permute-start | bytes 2752520 | tf_op jit(solution)/shard_map/ppermute | solution.py:170
  109.3 19.2 %collective-permute-start.7 = (bf16[128,896]{1,0:T(8,128)(2,1)S(1)}, bf16[128,896]{1,0:T(8,128)(2,1)S(1)}, u32[]{:S(2)}, u32[]{:S(2)}) collective-permute-start(bf16[128,896]{1,0:T(8,128)(2,1)S(1)} %get-tuple-element.23), channel_id=1, source_target_pairs={{0,1},{1,2},{2,3},{3,0},{4,5},{5,6},{6,7},{7,4},{8,9},{9,10},{10,1... | collective-permute-start | bytes 688136 | tf_op jit(solution)/shard_map/ppermute | solution.py:22
  110.8 17.8 %collective-permute-start.8 = (bf16[128,896]{1,0:T(8,128)(2,1)S(1)}, bf16[128,896]{1,0:T(8,128)(2,1)S(1)}, u32[]{:S(2)}, u32[]{:S(2)}) collective-permute-start(bf16[128,896]{1,0:T(8,128)(2,1)S(1)} %get-tuple-element.24), channel_id=1, source_target_pairs={{0,2},{1,3},{2,0},{3,1},{4,6},{5,7},{6,4},{7,5},{8,10},{9,11},{10,... | collective-permute-start | bytes 688136 | tf_op jit(solution)/shard_map/ppermute | solution.py:22
  112.8 38.8 %collective-permute-start.9 = (bf16[128,896]{1,0:T(8,128)(2,1)S(1)}, bf16[128,896]{1,0:T(8,128)(2,1)S(1)}, u32[]{:S(2)}, u32[]{:S(2)}) collective-permute-start(bf16[128,896]{1,0:T(8,128)(2,1)S(1)} %get-tuple-element.25), channel_id=1, source_target_pairs={{0,3},{1,0},{2,1},{3,2},{4,7},{5,4},{6,5},{7,6},{8,11},{9,8},{10,9... | collective-permute-start | bytes 688136 | tf_op jit(solution)/shard_map/ppermute | solution.py:22
  122.7 30.2 %collective-permute-start.11 = (bf16[128,896]{1,0:T(8,128)(2,1)S(1)}, bf16[128,896]{1,0:T(8,128)(2,1)S(1)}, u32[]{:S(2)}, u32[]{:S(2)}) collective-permute-start(bf16[128,896]{1,0:T(8,128)(2,1)S(1)} %get-tuple-element.49), channel_id=1, source_target_pairs={{0,32},{1,33},{2,34},{3,35},{32,0},{33,1},{34,2},{35,3},{4,36},{5,... | collective-permute-start | bytes 688136 | tf_op jit(solution)/shard_map/ppermute | solution.py:178
  128.4 24.4 %collective-permute-start.12 = (bf16[128,896]{1,0:T(8,128)(2,1)S(1)}, bf16[128,896]{1,0:T(8,128)(2,1)S(1)}, u32[]{:S(2)}, u32[]{:S(2)}) collective-permute-start(bf16[128,896]{1,0:T(8,128)(2,1)S(1)} %get-tuple-element.48), channel_id=1, source_target_pairs={{0,33},{1,34},{2,35},{3,32},{32,1},{33,2},{34,3},{35,0},{4,37},{5,... | collective-permute-start | bytes 688136 | tf_op jit(solution)/shard_map/ppermute | solution.py:178
  128.6 38.9 %collective-permute-start.13 = (bf16[128,896]{1,0:T(8,128)(2,1)S(1)}, bf16[128,896]{1,0:T(8,128)(2,1)S(1)}, u32[]{:S(2)}, u32[]{:S(2)}) collective-permute-start(bf16[128,896]{1,0:T(8,128)(2,1)S(1)} %get-tuple-element.47), channel_id=1, source_target_pairs={{0,34},{1,35},{2,32},{3,33},{32,2},{33,3},{34,0},{35,1},{4,38},{5,... | collective-permute-start | bytes 688136 | tf_op jit(solution)/shard_map/ppermute | solution.py:178
  141.1 26.5 %collective-permute-start.14 = (bf16[128,896]{1,0:T(8,128)(2,1)S(1)}, bf16[128,896]{1,0:T(8,128)(2,1)S(1)}, u32[]{:S(2)}, u32[]{:S(2)}) collective-permute-start(bf16[128,896]{1,0:T(8,128)(2,1)S(1)} %get-tuple-element.46), channel_id=1, source_target_pairs={{0,35},{1,32},{2,33},{3,34},{32,3},{33,0},{34,1},{35,2},{4,39},{5,... | collective-permute-start | bytes 688136 | tf_op jit(solution)/shard_map/ppermute | solution.py:178
  151.6 25.4 %collective-permute-start.15 = (bf16[128,896]{1,0:T(8,128)(2,1)S(1)}, bf16[128,896]{1,0:T(8,128)(2,1)S(1)}, u32[]{:S(2)}, u32[]{:S(2)}) collective-permute-start(bf16[128,896]{1,0:T(8,128)(2,1)S(1)} %get-tuple-element.30), channel_id=1, source_target_pairs={{0,1},{1,2},{2,3},{3,0},{4,5},{5,6},{6,7},{7,4},{8,9},{9,10},{10,1... | collective-permute-start | bytes 688136 | tf_op jit(solution)/shard_map/ppermute | solution.py:22
  152.9 27.2 %collective-permute-start.16 = (bf16[128,896]{1,0:T(8,128)(2,1)S(1)}, bf16[128,896]{1,0:T(8,128)(2,1)S(1)}, u32[]{:S(2)}, u32[]{:S(2)}) collective-permute-start(bf16[128,896]{1,0:T(8,128)(2,1)S(1)} %get-tuple-element.31), channel_id=1, source_target_pairs={{0,2},{1,3},{2,0},{3,1},{4,6},{5,7},{6,4},{7,5},{8,10},{9,11},{10,... | collective-permute-start | bytes 688136 | tf_op jit(solution)/shard_map/ppermute | solution.py:22
  152.9 33.6 %collective-permute-start.17 = (bf16[128,896]{1,0:T(8,128)(2,1)S(1)}, bf16[128,896]{1,0:T(8,128)(2,1)S(1)}, u32[]{:S(2)}, u32[]{:S(2)}) collective-permute-start(bf16[128,896]{1,0:T(8,128)(2,1)S(1)} %get-tuple-element.32), channel_id=1, source_target_pairs={{0,3},{1,0},{2,1},{3,2},{4,7},{5,4},{6,5},{7,6},{8,11},{9,8},{10,9... | collective-permute-start | bytes 688136 | tf_op jit(solution)/shard_map/ppermute | solution.py:22
  167.5 25.4 %collective-permute-start.19 = (bf16[128,896]{1,0:T(8,128)(2,1)S(1)}, bf16[128,896]{1,0:T(8,128)(2,1)S(1)}, u32[]{:S(2)}, u32[]{:S(2)}) collective-permute-start(bf16[128,896]{1,0:T(8,128)(2,1)S(1)} %get-tuple-element.53), channel_id=1, source_target_pairs={{0,32},{1,33},{2,34},{3,35},{32,0},{33,1},{34,2},{35,3},{4,36},{5,... | collective-permute-start | bytes 688136 | tf_op jit(solution)/shard_map/ppermute | solution.py:178
  167.5 33.8 %collective-permute-start.20 = (bf16[128,896]{1,0:T(8,128)(2,1)S(1)}, bf16[128,896]{1,0:T(8,128)(2,1)S(1)}, u32[]{:S(2)}, u32[]{:S(2)}) collective-permute-start(bf16[128,896]{1,0:T(8,128)(2,1)S(1)} %get-tuple-element.52), channel_id=1, source_target_pairs={{0,33},{1,34},{2,35},{3,32},{32,1},{33,2},{34,3},{35,0},{4,37},{5,... | collective-permute-start | bytes 688136 | tf_op jit(solution)/shard_map/ppermute | solution.py:178
  177.0 29.2 %collective-permute-start.21 = (bf16[128,896]{1,0:T(8,128)(2,1)S(1)}, bf16[128,896]{1,0:T(8,128)(2,1)S(1)}, u32[]{:S(2)}, u32[]{:S(2)}) collective-permute-start(bf16[128,896]{1,0:T(8,128)(2,1)S(1)} %get-tuple-element.51), channel_id=1, source_target_pairs={{0,34},{1,35},{2,32},{3,33},{32,2},{33,3},{34,0},{35,1},{4,38},{5,... | collective-permute-start | bytes 688136 | tf_op jit(solution)/shard_map/ppermute | solution.py:178
  180.0 31.1 %collective-permute-start.22 = (bf16[128,896]{1,0:T(8,128)(2,1)S(1)}, bf16[128,896]{1,0:T(8,128)(2,1)S(1)}, u32[]{:S(2)}, u32[]{:S(2)}) collective-permute-start(bf16[128,896]{1,0:T(8,128)(2,1)S(1)} %get-tuple-element.50), channel_id=1, source_target_pairs={{0,35},{1,32},{2,33},{3,34},{32,3},{33,0},{34,1},{35,2},{4,39},{5,... | collective-permute-start | bytes 688136 | tf_op jit(solution)/shard_map/ppermute | solution.py:178
  186.5 44.1 %collective-permute-start.26 = (bf16[1024,448]{0,1:T(8,128)(2,1)}, bf16[1024,448]{0,1:T(8,128)(2,1)}, u32[]{:S(2)}, u32[]{:S(2)}) collective-permute-start(bf16[1024,448]{0,1:T(8,128)(2,1)} %convolution_convert_fusion.4), channel_id=1, source_target_pairs={{0,4},{4,8},{8,12},{12,0},{1,5},{5,9},{9,13},{13,1},{2,6},{6,10},{... | collective-permute-start | bytes 2752520 | tf_op jit(solution)/shard_map/ppermute | solution.py:22
  214.9 15.7 %all-to-all-start = ((f32[16,1,2]{2,1,0:T(1,128)}), f32[16,1,2]{2,1,0:T(1,128)S(1)}, u32[]{:S(2)}, u32[]{:S(2)}) async-start(f32[16,1,2]{2,1,0:T(1,128)} %broadcast_in_dim.60), calls=%async_computation | async-start | bytes 16384 | tf_op jit(solution)/shard_map/all_to_all | solution.py:211
  222.7 5.9 %copy-start.2 = (bf16[512,2048]{1,0:T(8,128)(2,1)S(1)}, bf16[512,2048]{1,0:T(8,128)(2,1)}, u32[]{:S(2)}) copy-start(bf16[512,2048]{1,0:T(8,128)(2,1)} %copy-done.1) | copy-start | bytes 6291460
  222.7 20.6 %collective-permute-start.28 = (bf16[1024,448]{0,1:T(8,128)(2,1)}, bf16[1024,448]{0,1:T(8,128)(2,1)}, u32[]{:S(2)}, u32[]{:S(2)}) collective-permute-start(bf16[1024,448]{0,1:T(8,128)(2,1)} %convolution_convert_fusion.1), channel_id=1, source_target_pairs={{0,12},{4,0},{8,4},{12,8},{1,13},{5,1},{9,5},{13,9},{2,14},{6,2},{... | collective-permute-start | bytes 2752520 | tf_op jit(solution)/shard_map/ppermute | solution.py:22
  230.6 2.5 copy-start.6
  230.6 18.2 %slice-start.2 = ((s8[7340032]{0:T(1024)(128)(4,1)}), s8[4194304]{0:T(1024)(128)(4,1)S(1)}, s32[]{:S(2)}) async-start(s8[7340032]{0:T(1024)(128)(4,1)} %bitcast.43), calls=%async_computation.3 | async-start | bytes 8388608
  233.1 10.1 %copy-start.3 = (bf16[512,2048]{1,0:T(8,128)(2,1)S(1)}, bf16[512,2048]{1,0:T(8,128)(2,1)}, u32[]{:S(2)}) copy-start(bf16[512,2048]{1,0:T(8,128)(2,1)} %copy-done.1) | copy-start | bytes 6291460
  233.3 15.5 %slice-start.3 = ((s8[7340032]{0:T(1024)(128)(4,1)}), s8[3145728]{0:T(1024)(128)(4,1)S(1)}, s32[]{:S(2)}) async-start(s8[7340032]{0:T(1024)(128)(4,1)} %bitcast.43), calls=%async_computation.4 | async-start | bytes 6291456
  233.3 65.6 %collective-permute-start.27 = (bf16[2048,448]{0,1:T(8,128)(2,1)S(1)}, bf16[2048,448]{0,1:T(8,128)(2,1)S(1)}, u32[]{:S(2)}, u32[]{:S(2)}) collective-permute-start(bf16[2048,448]{0,1:T(8,128)(2,1)S(1)} %pad_maximum_fusion.3), channel_id=1, source_target_pairs={{0,4},{4,8},{8,12},{12,0},{1,5},{5,9},{9,13},{13,1},{2,6},{6,10},{... | collective-permute-start | bytes 5505032 | tf_op jit(solution)/shard_map/ppermute | solution.py:22
  245.1 3.7 %copy-start.5 = (bf16[512,1792]{1,0:T(8,128)(2,1)S(1)}, bf16[512,1792]{1,0:T(8,128)(2,1)}, u32[]{:S(2)}) copy-start(bf16[512,1792]{1,0:T(8,128)(2,1)} %pad_maximum_fusion.2) | copy-start | bytes 5505028
  245.3 53.6 %collective-permute-start.29 = (bf16[2048,448]{0,1:T(8,128)(2,1)S(1)}, bf16[2048,448]{0,1:T(8,128)(2,1)S(1)}, u32[]{:S(2)}, u32[]{:S(2)}) collective-permute-start(bf16[2048,448]{0,1:T(8,128)(2,1)S(1)} %pad_maximum_fusion.4), channel_id=1, source_target_pairs={{0,12},{4,0},{8,4},{12,8},{1,13},{5,1},{9,5},{13,9},{2,14},{6,2},{... | collective-permute-start | bytes 5505032 | tf_op jit(solution)/shard_map/ppermute | solution.py:22
  253.0 3.7 %copy-start.8 = (bf16[128,2048]{1,0:T(8,128)(2,1)S(1)}, bf16[128,2048]{1,0:T(8,128)(2,1)}, u32[]{:S(2)}) copy-start(bf16[128,2048]{1,0:T(8,128)(2,1)} %copy-done.7) | copy-start | bytes 1572868
  253.1 10.9 %collective-permute-start.23 = (bf16[128,2048]{1,0:T(8,128)(2,1)S(1)}, bf16[128,2048]{1,0:T(8,128)(2,1)S(1)}, u32[]{:S(2)}, u32[]{:S(2)}) collective-permute-start(bf16[128,2048]{1,0:T(8,128)(2,1)S(1)} %get-tuple-element.43), channel_id=1, source_target_pairs={{0,3},{1,0},{2,1},{3,2},{4,7},{5,4},{6,5},{7,6},{8,11},{9,8},{10,9... | collective-permute-start | bytes 1572872 | tf_op jit(solution)/shard_map/ppermute | solution.py:22
  256.1 41.6 %collective-permute-start.24 = (bf16[128,2048]{1,0:T(8,128)(2,1)S(1)}, bf16[128,2048]{1,0:T(8,128)(2,1)S(1)}, u32[]{:S(2)}, u32[]{:S(2)}) collective-permute-start(bf16[128,2048]{1,0:T(8,128)(2,1)S(1)} %get-tuple-element.45), channel_id=1, source_target_pairs={{0,2},{1,3},{2,0},{3,1},{4,6},{5,7},{6,4},{7,5},{8,10},{9,11},{10,... | collective-permute-start | bytes 1572872 | tf_op jit(solution)/shard_map/ppermute | solution.py:22
  256.1 41.6 %collective-permute-start.25 = (bf16[128,2048]{1,0:T(8,128)(2,1)S(1)}, bf16[128,2048]{1,0:T(8,128)(2,1)S(1)}, u32[]{:S(2)}, u32[]{:S(2)}) collective-permute-start(bf16[128,2048]{1,0:T(8,128)(2,1)S(1)} %get-tuple-element.44), channel_id=1, source_target_pairs={{0,1},{1,2},{2,3},{3,0},{4,5},{5,6},{6,7},{7,4},{8,9},{9,10},{10,1... | collective-permute-start | bytes 1572872 | tf_op jit(solution)/shard_map/ppermute | solution.py:22

commit v4 on v3

--- a/solution.py
+++ b/solution.py
@@ -81,7 +81,7 @@
             out_specs=[written(dims) for dims in lead],
             scratch_shapes=[pltpu.VMEM((2, 4, rows, wide), jnp.bfloat16)],
         ),
-        compiler_params=pltpu.CompilerParams(dimension_semantics=("arbitrary",), vmem_limit_bytes=12 << 20),
+        compiler_params=pltpu.CompilerParams(dimension_semantics=("arbitrary",), vmem_limit_bytes=58 << 20),
     )(info, mine, theirs)
 
 
@@ -132,7 +132,6 @@
     here = 2 * chip + core
     weights = projector[0]
     tokens = student_states.shape[1]
-    half = weights.shape[0] // 2
     width = weights.shape[1]
 
     theirs = exchange(teacher_states, "core", 1)
@@ -188,54 +187,47 @@
     crossed_second = send_across(1)
     own_second = send_own(1)
 
-    rows = jnp.concatenate(students, axis=0)
+    rows = lax.optimization_barrier(jnp.concatenate(students, axis=0))
     w_all = lax.optimization_barrier(jnp.concatenate([w_opp, w_next, w_prev, weights], axis=1))
     projected = lax.optimization_barrier(dot(rows, w_all, 1, 0))
     near = near[2:]
-    top, bot = rows[:, :half], rows[:, half:]
-
-    def grad(part, residual):
-        return dot(part, residual, 0, 0)
+
+    def grad(residual):
+        return dot(rows, residual, 0, 0)
 
     first_res, squares_first = residual_of(near, projected, own_first, 0, crossed_first)
-    opp_res, next_res = first_res[:, :width], first_res[:, width:]
-    opp_top = grad(top, opp_res).astype(jnp.bfloat16)
-    opp_bot = grad(bot, opp_res).astype(jnp.bfloat16)
-    next_bot = grad(bot, next_res).astype(jnp.bfloat16)
-    up_top = rotate(opp_top, "x", 1)
-    down_bot = rotate(opp_bot, "x", -1)
+    opp_part = grad(first_res[:, :width])
+    from_opp = rotate(opp_part.astype(jnp.bfloat16), "x", 2)
+    next_part = lax.optimization_barrier(grad(first_res[:, width:]).astype(jnp.bfloat16))
+    part_first = lax.optimization_barrier(dot(first_res, w_all[:, : 2 * width], 1, 1))
     second_res, squares_second = residual_of(near, projected, own_second, 1, crossed_second)
+    student_part = (part_first + dot(second_res, w_all[:, 2 * width :], 1, 1)).astype(jnp.bfloat16)
+    parts = [student_part[k * tokens : (k + 1) * tokens] for k in range(4)]
+    prev_part = grad(second_res[:, :width]).astype(jnp.bfloat16)
 
     sums = jnp.stack([squares_first[0] + squares_second[0], valid_counts[0].astype(jnp.float32)])
+    sums, parts, prev_part = lax.optimization_barrier((sums, parts, prev_part))
     copies = jnp.broadcast_to(sums, (lax.axis_size(DP), 2))
     sums = jnp.sum(lax.all_to_all(copies, DP, split_axis=0, concat_axis=0, tiled=True), axis=0)
+    sums, parts, prev_part, next_part = lax.optimization_barrier((sums, parts, prev_part, next_part))
     total = sums[1]
     loss = sums[:1] / (total * (width * lax.axis_size(DP)))
     factor = loss_scale / total
 
-    next_top = (grad(top, next_res) + up_top.astype(jnp.float32)).astype(jnp.bfloat16)
-    next_part = lax.optimization_barrier((jnp.concatenate([next_top, next_bot], axis=0), sums))[0]
-    from_prev = rotate(next_part, "x", 1)
-    prev_res, own_res = second_res[:, :width], second_res[:, width:]
-    prev_top = grad(top, prev_res).astype(jnp.bfloat16)
-    prev_bot = (grad(bot, prev_res) + down_bot.astype(jnp.float32)).astype(jnp.bfloat16)
-    prev_part = lax.optimization_barrier((jnp.concatenate([prev_top, prev_bot], axis=0), sums))[0]
-    from_next = rotate(prev_part, "x", -1)
-
-    residual = lax.optimization_barrier(jnp.concatenate([first_res, second_res], axis=1))
-    student_part = dot(residual, w_all, 1, 1).astype(jnp.bfloat16)
-    student_part = lax.optimization_barrier((student_part, sums))[0]
     returned = []
     for k in (1, 2, 3):
-        part = student_part[k * tokens : (k + 1) * tokens]
-        returned.append(rotate(part, "zl", -k))
-    own_part = lax.optimization_barrier(grad(rows, own_res))
-
-    student_grad = student_part[:tokens].astype(jnp.float32)
+        returned.append(rotate(parts[k], "zl", -k))
+    from_next = rotate(prev_part, "x", -1)
+    from_prev = rotate(next_part, "x", 1)
+    own_part = lax.optimization_barrier(grad(second_res[:, width:]))
+
+    student_grad = parts[0].astype(jnp.float32)
     for part in returned:
         student_grad = student_grad + part.astype(jnp.float32)
     student_grad = (student_grad * factor).astype(jnp.bfloat16)
-    projector_grad = own_part + from_prev.astype(jnp.float32) + from_next.astype(jnp.float32)
+    projector_grad = own_part
+    for part in (from_prev, from_next, from_opp):
+        projector_grad = projector_grad + part.astype(jnp.float32)
     projector_grad = (projector_grad * factor).astype(jnp.bfloat16)
     return (student_grad[None], projector_grad[None], loss)
 

time: 305 us -> 330 us (1.082)
  waiting for transfers between devices: 148 us -> 164 us
  other arithmetic: 16.9 us -> 21.1 us
  Pallas kernels: 15.6 us -> 19.2 us
    ppermute x19 -> x18, waiting for transfers between devices: 123 us -> 137 us  [rotate(): lax.ppermute(block, axis, [(i, (i + distance) % n) for i in range(n)])]
    ppermute x19 -> x18, starting transfers between devices: 40.1 us -> 32.4 us  [rotate(): lax.ppermute(block, axis, [(i, (i + distance) % n) for i in range(n)])]
    ppermute x8, starting transfers between devices: 35.2 us -> 40.2 us  [send_across(): sent.append(lax.ppermute(slab, ('zh', 'zl'), route))]
    ppermute x8, waiting for transfers between devices: 22.2 us -> 27.2 us  [send_across(): sent.append(lax.ppermute(slab, ('zh', 'zl'), route))]
    pallas_call x3, Pallas kernels: 12.1 us -> 15.7 us  [prepare(): pl.pallas_call(functools.partial(prepare_body, piece), out_shape=[jax.Sha...]
    ppermute x2, waiting for transfers between devices: 3.34 us -> 0.01 us  [compute(): relayed.append(lax.ppermute(beyond_slabs[chunk], ('y', 'zh'), y_route))]
    dot_general x9 -> x7, matrix products: 23.2 us -> 25.8 us  [dot(): lax.dot_general(a, b, (((ca,), (cb,)), ((), ())), preferred_element_type=...]
  transfers between devices with their start and end apart: 31 -> 30, of which waited for: 16 -> 14; matrix products, arithmetic and copies ran while one was open for 13% -> 12% of each run, Pallas kernels for 4% -> 4%
where the time goes in v4:
time: 330 us; the launch traced here: 329 us
  waiting for transfers between devices  164 us (50%)
  starting transfers between devices  87.6 us (27%)
  matrix products  25.8 us (8%)
  other arithmetic  21.1 us (6%)
  Pallas kernels  19.2 us (6%)
  between operations  6.59 us (2%)
  local copies, waits for them, and re-layouts  5.11 us (2%)
    ppermute x18, waiting for transfers between devices, rotate(): lax.ppermute(block, axis, [(i, (i + distance) % n) for i in range(n)])  137 us
    ppermute x8, starting transfers between devices, send_across(): sent.append(lax.ppermute(slab, ('zh', 'zl'), route))  40.2 us
    ppermute x18, starting transfers between devices, rotate(): lax.ppermute(block, axis, [(i, (i + distance) % n) for i in range(n)])  32.4 us
    ppermute x8, waiting for transfers between devices, send_across(): sent.append(lax.ppermute(slab, ('zh', 'zl'), route))  27.2 us
    dot_general x7, matrix products, dot(): lax.dot_general(a, b, (((ca,), (cb,)), ((), ())), preferred_element_type=...  25.8 us
    pallas_call x3, Pallas kernels, prepare(): pl.pallas_call(functools.partial(prepare_body, piece), out_shape=[jax.Sha...  15.7 us
    all_to_all x1, starting transfers between devices, compute(): lax.all_to_all(copies, DP, split_axis=0, concat_axis=0, tiled=True)  9.05 us
  transfers between devices with their start and end apart: 30, of which 14 were waited for; matrix products, arithmetic and copies ran while one was open for 12% of the time, Pallas kernels for 4%

profile of v4, /device:TPU:1, one launch (start us, length us, event | category | flops | bytes accessed | tf_op | source)
XLA Modules:
  0.0 329.1 jit_solution(1100526636921208693)
XLA Ops:
  0.6 3.3 collective-permute-start.6
  5.8 2.7 collective-permute-start.3
  10.0 11.2 %collective-permute-done = bf16[128,2048]{1,0:T(8,128)(2,1)S(1)} collective-permute-done((bf16[128,2048]{1,0:T(8,128)(2,1)S(1)}, bf16[128,2048]{1,0:T(8,128)(2,1)S(1)}, u32[]{:S(2)}, u32[]{:S(2)}) %collective-permute-start) | collective-permute-done | bytes 524320 | tf_op jit(solution)/shard_map/ppermute | solution.py:22
  24.5 22.0 %collective-permute-done.1 = bf16[128,2048]{1,0:T(8,128)(2,1)S(1)} collective-permute-done((bf16[128,2048]{1,0:T(8,128)(2,1)S(1)}, bf16[128,2048]{1,0:T(8,128)(2,1)S(1)}, u32[]{:S(2)}, u32[]{:S(2)}) %collective-permute-start.1) | collective-permute-done | bytes 524320 | tf_op jit(solution)/shard_map/ppermute | solution.py:22
  46.5 2.3 collective-permute-start.2
  51.6 8.2 %collective-permute-done.2 = bf16[128,2048]{1,0:T(8,128)(2,1)} collective-permute-done((bf16[128,2048]{1,0:T(8,128)(2,1)S(1)}, bf16[128,2048]{1,0:T(8,128)(2,1)}, u32[]{:S(2)}, u32[]{:S(2)}) %collective-permute-start.2) | collective-permute-done | bytes 524320 | tf_op jit(solution)/shard_map/ppermute | solution.py:22
  59.7 1.6 pad_maximum_fusion.1
  61.3 26.9 %collective-permute-done.4 = bf16[2048,448]{0,1:T(8,128)(2,1)} collective-permute-done((bf16[2048,448]{0,1:T(8,128)(2,1)}, bf16[2048,448]{0,1:T(8,128)(2,1)}, u32[]{:S(2)}, u32[]{:S(2)}) %collective-permute-start.4) | collective-permute-done | bytes 1835040 | tf_op jit(solution)/shard_map/ppermute | solution.py:22
  89.0 6.0 %pad_maximum_fusion = bf16[2048,1792]{0,1:T(8,128)(2,1)} fusion(bf16[2048,448]{0,1:T(8,128)(2,1)S(1)} %bitcast.51, bf16[2048,448]{0,1:T(8,128)(2,1)} %collective-permute-done.5, bf16[2048,448]{0,1:T(8,128)(2,1)} %collective-permute-done.4, bf16[2048,448]{0,1:T(8,128)(2,1)} %collective-permute-done.3), kind=kLoop, calls=%fused_computation | loop fusion | flops 29360128 | bytes 14680064 | tf_op jit(solution)/shard_map/concatenate | solution.py:191
  95.0 5.3 %shard_map.87 = (bf16[4,128,896]{2,1,0:T(8,128)(2,1)}, bf16[4,128,896]{2,1,0:T(8,128)(2,1)}) custom-call(s32[12]{0:T(128)} %concatenate.11.info, bf16[4,128,7168]{2,1,0:T(8,128)(2,1)} %mine.5, bf16[4,128,7168]{2,1,0:T(8,128)(2,1)} %collective-permute-done.6.theirs), custom_call_target="tpu_custom_call" | custom-call | tf_op jit(solution)/shard_map/pallas_call | solution.py:74
  101.6 1.3 collective-permute-start.10
  102.9 7.1 %fusion.22.projected = f32[512,1792]{1,0:T(8,128)S(1)} fusion(bf16[512,2048]{1,0:T(8,128)(2,1)S(1)} %pad_maximum_fusion.1, bf16[2048,1792]{0,1:T(8,128)(2,1)} %pad_maximum_fusion), kind=kOutput, calls=%fused_computation.51 | convolution fusion | flops 3758096384 | bytes 13107200 | tf_op jit(solution)/shard_map/dot_general | solution.py:124
  109.9 5.2 %shard_map.85 = (bf16[128,896]{1,0:T(8,128)(2,1)}, bf16[128,896]{1,0:T(8,128)(2,1)}, bf16[128,896]{1,0:T(8,128)(2,1)}, bf16[128,896]{1,0:T(8,128)(2,1)}, bf16[12...) custom-call(s32[12]{0:T(128)} %concatenate.11.info, ...), custom_call_target="tpu_custom_call" | custom-call | tf_op jit(solution)/shard_map/pallas_call | solution.py:74
  115.1 1.5 collective-permute-start.15
  116.7 2.0 collective-permute-start.16
  118.7 1.7 collective-permute-start.17
  120.4 5.3 %shard_map.86 = (bf16[4,128,896]{2,1,0:T(8,128)(2,1)}, bf16[4,128,896]{2,1,0:T(8,128)(2,1)}) custom-call(s32[12]{0:T(128)} %concatenate.11.info, bf16[4,128,7168]{2,1,0:T(8,128)(2,1)} %mine.5, bf16[4,128,7168]{2,1,0:T(8,128)(2,1)} %collective-permute-done.6.theirs), custom_call_target="tpu_custom_call" | custom-call | tf_op jit(solution)/shard_map/pallas_call | solution.py:74
  125.7 1.7 fusion.11
  127.4 9.1 %collective-permute-start.19 = (bf16[128,896]{1,0:T(8,128)(2,1)S(1)}, bf16[128,896]{1,0:T(8,128)(2,1)S(1)}, u32[]{:S(2)}, u32[]{:S(2)}) collective-permute-start(bf16[128,896]{1,0:T(8,128)(2,1)S(1)} %get-tuple-element.70), channel_id=1, source_target_pairs={{0,32},{1,33},{2,34},{3,35},{32,0},{33,1},{34,2},{35,3},{4,36},{5,... | collective-permute-start | bytes 688136 | tf_op jit(solution)/shard_map/ppermute | solution.py:177
  136.5 7.1 %collective-permute-start.21 = (bf16[128,896]{1,0:T(8,128)(2,1)S(1)}, bf16[128,896]{1,0:T(8,128)(2,1)S(1)}, u32[]{:S(2)}, u32[]{:S(2)}) collective-permute-start(bf16[128,896]{1,0:T(8,128)(2,1)S(1)} %get-tuple-element.68), channel_id=1, source_target_pairs={{0,34},{1,35},{2,32},{3,33},{32,2},{33,3},{34,0},{35,1},{4,38},{5,... | collective-permute-start | bytes 688136 | tf_op jit(solution)/shard_map/ppermute | solution.py:177
  143.6 12.1 %collective-permute-start.22 = (bf16[128,896]{1,0:T(8,128)(2,1)S(1)}, bf16[128,896]{1,0:T(8,128)(2,1)S(1)}, u32[]{:S(2)}, u32[]{:S(2)}) collective-permute-start(bf16[128,896]{1,0:T(8,128)(2,1)S(1)} %get-tuple-element.67), channel_id=1, source_target_pairs={{0,35},{1,32},{2,33},{3,34},{32,3},{33,0},{34,1},{35,2},{4,39},{5,... | collective-permute-start | bytes 688136 | tf_op jit(solution)/shard_map/ppermute | solution.py:177
  155.7 1.7 fusion.15
  158.7 4.2 %collective-permute-done.20.refs_5_ = bf16[128,896]{1,0:T(8,128)(2,1)S(1)} collective-permute-done((bf16[128,896]{1,0:T(8,128)(2,1)S(1)}, bf16[128,896]{1,0:T(8,128)(2,1)S(1)}, u32[]{:S(2)}, u32[]{:S(2)}) %collective-permute-start.20) | collective-permute-done | bytes 229408 | tf_op jit(solution)/shard_map/ppermute | solution.py:177
  162.9 10.5 %collective-permute-start.9 = (bf16[128,896]{1,0:T(8,128)(2,1)S(1)}, bf16[128,896]{1,0:T(8,128)(2,1)S(1)}, u32[]{:S(2)}, u32[]{:S(2)}) collective-permute-start(bf16[128,896]{1,0:T(8,128)(2,1)S(1)} %copy-done.7), channel_id=1, source_target_pairs={{0,3},{1,0},{2,1},{3,2},{4,7},{5,4},{6,5},{7,6},{8,11},{9,8},{10,9... | collective-permute-start | bytes 688136 | tf_op jit(solution)/shard_map/ppermute | solution.py:22
  173.4 1.3 collective-permute-start.11
  174.9 2.9 collective-permute-start.12
  177.8 1.7 shard_map.89
  179.5 4.5 %fusion = f32[512,2048]{1,0:T(8,128)S(1)} fusion(bf16[512,896]{1,0:T(8,128)(2,1)S(1)} %get-tuple-element.47, bf16[2048,1792]{0,1:T(8,128)(2,1)} %pad_maximum_fusion), kind=kOutput, calls=%fused_computation.2 | convolution fusion | flops 1879048192 | bytes 8781824 | tf_op jit(solution)/shard_map/dot_general | solution.py:124
  184.1 5.3 %collective-permute-start.13 = (bf16[128,896]{1,0:T(8,128)(2,1)S(1)}, bf16[128,896]{1,0:T(8,128)(2,1)S(1)}, u32[]{:S(2)}, u32[]{:S(2)}) collective-permute-start(bf16[128,896]{1,0:T(8,128)(2,1)S(1)} %get-tuple-element.72), channel_id=1, source_target_pairs={{0,34},{1,35},{2,32},{3,33},{32,2},{33,3},{34,0},{35,1},{4,38},{5,... | collective-permute-start | bytes 688136 | tf_op jit(solution)/shard_map/ppermute | solution.py:177
  189.4 2.4 collective-permute-start.14
  191.8 2.4 convolution_convert_fusion.2
  194.3 5.5 %collective-permute-done.11.refs_4_ = bf16[128,896]{1,0:T(8,128)(2,1)S(1)} collective-permute-done((bf16[128,896]{1,0:T(8,128)(2,1)S(1)}, bf16[128,896]{1,0:T(8,128)(2,1)S(1)}, u32[]{:S(2)}, u32[]{:S(2)}) %collective-permute-start.11) | collective-permute-done | bytes 229408 | tf_op jit(solution)/shard_map/ppermute | solution.py:177
  199.8 7.4 %collective-permute-done.12.refs_5_ = bf16[128,896]{1,0:T(8,128)(2,1)S(1)} collective-permute-done((bf16[128,896]{1,0:T(8,128)(2,1)S(1)}, bf16[128,896]{1,0:T(8,128)(2,1)S(1)}, u32[]{:S(2)}, u32[]{:S(2)}) %collective-permute-start.12) | collective-permute-done | bytes 229408 | tf_op jit(solution)/shard_map/ppermute | solution.py:177
  207.2 4.9 %collective-permute-done.13.refs_6_ = bf16[128,896]{1,0:T(8,128)(2,1)S(1)} collective-permute-done((bf16[128,896]{1,0:T(8,128)(2,1)S(1)}, bf16[128,896]{1,0:T(8,128)(2,1)S(1)}, u32[]{:S(2)}, u32[]{:S(2)}) %collective-permute-start.13) | collective-permute-done | bytes 229408 | tf_op jit(solution)/shard_map/ppermute | solution.py:177
  212.1 4.9 %collective-permute-done.14.refs_7_ = bf16[128,896]{1,0:T(8,128)(2,1)S(1)} collective-permute-done((bf16[128,896]{1,0:T(8,128)(2,1)S(1)}, bf16[128,896]{1,0:T(8,128)(2,1)S(1)}, u32[]{:S(2)}, u32[]{:S(2)}) %collective-permute-start.14) | collective-permute-done | bytes 229408 | tf_op jit(solution)/shard_map/ppermute | solution.py:177
  217.0 1.7 shard_map.88
  218.8 2.4 fusion.2
  221.2 2.6 convolution_convert_fusion.1
  227.8 9.1 %all-to-all-start = ((f32[16,1,2]{2,1,0:T(1,128)}), f32[16,1,2]{2,1,0:T(1,128)S(1)}, u32[]{:S(2)}, u32[]{:S(2)}) async-start(f32[16,1,2]{2,1,0:T(1,128)} %broadcast_in_dim.60), calls=%async_computation | async-start | bytes 16384 | tf_op jit(solution)/shard_map/all_to_all | solution.py:211
  236.9 4.0 %convolution_convert_fusion = bf16[2048,448]{0,1:T(8,128)(2,1)} fusion(bf16[512,2048]{1,0:T(8,128)(2,1)} %copy-done.2, bf16[512,896]{1,0:T(8,128)(2,1)S(1)} %get-tuple-element.46), kind=kOutput, calls=%fused_computation.7 | convolution fusion | flops 940441600 | bytes 4456448 | tf_op jit(solution)/shard_map/dot_general | solution.py:124
  240.9 2.9 collective-permute-start.28
  244.2 2.4 collective-permute-start.27
  246.5 3.0 collective-permute-start.23
  249.5 8.9 %collective-permute-done.23 = bf16[128,2048]{1,0:T(8,128)(2,1)S(1)} collective-permute-done((bf16[128,2048]{1,0:T(8,128)(2,1)}, bf16[128,2048]{1,0:T(8,128)(2,1)S(1)}, u32[]{:S(2)}, u32[]{:S(2)}) %collective-permute-start.23) | collective-permute-done | bytes 524320 | tf_op jit(solution)/shard_map/ppermute | solution.py:22
  258.8 2.9 fusion.7
  264.3 27.8 %collective-permute-done.24 = bf16[128,2048]{1,0:T(8,128)(2,1)S(1)} collective-permute-done((bf16[128,2048]{1,0:T(8,128)(2,1)}, bf16[128,2048]{1,0:T(8,128)(2,1)S(1)}, u32[]{:S(2)}, u32[]{:S(2)}) %collective-permute-start.24) | collective-permute-done | bytes 524320 | tf_op jit(solution)/shard_map/ppermute | solution.py:22
  293.2 30.6 %collective-permute-done.26 = bf16[2048,448]{0,1:T(8,128)(2,1)S(1)} collective-permute-done((bf16[2048,448]{0,1:T(8,128)(2,1)}, bf16[2048,448]{0,1:T(8,128)(2,1)S(1)}, u32[]{:S(2)}, u32[]{:S(2)}) %collective-permute-start.26) | collective-permute-done | bytes 1835040 | tf_op jit(solution)/shard_map/ppermute | solution.py:22
  323.9 4.1 %fusion.4 = bf16[1,2048,448]{1,2,0:T(8,128)(2,1)} fusion(bf16[2048,448]{0,1:T(8,128)(2,1)} %collective-permute-done.28, bf16[2048,448]{0,1:T(8,128)(2,1)S(1)} %collective-permute-done.27, f32[2048,448]{0,1:T(8,128)S(1)} %fusion.7, bf16[2048,448]{0,1:T(8,128)(2,1)S(1)} %collective-permute-done.26, f32[]{:T(128)} %bitcast.21), kind=kLoop, calls=%fused_computation.11 | loop fusion | flops 7340032 | bytes 11010052 | tf_op jit(solution)/shard_map/broadcast_in_dim | solution.py:232
  (72 shorter events, 16.9 us)
Async XLA Ops:
  0.6 94.4 %collective-permute-start.6 = (bf16[4,128,7168]{2,1,0:T(8,128)(2,1)}, bf16[4,128,7168]{2,1,0:T(8,128)(2,1)}, u32[]{:S(2)}, u32[]{:S(2)}) collective-permute-start(bf16[4,128,7168]{2,1,0:T(8,128)(2,1)} %mine.5), channel_id=1, source_target_pairs={{0,16},{16,0},{1,17},{17,1},{2,18},{18,2},{3,19},{19,3},{4,20},{20... | collective-permute-start | bytes 22020104 | tf_op jit(solution)/shard_map/ppermute | solution.py:27
  5.7 15.5 %collective-permute-start = (bf16[128,2048]{1,0:T(8,128)(2,1)S(1)}, bf16[128,2048]{1,0:T(8,128)(2,1)S(1)}, u32[]{:S(2)}, u32[]{:S(2)}) collective-permute-start(bf16[128,2048]{1,0:T(8,128)(2,1)S(1)} %bitcast_select_fusion), channel_id=1, source_target_pairs={{0,1},{1,2},{2,3},{3,0},{4,5},{5,6},{6,7},{7,4},{8,9},{9,10},{10,1... | collective-permute-start | bytes 1572872 | tf_op jit(solution)/shard_map/ppermute | solution.py:22
  5.8 55.5 %collective-permute-start.3 = (bf16[2048,448]{0,1:T(8,128)(2,1)}, bf16[2048,448]{0,1:T(8,128)(2,1)}, u32[]{:S(2)}, u32[]{:S(2)}) collective-permute-start(bf16[2048,448]{0,1:T(8,128)(2,1)} %bitcast.48), channel_id=1, source_target_pairs={{0,8},{4,12},{8,0},{12,4},{1,9},{5,13},{9,1},{13,5},{2,10},{6,14},... | collective-permute-start | bytes 5505032 | tf_op jit(solution)/shard_map/ppermute | solution.py:22
  8.5 79.8 %collective-permute-start.4 = (bf16[2048,448]{0,1:T(8,128)(2,1)}, bf16[2048,448]{0,1:T(8,128)(2,1)}, u32[]{:S(2)}, u32[]{:S(2)}) collective-permute-start(bf16[2048,448]{0,1:T(8,128)(2,1)} %bitcast.49), channel_id=1, source_target_pairs={{0,12},{4,0},{8,4},{12,8},{1,13},{5,1},{9,5},{13,9},{2,14},{6,2},{... | collective-permute-start | bytes 5505032 | tf_op jit(solution)/shard_map/ppermute | solution.py:22
  9.3 79.6 %collective-permute-start.5 = (bf16[2048,448]{0,1:T(8,128)(2,1)}, bf16[2048,448]{0,1:T(8,128)(2,1)}, u32[]{:S(2)}, u32[]{:S(2)}) collective-permute-start(bf16[2048,448]{0,1:T(8,128)(2,1)} %bitcast.50), channel_id=1, source_target_pairs={{0,4},{4,8},{8,12},{12,0},{1,5},{5,9},{9,13},{13,1},{2,6},{6,10},{... | collective-permute-start | bytes 5505032 | tf_op jit(solution)/shard_map/ppermute | solution.py:22
  21.2 0.8 copy-start.5
  22.0 24.6 %collective-permute-start.1 = (bf16[128,2048]{1,0:T(8,128)(2,1)S(1)}, bf16[128,2048]{1,0:T(8,128)(2,1)S(1)}, u32[]{:S(2)}, u32[]{:S(2)}) collective-permute-start(bf16[128,2048]{1,0:T(8,128)(2,1)S(1)} %bitcast_select_fusion), channel_id=1, source_target_pairs={{0,2},{1,3},{2,0},{3,1},{4,6},{5,7},{6,4},{7,5},{8,10},{9,11},{10,... | collective-permute-start | bytes 1572872 | tf_op jit(solution)/shard_map/ppermute | solution.py:22
  46.5 5.0 %copy-start.6 = (bf16[128,2048]{1,0:T(8,128)(2,1)}, bf16[128,2048]{1,0:T(8,128)(2,1)S(1)}, u32[]{:S(2)}) copy-start(bf16[128,2048]{1,0:T(8,128)(2,1)S(1)} %collective-permute-done.1) | copy-start | bytes 1572868
  46.5 13.2 %collective-permute-start.2 = (bf16[128,2048]{1,0:T(8,128)(2,1)S(1)}, bf16[128,2048]{1,0:T(8,128)(2,1)}, u32[]{:S(2)}, u32[]{:S(2)}) collective-permute-start(bf16[128,2048]{1,0:T(8,128)(2,1)S(1)} %bitcast_select_fusion), channel_id=1, source_target_pairs={{0,3},{1,0},{2,1},{3,2},{4,7},{5,4},{6,5},{7,6},{8,11},{9,8},{10,9... | collective-permute-start | bytes 1572872 | tf_op jit(solution)/shard_map/ppermute | solution.py:22
  51.6 37.4 %copy-start.4 = (bf16[1,2048,448]{1,2,0:T(8,128)(2,1)S(1)}, bf16[1,2048,448]{1,2,0:T(8,128)(2,1)}, u32[]{:S(2)}) copy-start(bf16[1,2048,448]{1,2,0:T(8,128)(2,1)} %param.8) | copy-start | bytes 5505028
  61.3 41.5 %copy-start.2 = (bf16[512,2048]{1,0:T(8,128)(2,1)}, bf16[512,2048]{1,0:T(8,128)(2,1)S(1)}, u32[]{:S(2)}) copy-start(bf16[512,2048]{1,0:T(8,128)(2,1)S(1)} %pad_maximum_fusion.1) | copy-start | bytes 6291460
  100.3 25.4 %collective-permute-start.18 = (bf16[4,128,896]{2,1,0:T(8,128)(2,1)}, bf16[4,128,896]{2,1,0:T(8,128)(2,1)}, u32[]{:S(2)}, u32[]{:S(2)}) collective-permute-start(bf16[4,128,896]{2,1,0:T(8,128)(2,1)} %get-tuple-element.44), channel_id=1, source_target_pairs={{64,0},{128,64},{192,128},{32,96},{96,160},{160,224},{65,1},{129,6... | collective-permute-start | bytes 2752520 | tf_op jit(solution)/shard_map/ppermute | solution.py:169
  101.6 42.1 %collective-permute-start.10 = (bf16[4,128,896]{2,1,0:T(8,128)(2,1)}, bf16[4,128,896]{2,1,0:T(8,128)(2,1)}, u32[]{:S(2)}, u32[]{:S(2)}) collective-permute-start(bf16[4,128,896]{2,1,0:T(8,128)(2,1)} %get-tuple-element.37), channel_id=1, source_target_pairs={{64,0},{128,64},{192,128},{32,96},{96,160},{160,224},{65,1},{129,6... | collective-permute-start | bytes 2752520 | tf_op jit(solution)/shard_map/ppermute | solution.py:169
  115.1 21.4 %collective-permute-start.15 = (bf16[128,896]{1,0:T(8,128)(2,1)}, bf16[128,896]{1,0:T(8,128)(2,1)S(1)}, u32[]{:S(2)}, u32[]{:S(2)}) collective-permute-start(bf16[128,896]{1,0:T(8,128)(2,1)} %get-tuple-element.40), channel_id=1, source_target_pairs={{0,1},{1,2},{2,3},{3,0},{4,5},{5,6},{6,7},{7,4},{8,9},{9,10},{10,1... | collective-permute-start | bytes 688136 | tf_op jit(solution)/shard_map/ppermute | solution.py:22
  116.7 19.9 %collective-permute-start.16 = (bf16[128,896]{1,0:T(8,128)(2,1)}, bf16[128,896]{1,0:T(8,128)(2,1)S(1)}, u32[]{:S(2)}, u32[]{:S(2)}) collective-permute-start(bf16[128,896]{1,0:T(8,128)(2,1)} %get-tuple-element.41), channel_id=1, source_target_pairs={{0,2},{1,3},{2,0},{3,1},{4,6},{5,7},{6,4},{7,5},{8,10},{9,11},{10,... | collective-permute-start | bytes 688136 | tf_op jit(solution)/shard_map/ppermute | solution.py:22
  118.7 38.7 %collective-permute-start.17 = (bf16[128,896]{1,0:T(8,128)(2,1)}, bf16[128,896]{1,0:T(8,128)(2,1)S(1)}, u32[]{:S(2)}, u32[]{:S(2)}) collective-permute-start(bf16[128,896]{1,0:T(8,128)(2,1)} %get-tuple-element.42), channel_id=1, source_target_pairs={{0,3},{1,0},{2,1},{3,2},{4,7},{5,4},{6,5},{7,6},{8,11},{9,8},{10,9... | collective-permute-start | bytes 688136 | tf_op jit(solution)/shard_map/ppermute | solution.py:22
  125.7 31.7 %copy-start.9 = (bf16[128,896]{1,0:T(8,128)(2,1)S(1)}, bf16[128,896]{1,0:T(8,128)(2,1)}, u32[]{:S(2)}) copy-start(bf16[128,896]{1,0:T(8,128)(2,1)} %get-tuple-element.33) | copy-start | bytes 688132
  125.7 33.0 %copy-start.8 = (bf16[128,896]{1,0:T(8,128)(2,1)S(1)}, bf16[128,896]{1,0:T(8,128)(2,1)}, u32[]{:S(2)}) copy-start(bf16[128,896]{1,0:T(8,128)(2,1)} %get-tuple-element.34) | copy-start | bytes 688132
  125.7 37.2 %copy-start.7 = (bf16[128,896]{1,0:T(8,128)(2,1)S(1)}, bf16[128,896]{1,0:T(8,128)(2,1)}, u32[]{:S(2)}) copy-start(bf16[128,896]{1,0:T(8,128)(2,1)} %get-tuple-element.35) | copy-start | bytes 688132
  125.7 52.1 %copy-start.1 = (bf16[128,896]{1,0:T(8,128)(2,1)S(1)}, bf16[128,896]{1,0:T(8,128)(2,1)}, u32[]{:S(2)}) copy-start(bf16[128,896]{1,0:T(8,128)(2,1)} %get-tuple-element.39.refs_0_) | copy-start | bytes 688132
  127.4 31.2 %collective-permute-start.19 = (bf16[128,896]{1,0:T(8,128)(2,1)S(1)}, bf16[128,896]{1,0:T(8,128)(2,1)S(1)}, u32[]{:S(2)}, u32[]{:S(2)}) collective-permute-start(bf16[128,896]{1,0:T(8,128)(2,1)S(1)} %get-tuple-element.70), channel_id=1, source_target_pairs={{0,32},{1,33},{2,34},{3,35},{32,0},{33,1},{34,2},{35,3},{4,36},{5,... | collective-permute-start | bytes 688136 | tf_op jit(solution)/shard_map/ppermute | solution.py:177
  136.5 26.4 %collective-permute-start.20 = (bf16[128,896]{1,0:T(8,128)(2,1)S(1)}, bf16[128,896]{1,0:T(8,128)(2,1)S(1)}, u32[]{:S(2)}, u32[]{:S(2)}) collective-permute-start(bf16[128,896]{1,0:T(8,128)(2,1)S(1)} %get-tuple-element.69), channel_id=1, source_target_pairs={{0,33},{1,34},{2,35},{3,32},{32,1},{33,2},{34,3},{35,0},{4,37},{5,... | collective-permute-start | bytes 688136 | tf_op jit(solution)/shard_map/ppermute | solution.py:177
  136.5 36.9 %collective-permute-start.21 = (bf16[128,896]{1,0:T(8,128)(2,1)S(1)}, bf16[128,896]{1,0:T(8,128)(2,1)S(1)}, u32[]{:S(2)}, u32[]{:S(2)}) collective-permute-start(bf16[128,896]{1,0:T(8,128)(2,1)S(1)} %get-tuple-element.68), channel_id=1, source_target_pairs={{0,34},{1,35},{2,32},{3,33},{32,2},{33,3},{34,0},{35,1},{4,38},{5,... | collective-permute-start | bytes 688136 | tf_op jit(solution)/shard_map/ppermute | solution.py:177
  143.6 31.3 %collective-permute-start.22 = (bf16[128,896]{1,0:T(8,128)(2,1)S(1)}, bf16[128,896]{1,0:T(8,128)(2,1)S(1)}, u32[]{:S(2)}, u32[]{:S(2)}) collective-permute-start(bf16[128,896]{1,0:T(8,128)(2,1)S(1)} %get-tuple-element.67), channel_id=1, source_target_pairs={{0,35},{1,32},{2,33},{3,34},{32,3},{33,0},{34,1},{35,2},{4,39},{5,... | collective-permute-start | bytes 688136 | tf_op jit(solution)/shard_map/ppermute | solution.py:177
  157.4 26.6 %collective-permute-start.7 = (bf16[128,896]{1,0:T(8,128)(2,1)S(1)}, bf16[128,896]{1,0:T(8,128)(2,1)S(1)}, u32[]{:S(2)}, u32[]{:S(2)}) collective-permute-start(bf16[128,896]{1,0:T(8,128)(2,1)S(1)} %copy-done.9), channel_id=1, source_target_pairs={{0,1},{1,2},{2,3},{3,0},{4,5},{5,6},{6,7},{7,4},{8,9},{9,10},{10,1... | collective-permute-start | bytes 688136 | tf_op jit(solution)/shard_map/ppermute | solution.py:22
  158.7 30.7 %collective-permute-start.8 = (bf16[128,896]{1,0:T(8,128)(2,1)S(1)}, bf16[128,896]{1,0:T(8,128)(2,1)S(1)}, u32[]{:S(2)}, u32[]{:S(2)}) collective-permute-start(bf16[128,896]{1,0:T(8,128)(2,1)S(1)} %copy-done.8), channel_id=1, source_target_pairs={{0,2},{1,3},{2,0},{3,1},{4,6},{5,7},{6,4},{7,5},{8,10},{9,11},{10,... | collective-permute-start | bytes 688136 | tf_op jit(solution)/shard_map/ppermute | solution.py:22
  162.9 31.4 %collective-permute-start.9 = (bf16[128,896]{1,0:T(8,128)(2,1)S(1)}, bf16[128,896]{1,0:T(8,128)(2,1)S(1)}, u32[]{:S(2)}, u32[]{:S(2)}) collective-permute-start(bf16[128,896]{1,0:T(8,128)(2,1)S(1)} %copy-done.7), channel_id=1, source_target_pairs={{0,3},{1,0},{2,1},{3,2},{4,7},{5,4},{6,5},{7,6},{8,11},{9,8},{10,9... | collective-permute-start | bytes 688136 | tf_op jit(solution)/shard_map/ppermute | solution.py:22
  173.4 26.3 %collective-permute-start.11 = (bf16[128,896]{1,0:T(8,128)(2,1)S(1)}, bf16[128,896]{1,0:T(8,128)(2,1)S(1)}, u32[]{:S(2)}, u32[]{:S(2)}) collective-permute-start(bf16[128,896]{1,0:T(8,128)(2,1)S(1)} %get-tuple-element.74), channel_id=1, source_target_pairs={{0,32},{1,33},{2,34},{3,35},{32,0},{33,1},{34,2},{35,3},{4,36},{5,... | collective-permute-start | bytes 688136 | tf_op jit(solution)/shard_map/ppermute | solution.py:177
  174.9 32.3 %collective-permute-start.12 = (bf16[128,896]{1,0:T(8,128)(2,1)S(1)}, bf16[128,896]{1,0:T(8,128)(2,1)S(1)}, u32[]{:S(2)}, u32[]{:S(2)}) collective-permute-start(bf16[128,896]{1,0:T(8,128)(2,1)S(1)} %get-tuple-element.73), channel_id=1, source_target_pairs={{0,33},{1,34},{2,35},{3,32},{32,1},{33,2},{34,3},{35,0},{4,37},{5,... | collective-permute-start | bytes 688136 | tf_op jit(solution)/shard_map/ppermute | solution.py:177
  179.5 12.3 %copy-start.3 = (bf16[512,2048]{1,0:T(8,128)(2,1)S(1)}, bf16[512,2048]{1,0:T(8,128)(2,1)}, u32[]{:S(2)}) copy-start(bf16[512,2048]{1,0:T(8,128)(2,1)} %copy-done.2) | copy-start | bytes 6291460
  184.1 28.1 %collective-permute-start.13 = (bf16[128,896]{1,0:T(8,128)(2,1)S(1)}, bf16[128,896]{1,0:T(8,128)(2,1)S(1)}, u32[]{:S(2)}, u32[]{:S(2)}) collective-permute-start(bf16[128,896]{1,0:T(8,128)(2,1)S(1)} %get-tuple-element.72), channel_id=1, source_target_pairs={{0,34},{1,35},{2,32},{3,33},{32,2},{33,3},{34,0},{35,1},{4,38},{5,... | collective-permute-start | bytes 688136 | tf_op jit(solution)/shard_map/ppermute | solution.py:177
  189.4 29.4 %slice-start = ((s8[7340032]{0:T(1024)(128)(4,1)}), s8[4194304]{0:T(1024)(128)(4,1)S(1)}, s32[]{:S(2)}) async-start(s8[7340032]{0:T(1024)(128)(4,1)} %bitcast.46), calls=%async_computation.1 | async-start | bytes 8388608
  189.4 27.6 %copy-start = (bf16[128,896]{1,0:T(8,128)(2,1)S(1)}, bf16[128,896]{1,0:T(8,128)(2,1)}, u32[]{:S(2)}) copy-start(bf16[128,896]{1,0:T(8,128)(2,1)} %get-tuple-element.32.refs_0_) | copy-start | bytes 688132
  189.4 29.4 %slice-start.1 = ((s8[7340032]{0:T(1024)(128)(4,1)}), s8[3145728]{0:T(1024)(128)(4,1)S(1)}, s32[]{:S(2)}) async-start(s8[7340032]{0:T(1024)(128)(4,1)} %bitcast.46), calls=%async_computation.2 | async-start | bytes 6291456
  189.4 27.6 %collective-permute-start.14 = (bf16[128,896]{1,0:T(8,128)(2,1)S(1)}, bf16[128,896]{1,0:T(8,128)(2,1)S(1)}, u32[]{:S(2)}, u32[]{:S(2)}) collective-permute-start(bf16[128,896]{1,0:T(8,128)(2,1)S(1)} %get-tuple-element.71), channel_id=1, source_target_pairs={{0,35},{1,32},{2,33},{3,34},{32,3},{33,0},{34,1},{35,2},{4,39},{5,... | collective-permute-start | bytes 688136 | tf_op jit(solution)/shard_map/ppermute | solution.py:177
  227.8 15.9 %all-to-all-start = ((f32[16,1,2]{2,1,0:T(1,128)}), f32[16,1,2]{2,1,0:T(1,128)S(1)}, u32[]{:S(2)}, u32[]{:S(2)}) async-start(f32[16,1,2]{2,1,0:T(1,128)} %broadcast_in_dim.60), calls=%async_computation | async-start | bytes 16384 | tf_op jit(solution)/shard_map/all_to_all | solution.py:211
  240.9 52.4 %collective-permute-start.28 = (bf16[2048,448]{0,1:T(8,128)(2,1)}, bf16[2048,448]{0,1:T(8,128)(2,1)}, u32[]{:S(2)}, u32[]{:S(2)}) collective-permute-start(bf16[2048,448]{0,1:T(8,128)(2,1)} %convolution_convert_fusion), channel_id=1, source_target_pairs={{0,8},{4,12},{8,0},{12,4},{1,9},{5,13},{9,1},{13,5},{2,10},{6,14},... | collective-permute-start | bytes 5505032 | tf_op jit(solution)/shard_map/ppermute | solution.py:22
  243.8 80.1 %collective-permute-start.26 = (bf16[2048,448]{0,1:T(8,128)(2,1)}, bf16[2048,448]{0,1:T(8,128)(2,1)S(1)}, u32[]{:S(2)}, u32[]{:S(2)}) collective-permute-start(bf16[2048,448]{0,1:T(8,128)(2,1)} %convolution_convert_fusion.1), channel_id=1, source_target_pairs={{0,4},{4,8},{8,12},{12,0},{1,5},{5,9},{9,13},{13,1},{2,6},{6,10},{... | collective-permute-start | bytes 5505032 | tf_op jit(solution)/shard_map/ppermute | solution.py:22
  244.2 79.7 %collective-permute-start.27 = (bf16[2048,448]{0,1:T(8,128)(2,1)}, bf16[2048,448]{0,1:T(8,128)(2,1)S(1)}, u32[]{:S(2)}, u32[]{:S(2)}) collective-permute-start(bf16[2048,448]{0,1:T(8,128)(2,1)} %convolution_convert_fusion.2), channel_id=1, source_target_pairs={{0,12},{4,0},{8,4},{12,8},{1,13},{5,1},{9,5},{13,9},{2,14},{6,2},{... | collective-permute-start | bytes 5505032 | tf_op jit(solution)/shard_map/ppermute | solution.py:22
  246.5 11.9 %collective-permute-start.23 = (bf16[128,2048]{1,0:T(8,128)(2,1)}, bf16[128,2048]{1,0:T(8,128)(2,1)S(1)}, u32[]{:S(2)}, u32[]{:S(2)}) collective-permute-start(bf16[128,2048]{1,0:T(8,128)(2,1)} %get-tuple-element.55), channel_id=1, source_target_pairs={{0,3},{1,0},{2,1},{3,2},{4,7},{5,4},{6,5},{7,6},{8,11},{9,8},{10,9... | collective-permute-start | bytes 1572872 | tf_op jit(solution)/shard_map/ppermute | solution.py:22
  249.5 42.6 %collective-permute-start.24 = (bf16[128,2048]{1,0:T(8,128)(2,1)}, bf16[128,2048]{1,0:T(8,128)(2,1)S(1)}, u32[]{:S(2)}, u32[]{:S(2)}) collective-permute-start(bf16[128,2048]{1,0:T(8,128)(2,1)} %get-tuple-element.56), channel_id=1, source_target_pairs={{0,2},{1,3},{2,0},{3,1},{4,6},{5,7},{6,4},{7,5},{8,10},{9,11},{10,... | collective-permute-start | bytes 1572872 | tf_op jit(solution)/shard_map/ppermute | solution.py:22
  258.5 33.6 %collective-permute-start.25 = (bf16[128,2048]{1,0:T(8,128)(2,1)S(1)}, bf16[128,2048]{1,0:T(8,128)(2,1)S(1)}, u32[]{:S(2)}, u32[]{:S(2)}) collective-permute-start(bf16[128,2048]{1,0:T(8,128)(2,1)S(1)} %get-tuple-element.57), channel_id=1, source_target_pairs={{0,1},{1,2},{2,3},{3,0},{4,5},{5,6},{6,7},{7,4},{8,9},{9,10},{10,1... | collective-permute-start | bytes 1572872 | tf_op jit(solution)/shard_map/ppermute | solution.py:22

commit v5 on v4

--- a/solution.py
+++ b/solution.py
@@ -85,20 +85,23 @@
     )(info, mine, theirs)
 
 
-def residual_body(near, projected, *refs):
-    own, cross, (out, squares) = refs[:4], refs[4:8], refs[8:]
-    rows = cross[0].shape[0]
+def residual_body(chunk, near, projected, *refs):
+    own, cross, earlier, (out, squares) = refs[:4], refs[4:8], refs[8:-2], refs[-2:]
+    rows, wide = cross[0].shape
+    left = chunk * wide
+    for ref in earlier:
+        out[:, :left] = ref[...]
     total = jnp.zeros((), jnp.float32)
     for k in range(4):
         cut = slice(k * rows, (k + 1) * rows)
         target = jnp.where(near[0] == 1, own[k][...].astype(jnp.float32), cross[k][...].astype(jnp.float32))
         residual = projected[cut] - target
-        out[cut] = residual.astype(jnp.bfloat16)
+        out[cut, left:] = residual.astype(jnp.bfloat16)
         total = total + jnp.sum(residual * residual)
     squares[0] = total
 
 
-def residual_of(near, projected, own, chunk, cross):
+def residual_of(near, projected, own, chunk, cross, *earlier):
     tokens = projected.shape[0]
     rows, wide = cross[0].shape
 
@@ -107,17 +110,18 @@
 
     smem = pl.BlockSpec(memory_space=pltpu.SMEM)
     return pl.pallas_call(
-        residual_body,
+        functools.partial(residual_body, chunk),
         out_shape=(
-            jax.ShapeDtypeStruct((tokens, wide), jnp.bfloat16),
+            jax.ShapeDtypeStruct((tokens, (chunk + 1) * wide), jnp.bfloat16),
             jax.ShapeDtypeStruct((1,), jnp.float32),
         ),
         grid=(1,),
         in_specs=[smem, pl.BlockSpec((tokens, wide), lambda i: (0, chunk))]
-        + [whole((rows, wide))] * 8,
-        out_specs=(whole((tokens, wide)), smem),
+        + [whole((rows, wide))] * 8
+        + [whole((tokens, wide))] * chunk,
+        out_specs=(whole((tokens, (chunk + 1) * wide)), smem),
         compiler_params=pltpu.CompilerParams(vmem_limit_bytes=16 << 20),
-    )(near, projected, *own, *cross)
+    )(near, projected, *own, *cross, *earlier)
 
 
 def dot(a, b, ca, cb):
@@ -132,6 +136,7 @@
     here = 2 * chip + core
     weights = projector[0]
     tokens = student_states.shape[1]
+    half = weights.shape[0] // 2
     width = weights.shape[1]
 
     theirs = exchange(teacher_states, "core", 1)
@@ -196,20 +201,26 @@
         return dot(rows, residual, 0, 0)
 
     first_res, squares_first = residual_of(near, projected, own_first, 0, crossed_first)
-    opp_part = grad(first_res[:, :width])
-    from_opp = rotate(opp_part.astype(jnp.bfloat16), "x", 2)
+    opp_part = grad(first_res[:, :width]).astype(jnp.bfloat16)
+    up_top = rotate(opp_part[:half], "x", 1)
+    down_bot = rotate(opp_part[half:], "x", -1)
     next_part = lax.optimization_barrier(grad(first_res[:, width:]).astype(jnp.bfloat16))
-    part_first = lax.optimization_barrier(dot(first_res, w_all[:, : 2 * width], 1, 1))
-    second_res, squares_second = residual_of(near, projected, own_second, 1, crossed_second)
-    student_part = (part_first + dot(second_res, w_all[:, 2 * width :], 1, 1)).astype(jnp.bfloat16)
+    residual, squares_second = residual_of(near, projected, own_second, 1, crossed_second, first_res)
+    student_part = dot(residual, w_all, 1, 1).astype(jnp.bfloat16)
     parts = [student_part[k * tokens : (k + 1) * tokens] for k in range(4)]
-    prev_part = grad(second_res[:, :width]).astype(jnp.bfloat16)
+    prev_part = grad(residual[:, 2 * width : 3 * width])
+
+    def plus(part, arrived, low, high):
+        padded = jnp.pad(arrived.astype(jnp.float32), ((low, high), (0, 0)))
+        return (part.astype(jnp.float32) + padded).astype(jnp.bfloat16)
+
+    next_part = plus(next_part, up_top, 0, half)
+    prev_part = plus(prev_part, down_bot, half, 0)
 
     sums = jnp.stack([squares_first[0] + squares_second[0], valid_counts[0].astype(jnp.float32)])
-    sums, parts, prev_part = lax.optimization_barrier((sums, parts, prev_part))
-    copies = jnp.broadcast_to(sums, (lax.axis_size(DP), 2))
-    sums = jnp.sum(lax.all_to_all(copies, DP, split_axis=0, concat_axis=0, tiled=True), axis=0)
-    sums, parts, prev_part, next_part = lax.optimization_barrier((sums, parts, prev_part, next_part))
+    for axis in ("zl", "x"):
+        sums = sums + exchange(sums, axis, 1)
+        sums = sums + exchange(sums, axis, 2)
     total = sums[1]
     loss = sums[:1] / (total * (width * lax.axis_size(DP)))
     factor = loss_scale / total
@@ -219,17 +230,17 @@
         returned.append(rotate(parts[k], "zl", -k))
     from_next = rotate(prev_part, "x", -1)
     from_prev = rotate(next_part, "x", 1)
-    own_part = lax.optimization_barrier(grad(second_res[:, width:]))
+    own_part = lax.optimization_barrier(grad(residual[:, 3 * width :]))
 
     student_grad = parts[0].astype(jnp.float32)
     for part in returned:
         student_grad = student_grad + part.astype(jnp.float32)
     student_grad = (student_grad * factor).astype(jnp.bfloat16)
     projector_grad = own_part
-    for part in (from_prev, from_next, from_opp):
+    for part in (from_prev, from_next):
         projector_grad = projector_grad + part.astype(jnp.float32)
-    projector_grad = (projector_grad * factor).astype(jnp.bfloat16)
-    return (student_grad[None], projector_grad[None], loss)
+    projector_grad = (projector_grad * factor).astype(jnp.bfloat16)[None]
+    return (student_grad[None], projector_grad, loss)
 
 
 def solution(mesh):

time: 330 us -> 317 us (0.961)
  waiting for transfers between devices: 164 us -> 180 us
  starting transfers between devices: 87.6 us -> 73.3 us
  matrix products: 25.8 us -> 16.2 us
  other arithmetic: 21.1 us -> 16.5 us
    ppermute x18 -> x19, waiting for transfers between devices: 137 us -> 83.3 us  [rotate(): lax.ppermute(block, axis, [(i, (i + distance) % n) for i in range(n)])]
    ppermute x1 -> x5, waiting for transfers between devices: 0.01 us -> 35.9 us  [exchange(): return lax.ppermute(block, axis, [(i, i ^ bit) for i in range(n)])]
    ppermute x8, waiting for transfers between devices: 27.2 us -> 60.5 us  [send_across(): sent.append(lax.ppermute(slab, ('zh', 'zl'), route))]
    dot_general x7 -> x6, matrix products: 25.8 us -> 16.2 us  [dot(): lax.dot_general(a, b, (((ca,), (cb,)), ((), ())), preferred_element_type=...]
    all_to_all x1 -> x0, starting transfers between devices: 9.05 us -> none  [compute(): lax.all_to_all(copies, DP, split_axis=0, concat_axis=0, tiled=True)]
    ppermute x1 -> x5, starting transfers between devices: 3.29 us -> 11.8 us  [exchange(): return lax.ppermute(block, axis, [(i, i ^ bit) for i in range(n)])]
    ppermute x18 -> x19, starting transfers between devices: 32.4 us -> 25.4 us  [rotate(): lax.ppermute(block, axis, [(i, (i + distance) % n) for i in range(n)])]
    ppermute x8, starting transfers between devices: 40.2 us -> 33.4 us  [send_across(): sent.append(lax.ppermute(slab, ('zh', 'zl'), route))]
  transfers between devices with their start and end apart: 30 -> 34, of which waited for: 14 -> 13; matrix products, arithmetic and copies ran while one was open for 12% -> 11% of each run, Pallas kernels for 4% -> 6%
where the time goes in v5:
time: 317 us; the launch traced here: 315 us
  waiting for transfers between devices  180 us (57%)
  starting transfers between devices  73.3 us (23%)
  Pallas kernels  19.3 us (6%)
  other arithmetic  16.5 us (5%)
  matrix products  16.2 us (5%)
  between operations  6.72 us (2%)
  local copies, waits for them, and re-layouts  3.6 us (1%)
    ppermute x19, waiting for transfers between devices, rotate(): lax.ppermute(block, axis, [(i, (i + distance) % n) for i in range(n)])  83.3 us
    ppermute x8, waiting for transfers between devices, send_across(): sent.append(lax.ppermute(slab, ('zh', 'zl'), route))  60.5 us
    ppermute x5, waiting for transfers between devices, exchange(): return lax.ppermute(block, axis, [(i, i ^ bit) for i in range(n)])  35.9 us
    ppermute x8, starting transfers between devices, send_across(): sent.append(lax.ppermute(slab, ('zh', 'zl'), route))  33.4 us
    ppermute x19, starting transfers between devices, rotate(): lax.ppermute(block, axis, [(i, (i + distance) % n) for i in range(n)])  25.4 us
    dot_general x6, matrix products, dot(): lax.dot_general(a, b, (((ca,), (cb,)), ((), ())), preferred_element_type=...  16.2 us
    pallas_call x3, Pallas kernels, prepare(): pl.pallas_call(functools.partial(prepare_body, piece), out_shape=[jax.Sha...  15.8 us
    ppermute x5, starting transfers between devices, exchange(): return lax.ppermute(block, axis, [(i, i ^ bit) for i in range(n)])  11.8 us
  transfers between devices with their start and end apart: 34, of which 13 were waited for; matrix products, arithmetic and copies ran while one was open for 11% of the time, Pallas kernels for 6%

profile of v5, /device:TPU:1, one launch (start us, length us, event | category | flops | bytes accessed | tf_op | source)
XLA Modules:
  0.0 315.2 jit_solution(11436148814214023834)
XLA Ops:
  0.6 3.3 %collective-permute-start.6 = (bf16[4,128,7168]{2,1,0:T(8,128)(2,1)}, bf16[4,128,7168]{2,1,0:T(8,128)(2,1)}, u32[]{:S(2)}, u32[]{:S(2)}) collective-permute-start(bf16[4,128,7168]{2,1,0:T(8,128)(2,1)} %mine.5), channel_id=1, source_target_pairs={{0,16},{16,0},{1,17},{17,1},{2,18},{18,2},{3,19},{19,3},{4,20},{20... | collective-permute-start | bytes 22020104 | tf_op jit(solution)/shard_map/ppermute | solution.py:27
  3.9 1.0 collective-permute-start.3
  7.1 1.1 bitcast_select_fusion
  8.2 1.7 collective-permute-start
  12.5 11.6 %collective-permute-done = bf16[128,2048]{1,0:T(8,128)(2,1)S(1)} collective-permute-done((bf16[128,2048]{1,0:T(8,128)(2,1)S(1)}, bf16[128,2048]{1,0:T(8,128)(2,1)S(1)}, u32[]{:S(2)}, u32[]{:S(2)}) %collective-permute-start) | collective-permute-done | bytes 524320 | tf_op jit(solution)/shard_map/ppermute | solution.py:22
  24.0 1.3 collective-permute-start.2
  28.0 5.3 %shard_map.87 = (bf16[4,128,896]{2,1,0:T(8,128)(2,1)}, bf16[4,128,896]{2,1,0:T(8,128)(2,1)}) custom-call(s32[12]{0:T(128)} %concatenate.11.info, bf16[4,128,7168]{2,1,0:T(8,128)(2,1)} %mine.5, bf16[4,128,7168]{2,1,0:T(8,128)(2,1)} %collective-permute-done.6.theirs), custom_call_target="tpu_custom_call" | custom-call | tf_op jit(solution)/shard_map/pallas_call | solution.py:74
  33.3 15.7 %collective-permute-done.1 = bf16[128,2048]{1,0:T(8,128)(2,1)S(1)} collective-permute-done((bf16[128,2048]{1,0:T(8,128)(2,1)S(1)}, bf16[128,2048]{1,0:T(8,128)(2,1)S(1)}, u32[]{:S(2)}, u32[]{:S(2)}) %collective-permute-start.1) | collective-permute-done | bytes 524320 | tf_op jit(solution)/shard_map/ppermute | solution.py:22
  49.8 1.4 collective-permute-start.18
  51.2 1.6 pad_maximum_fusion.1
  52.8 32.2 %collective-permute-done.4 = bf16[2048,448]{0,1:T(8,128)(2,1)} collective-permute-done((bf16[2048,448]{0,1:T(8,128)(2,1)}, bf16[2048,448]{0,1:T(8,128)(2,1)}, u32[]{:S(2)}, u32[]{:S(2)}) %collective-permute-start.4) | collective-permute-done | bytes 1835040 | tf_op jit(solution)/shard_map/ppermute | solution.py:22
  85.0 2.0 collective-permute-done.5
  87.0 5.6 %pad_maximum_fusion = bf16[2048,1792]{0,1:T(8,128)(2,1)} fusion(bf16[2048,448]{0,1:T(8,128)(2,1)S(1)} %bitcast.51, bf16[2048,448]{0,1:T(8,128)(2,1)} %collective-permute-done.5, bf16[2048,448]{0,1:T(8,128)(2,1)} %collective-permute-done.4, bf16[2048,448]{0,1:T(8,128)(2,1)S(1)} %collective-permute-done.3), kind=kLoop, calls=%fused_computation | loop fusion | flops 29360128 | bytes 14680064 | tf_op jit(solution)/shard_map/concatenate | solution.py:196
  92.6 5.2 %shard_map.85 = (bf16[128,896]{1,0:T(8,128)(2,1)}, bf16[128,896]{1,0:T(8,128)(2,1)}, bf16[128,896]{1,0:T(8,128)(2,1)}, bf16[128,896]{1,0:T(8,128)(2,1)}, bf16[12...) custom-call(s32[12]{0:T(128)} %concatenate.11.info, ...), custom_call_target="tpu_custom_call" | custom-call | tf_op jit(solution)/shard_map/pallas_call | solution.py:74
  97.9 2.9 collective-permute-start.16
  101.5 1.3 collective-permute-start.10
  102.8 5.3 %shard_map.86 = (bf16[4,128,896]{2,1,0:T(8,128)(2,1)}, bf16[4,128,896]{2,1,0:T(8,128)(2,1)}) custom-call(s32[12]{0:T(128)} %concatenate.11.info, bf16[4,128,7168]{2,1,0:T(8,128)(2,1)} %mine.5, bf16[4,128,7168]{2,1,0:T(8,128)(2,1)} %collective-permute-done.6.theirs), custom_call_target="tpu_custom_call" | custom-call | tf_op jit(solution)/shard_map/pallas_call | solution.py:74
  108.1 1.4 fusion.7
  109.5 7.3 %collective-permute-start.19 = (bf16[128,896]{1,0:T(8,128)(2,1)S(1)}, bf16[128,896]{1,0:T(8,128)(2,1)S(1)}, u32[]{:S(2)}, u32[]{:S(2)}) collective-permute-start(bf16[128,896]{1,0:T(8,128)(2,1)S(1)} %get-tuple-element.45), channel_id=1, source_target_pairs={{0,32},{1,33},{2,34},{3,35},{32,0},{33,1},{34,2},{35,3},{4,36},{5,... | collective-permute-start | bytes 688136 | tf_op jit(solution)/shard_map/ppermute | solution.py:182
  116.9 7.1 %fusion.19.projected = f32[512,1792]{1,0:T(8,128)S(1)} fusion(bf16[512,2048]{1,0:T(8,128)(2,1)S(1)} %pad_maximum_fusion.1, bf16[2048,1792]{0,1:T(8,128)(2,1)} %pad_maximum_fusion), kind=kOutput, calls=%fused_computation.49 | convolution fusion | flops 3758096384 | bytes 13107200 | tf_op jit(solution)/shard_map/dot_general | solution.py:128
  124.1 1.3 collective-permute-start.8
  125.4 20.5 %collective-permute-start.20 = (bf16[128,896]{1,0:T(8,128)(2,1)S(1)}, bf16[128,896]{1,0:T(8,128)(2,1)S(1)}, u32[]{:S(2)}, u32[]{:S(2)}) collective-permute-start(bf16[128,896]{1,0:T(8,128)(2,1)S(1)} %get-tuple-element.44), channel_id=1, source_target_pairs={{0,33},{1,34},{2,35},{3,32},{32,1},{33,2},{34,3},{35,0},{4,37},{5,... | collective-permute-start | bytes 688136 | tf_op jit(solution)/shard_map/ppermute | solution.py:182
  145.9 1.8 collective-permute-start.22
  147.8 17.1 %collective-permute-done.20.refs_5_ = bf16[128,896]{1,0:T(8,128)(2,1)S(1)} collective-permute-done((bf16[128,896]{1,0:T(8,128)(2,1)S(1)}, bf16[128,896]{1,0:T(8,128)(2,1)S(1)}, u32[]{:S(2)}, u32[]{:S(2)}) %collective-permute-start.20) | collective-permute-done | bytes 229408 | tf_op jit(solution)/shard_map/ppermute | solution.py:182
  164.8 7.3 %collective-permute-done.21.refs_6_ = bf16[128,896]{1,0:T(8,128)(2,1)S(1)} collective-permute-done((bf16[128,896]{1,0:T(8,128)(2,1)S(1)}, bf16[128,896]{1,0:T(8,128)(2,1)S(1)}, u32[]{:S(2)}, u32[]{:S(2)}) %collective-permute-start.21) | collective-permute-done | bytes 229408 | tf_op jit(solution)/shard_map/ppermute | solution.py:182
  172.1 14.8 %collective-permute-done.22.refs_7_ = bf16[128,896]{1,0:T(8,128)(2,1)S(1)} collective-permute-done((bf16[128,896]{1,0:T(8,128)(2,1)S(1)}, bf16[128,896]{1,0:T(8,128)(2,1)S(1)}, u32[]{:S(2)}, u32[]{:S(2)}) %collective-permute-start.22) | collective-permute-done | bytes 229408 | tf_op jit(solution)/shard_map/ppermute | solution.py:182
  186.9 1.6 shard_map.88
  188.7 3.7 %collective-permute-start.14 = (bf16[128,896]{1,0:T(8,128)(2,1)S(1)}, bf16[128,896]{1,0:T(8,128)(2,1)S(1)}, u32[]{:S(2)}, u32[]{:S(2)}) collective-permute-start(bf16[128,896]{1,0:T(8,128)(2,1)S(1)} %get-tuple-element.46), channel_id=1, source_target_pairs={{0,35},{1,32},{2,33},{3,34},{32,3},{33,0},{34,1},{35,2},{4,39},{5,... | collective-permute-start | bytes 688136 | tf_op jit(solution)/shard_map/ppermute | solution.py:182
  192.4 1.2 convolution_convert_fusion.1
  193.6 21.3 %collective-permute-done.12.refs_5_ = bf16[128,896]{1,0:T(8,128)(2,1)S(1)} collective-permute-done((bf16[128,896]{1,0:T(8,128)(2,1)S(1)}, bf16[128,896]{1,0:T(8,128)(2,1)S(1)}, u32[]{:S(2)}, u32[]{:S(2)}) %collective-permute-start.12) | collective-permute-done | bytes 229408 | tf_op jit(solution)/shard_map/ppermute | solution.py:182
  215.0 1.9 shard_map.89
  218.2 6.1 %collective-permute-start.26 = (f32[2]{0:T(128)S(1)}, f32[2]{0:T(128)S(1)}, u32[]{:S(2)}, u32[]{:S(2)}) collective-permute-start(f32[2]{0:T(128)S(1)} %pad_maximum_fusion.2), channel_id=1, source_target_pairs={{0,1},{1,0},{2,3},{3,2},{4,5},{5,4},{6,7},{7,6},{8,9},{9,8},{10,11... | collective-permute-start | bytes 32 | tf_op jit(solution)/shard_map/ppermute | solution.py:27
  224.6 2.7 collective-permute-start.32
  227.3 4.2 %convolution_convert_fusion = bf16[512,2048]{1,0:T(8,128)(2,1)S(1)} fusion(bf16[512,1792]{1,0:T(8,128)(2,1)S(1)} %get-tuple-element.32, bf16[2048,1792]{0,1:T(8,128)(2,1)S(1)} %bitcast.47), kind=kOutput, calls=%fused_computation.4 | convolution fusion | flops 3759144960 | bytes 11272192 | tf_op jit(solution)/shard_map/dot_general | solution.py:128
  231.5 1.3 convolution_convert_fusion.2
  232.8 14.1 %collective-permute-done.30 = bf16[1024,448]{0,1:T(8,128)(2,1)S(1)} collective-permute-done((bf16[1024,448]{0,1:T(8,128)(2,1)S(1)}, bf16[1024,448]{0,1:T(8,128)(2,1)S(1)}, u32[]{:S(2)}, u32[]{:S(2)}) %collective-permute-start.30) | collective-permute-done | bytes 917536 | tf_op jit(solution)/shard_map/ppermute | solution.py:22
  247.4 1.2 add_convert_fusion
  248.6 2.7 collective-permute-start.33
  251.4 7.2 %collective-permute-start.23 = (bf16[128,2048]{1,0:T(8,128)(2,1)S(1)}, bf16[128,2048]{1,0:T(8,128)(2,1)S(1)}, u32[]{:S(2)}, u32[]{:S(2)}) collective-permute-start(bf16[128,2048]{1,0:T(8,128)(2,1)S(1)} %get-tuple-element.37), channel_id=1, source_target_pairs={{0,3},{1,0},{2,1},{3,2},{4,7},{5,4},{6,5},{7,6},{8,11},{9,8},{10,9... | collective-permute-start | bytes 1572872 | tf_op jit(solution)/shard_map/ppermute | solution.py:22
  258.6 2.4 collective-permute-start.27
  261.0 29.5 %collective-permute-done.27 = f32[2]{0:T(128)S(1)} collective-permute-done((f32[2]{0:T(128)S(1)}, f32[2]{0:T(128)S(1)}, u32[]{:S(2)}, u32[]{:S(2)}) %collective-permute-start.27) | collective-permute-done | bytes 40 | tf_op jit(solution)/shard_map/ppermute | solution.py:27
  290.7 2.4 collective-permute-done.28
  293.1 3.9 %collective-permute-done.29 = f32[2]{0:T(128)S(1)} collective-permute-done((f32[2]{0:T(128)S(1)}, f32[2]{0:T(128)S(1)}, u32[]{:S(2)}, u32[]{:S(2)}) %collective-permute-start.29) | collective-permute-done | bytes 40 | tf_op jit(solution)/shard_map/ppermute | solution.py:27
  297.0 2.1 collective-permute-start.25
  299.2 1.3 fusion.5
  303.1 7.7 %collective-permute-done.25 = bf16[128,2048]{1,0:T(8,128)(2,1)S(1)} collective-permute-done((bf16[128,2048]{1,0:T(8,128)(2,1)S(1)}, bf16[128,2048]{1,0:T(8,128)(2,1)S(1)}, u32[]{:S(2)}, u32[]{:S(2)}) %collective-permute-start.25) | collective-permute-done | bytes 524320 | tf_op jit(solution)/shard_map/ppermute | solution.py:22
  310.8 1.1 fusion.1
  311.9 2.2 fusion
  (80 shorter events, 9.8 us)
Async XLA Ops:
  0.6 23.4 %collective-permute-start.6 = (bf16[4,128,7168]{2,1,0:T(8,128)(2,1)}, bf16[4,128,7168]{2,1,0:T(8,128)(2,1)}, u32[]{:S(2)}, u32[]{:S(2)}) collective-permute-start(bf16[4,128,7168]{2,1,0:T(8,128)(2,1)} %mine.5), channel_id=1, source_target_pairs={{0,16},{16,0},{1,17},{17,1},{2,18},{18,2},{3,19},{19,3},{4,20},{20... | collective-permute-start | bytes 22020104 | tf_op jit(solution)/shard_map/ppermute | solution.py:27
  3.9 48.9 %collective-permute-start.3 = (bf16[2048,448]{0,1:T(8,128)(2,1)}, bf16[2048,448]{0,1:T(8,128)(2,1)S(1)}, u32[]{:S(2)}, u32[]{:S(2)}) collective-permute-start(bf16[2048,448]{0,1:T(8,128)(2,1)} %bitcast.48), channel_id=1, source_target_pairs={{0,8},{4,12},{8,0},{12,4},{1,9},{5,13},{9,1},{13,5},{2,10},{6,14},... | collective-permute-start | bytes 5505032 | tf_op jit(solution)/shard_map/ppermute | solution.py:22
  5.0 80.0 %collective-permute-start.4 = (bf16[2048,448]{0,1:T(8,128)(2,1)}, bf16[2048,448]{0,1:T(8,128)(2,1)}, u32[]{:S(2)}, u32[]{:S(2)}) collective-permute-start(bf16[2048,448]{0,1:T(8,128)(2,1)} %bitcast.49), channel_id=1, source_target_pairs={{0,12},{4,0},{8,4},{12,8},{1,13},{5,1},{9,5},{13,9},{2,14},{6,2},{... | collective-permute-start | bytes 5505032 | tf_op jit(solution)/shard_map/ppermute | solution.py:22
  5.8 81.2 %collective-permute-start.5 = (bf16[2048,448]{0,1:T(8,128)(2,1)}, bf16[2048,448]{0,1:T(8,128)(2,1)}, u32[]{:S(2)}, u32[]{:S(2)}) collective-permute-start(bf16[2048,448]{0,1:T(8,128)(2,1)} %bitcast.50), channel_id=1, source_target_pairs={{0,4},{4,8},{8,12},{12,0},{1,5},{5,9},{9,13},{13,1},{2,6},{6,10},{... | collective-permute-start | bytes 5505032 | tf_op jit(solution)/shard_map/ppermute | solution.py:22
  8.2 15.8 %collective-permute-start = (bf16[128,2048]{1,0:T(8,128)(2,1)S(1)}, bf16[128,2048]{1,0:T(8,128)(2,1)S(1)}, u32[]{:S(2)}, u32[]{:S(2)}) collective-permute-start(bf16[128,2048]{1,0:T(8,128)(2,1)S(1)} %bitcast_select_fusion), channel_id=1, source_target_pairs={{0,1},{1,2},{2,3},{3,0},{4,5},{5,6},{6,7},{7,4},{8,9},{9,10},{10,1... | collective-permute-start | bytes 1572872 | tf_op jit(solution)/shard_map/ppermute | solution.py:22
  24.0 9.3 %copy-start.4 = (bf16[128,2048]{1,0:T(8,128)(2,1)}, bf16[128,2048]{1,0:T(8,128)(2,1)S(1)}, u32[]{:S(2)}) copy-start(bf16[128,2048]{1,0:T(8,128)(2,1)S(1)} %collective-permute-done) | copy-start | bytes 1572868
  24.0 24.9 %collective-permute-start.1 = (bf16[128,2048]{1,0:T(8,128)(2,1)S(1)}, bf16[128,2048]{1,0:T(8,128)(2,1)S(1)}, u32[]{:S(2)}, u32[]{:S(2)}) collective-permute-start(bf16[128,2048]{1,0:T(8,128)(2,1)S(1)} %bitcast_select_fusion), channel_id=1, source_target_pairs={{0,2},{1,3},{2,0},{3,1},{4,6},{5,7},{6,4},{7,5},{8,10},{9,11},{10,... | collective-permute-start | bytes 1572872 | tf_op jit(solution)/shard_map/ppermute | solution.py:22
  24.0 27.2 %collective-permute-start.2 = (bf16[128,2048]{1,0:T(8,128)(2,1)S(1)}, bf16[128,2048]{1,0:T(8,128)(2,1)}, u32[]{:S(2)}, u32[]{:S(2)}) collective-permute-start(bf16[128,2048]{1,0:T(8,128)(2,1)S(1)} %bitcast_select_fusion), channel_id=1, source_target_pairs={{0,3},{1,0},{2,1},{3,2},{4,7},{5,4},{6,5},{7,6},{8,11},{9,8},{10,9... | collective-permute-start | bytes 1572872 | tf_op jit(solution)/shard_map/ppermute | solution.py:22
  49.0 0.8 copy-start.5
  49.8 37.2 %copy-start.2 = (bf16[1,2048,448]{1,2,0:T(8,128)(2,1)S(1)}, bf16[1,2048,448]{1,2,0:T(8,128)(2,1)}, u32[]{:S(2)}) copy-start(bf16[1,2048,448]{1,2,0:T(8,128)(2,1)} %param.8) | copy-start | bytes 5505028
  49.8 58.4 %collective-permute-start.18 = (bf16[4,128,896]{2,1,0:T(8,128)(2,1)}, bf16[4,128,896]{2,1,0:T(8,128)(2,1)S(1)}, u32[]{:S(2)}, u32[]{:S(2)}) collective-permute-start(bf16[4,128,896]{2,1,0:T(8,128)(2,1)} %get-tuple-element.30), channel_id=1, source_target_pairs={{64,0},{128,64},{192,128},{32,96},{96,160},{160,224},{65,1},{129,6... | collective-permute-start | bytes 2752520 | tf_op jit(solution)/shard_map/ppermute | solution.py:174
  97.8 26.2 %collective-permute-start.15 = (bf16[128,896]{1,0:T(8,128)(2,1)}, bf16[128,896]{1,0:T(8,128)(2,1)S(1)}, u32[]{:S(2)}, u32[]{:S(2)}) collective-permute-start(bf16[128,896]{1,0:T(8,128)(2,1)} %get-tuple-element.26), channel_id=1, source_target_pairs={{0,1},{1,2},{2,3},{3,0},{4,5},{5,6},{6,7},{7,4},{8,9},{9,10},{10,1... | collective-permute-start | bytes 688136 | tf_op jit(solution)/shard_map/ppermute | solution.py:22
  97.9 26.3 %collective-permute-start.16 = (bf16[128,896]{1,0:T(8,128)(2,1)}, bf16[128,896]{1,0:T(8,128)(2,1)S(1)}, u32[]{:S(2)}, u32[]{:S(2)}) collective-permute-start(bf16[128,896]{1,0:T(8,128)(2,1)} %get-tuple-element.27), channel_id=1, source_target_pairs={{0,2},{1,3},{2,0},{3,1},{4,6},{5,7},{6,4},{7,5},{8,10},{9,11},{10,... | collective-permute-start | bytes 688136 | tf_op jit(solution)/shard_map/ppermute | solution.py:22
  100.8 24.6 %collective-permute-start.17 = (bf16[128,896]{1,0:T(8,128)(2,1)}, bf16[128,896]{1,0:T(8,128)(2,1)S(1)}, u32[]{:S(2)}, u32[]{:S(2)}) collective-permute-start(bf16[128,896]{1,0:T(8,128)(2,1)} %get-tuple-element.28), channel_id=1, source_target_pairs={{0,3},{1,0},{2,1},{3,2},{4,7},{5,4},{6,5},{7,6},{8,11},{9,8},{10,9... | collective-permute-start | bytes 688136 | tf_op jit(solution)/shard_map/ppermute | solution.py:22
  101.5 44.4 %collective-permute-start.10 = (bf16[4,128,896]{2,1,0:T(8,128)(2,1)}, bf16[4,128,896]{2,1,0:T(8,128)(2,1)S(1)}, u32[]{:S(2)}, u32[]{:S(2)}) collective-permute-start(bf16[4,128,896]{2,1,0:T(8,128)(2,1)} %get-tuple-element.24), channel_id=1, source_target_pairs={{64,0},{128,64},{192,128},{32,96},{96,160},{160,224},{65,1},{129,6... | collective-permute-start | bytes 2752520 | tf_op jit(solution)/shard_map/ppermute | solution.py:174
  109.5 14.5 %copy-start.8 = (bf16[128,896]{1,0:T(8,128)(2,1)S(1)}, bf16[128,896]{1,0:T(8,128)(2,1)}, u32[]{:S(2)}) copy-start(bf16[128,896]{1,0:T(8,128)(2,1)} %get-tuple-element.20) | copy-start | bytes 688132
  109.5 14.6 %copy-start.7 = (bf16[128,896]{1,0:T(8,128)(2,1)S(1)}, bf16[128,896]{1,0:T(8,128)(2,1)}, u32[]{:S(2)}) copy-start(bf16[128,896]{1,0:T(8,128)(2,1)} %get-tuple-element.21) | copy-start | bytes 688132
  109.5 38.1 %copy-start.3 = (bf16[4,128,896]{2,1,0:T(8,128)(2,1)S(1)}, bf16[4,128,896]{2,1,0:T(8,128)(2,1)}, u32[]{:S(2)}) copy-start(bf16[4,128,896]{2,1,0:T(8,128)(2,1)} %get-tuple-element.23) | copy-start | bytes 2752516
  109.5 36.3 %collective-permute-start.19 = (bf16[128,896]{1,0:T(8,128)(2,1)S(1)}, bf16[128,896]{1,0:T(8,128)(2,1)S(1)}, u32[]{:S(2)}, u32[]{:S(2)}) collective-permute-start(bf16[128,896]{1,0:T(8,128)(2,1)S(1)} %get-tuple-element.45), channel_id=1, source_target_pairs={{0,32},{1,33},{2,34},{3,35},{32,0},{33,1},{34,2},{35,3},{4,36},{5,... | collective-permute-start | bytes 688136 | tf_op jit(solution)/shard_map/ppermute | solution.py:182
  124.0 40.8 %copy-start.6 = (bf16[128,896]{1,0:T(8,128)(2,1)S(1)}, bf16[128,896]{1,0:T(8,128)(2,1)}, u32[]{:S(2)}) copy-start(bf16[128,896]{1,0:T(8,128)(2,1)} %get-tuple-element.22) | copy-start | bytes 688132
  124.0 63.0 %copy-start.1 = (bf16[128,896]{1,0:T(8,128)(2,1)S(1)}, bf16[128,896]{1,0:T(8,128)(2,1)}, u32[]{:S(2)}) copy-start(bf16[128,896]{1,0:T(8,128)(2,1)} %get-tuple-element.25.refs_0_) | copy-start | bytes 688132
  124.0 64.6 %collective-permute-start.7 = (bf16[128,896]{1,0:T(8,128)(2,1)S(1)}, bf16[128,896]{1,0:T(8,128)(2,1)S(1)}, u32[]{:S(2)}, u32[]{:S(2)}) collective-permute-start(bf16[128,896]{1,0:T(8,128)(2,1)S(1)} %copy-done.8), channel_id=1, source_target_pairs={{0,1},{1,2},{2,3},{3,0},{4,5},{5,6},{6,7},{7,4},{8,9},{9,10},{10,1... | collective-permute-start | bytes 688136 | tf_op jit(solution)/shard_map/ppermute | solution.py:22
  124.1 64.6 %collective-permute-start.8 = (bf16[128,896]{1,0:T(8,128)(2,1)S(1)}, bf16[128,896]{1,0:T(8,128)(2,1)S(1)}, u32[]{:S(2)}, u32[]{:S(2)}) collective-permute-start(bf16[128,896]{1,0:T(8,128)(2,1)S(1)} %copy-done.7), channel_id=1, source_target_pairs={{0,2},{1,3},{2,0},{3,1},{4,6},{5,7},{6,4},{7,5},{8,10},{9,11},{10,... | collective-permute-start | bytes 688136 | tf_op jit(solution)/shard_map/ppermute | solution.py:22
  125.4 39.4 %collective-permute-start.20 = (bf16[128,896]{1,0:T(8,128)(2,1)S(1)}, bf16[128,896]{1,0:T(8,128)(2,1)S(1)}, u32[]{:S(2)}, u32[]{:S(2)}) collective-permute-start(bf16[128,896]{1,0:T(8,128)(2,1)S(1)} %get-tuple-element.44), channel_id=1, source_target_pairs={{0,33},{1,34},{2,35},{3,32},{32,1},{33,2},{34,3},{35,0},{4,37},{5,... | collective-permute-start | bytes 688136 | tf_op jit(solution)/shard_map/ppermute | solution.py:182
  145.9 26.3 %collective-permute-start.21 = (bf16[128,896]{1,0:T(8,128)(2,1)S(1)}, bf16[128,896]{1,0:T(8,128)(2,1)S(1)}, u32[]{:S(2)}, u32[]{:S(2)}) collective-permute-start(bf16[128,896]{1,0:T(8,128)(2,1)S(1)} %get-tuple-element.43), channel_id=1, source_target_pairs={{0,34},{1,35},{2,32},{3,33},{32,2},{33,3},{34,0},{35,1},{4,38},{5,... | collective-permute-start | bytes 688136 | tf_op jit(solution)/shard_map/ppermute | solution.py:182
  145.9 41.1 %collective-permute-start.22 = (bf16[128,896]{1,0:T(8,128)(2,1)S(1)}, bf16[128,896]{1,0:T(8,128)(2,1)S(1)}, u32[]{:S(2)}, u32[]{:S(2)}) collective-permute-start(bf16[128,896]{1,0:T(8,128)(2,1)S(1)} %get-tuple-element.42), channel_id=1, source_target_pairs={{0,35},{1,32},{2,33},{3,34},{32,3},{33,0},{34,1},{35,2},{4,39},{5,... | collective-permute-start | bytes 688136 | tf_op jit(solution)/shard_map/ppermute | solution.py:182
  164.8 28.8 %collective-permute-start.9 = (bf16[128,896]{1,0:T(8,128)(2,1)S(1)}, bf16[128,896]{1,0:T(8,128)(2,1)S(1)}, u32[]{:S(2)}, u32[]{:S(2)}) collective-permute-start(bf16[128,896]{1,0:T(8,128)(2,1)S(1)} %copy-done.6), channel_id=1, source_target_pairs={{0,3},{1,0},{2,1},{3,2},{4,7},{5,4},{6,5},{7,6},{8,11},{9,8},{10,9... | collective-permute-start | bytes 688136 | tf_op jit(solution)/shard_map/ppermute | solution.py:22
  172.1 21.5 %collective-permute-start.11 = (bf16[128,896]{1,0:T(8,128)(2,1)S(1)}, bf16[128,896]{1,0:T(8,128)(2,1)S(1)}, u32[]{:S(2)}, u32[]{:S(2)}) collective-permute-start(bf16[128,896]{1,0:T(8,128)(2,1)S(1)} %get-tuple-element.49), channel_id=1, source_target_pairs={{0,32},{1,33},{2,34},{3,35},{32,0},{33,1},{34,2},{35,3},{4,36},{5,... | collective-permute-start | bytes 688136 | tf_op jit(solution)/shard_map/ppermute | solution.py:182
  186.9 28.0 %collective-permute-start.12 = (bf16[128,896]{1,0:T(8,128)(2,1)S(1)}, bf16[128,896]{1,0:T(8,128)(2,1)S(1)}, u32[]{:S(2)}, u32[]{:S(2)}) collective-permute-start(bf16[128,896]{1,0:T(8,128)(2,1)S(1)} %get-tuple-element.48), channel_id=1, source_target_pairs={{0,33},{1,34},{2,35},{3,32},{32,1},{33,2},{34,3},{35,0},{4,37},{5,... | collective-permute-start | bytes 688136 | tf_op jit(solution)/shard_map/ppermute | solution.py:182
  188.6 26.4 %collective-permute-start.13 = (bf16[128,896]{1,0:T(8,128)(2,1)S(1)}, bf16[128,896]{1,0:T(8,128)(2,1)S(1)}, u32[]{:S(2)}, u32[]{:S(2)}) collective-permute-start(bf16[128,896]{1,0:T(8,128)(2,1)S(1)} %get-tuple-element.47), channel_id=1, source_target_pairs={{0,34},{1,35},{2,32},{3,33},{32,2},{33,3},{34,0},{35,1},{4,38},{5,... | collective-permute-start | bytes 688136 | tf_op jit(solution)/shard_map/ppermute | solution.py:182
  188.7 26.2 %collective-permute-start.14 = (bf16[128,896]{1,0:T(8,128)(2,1)S(1)}, bf16[128,896]{1,0:T(8,128)(2,1)S(1)}, u32[]{:S(2)}, u32[]{:S(2)}) collective-permute-start(bf16[128,896]{1,0:T(8,128)(2,1)S(1)} %get-tuple-element.46), channel_id=1, source_target_pairs={{0,35},{1,32},{2,33},{3,34},{32,3},{33,0},{34,1},{35,2},{4,39},{5,... | collective-permute-start | bytes 688136 | tf_op jit(solution)/shard_map/ppermute | solution.py:182
  192.4 22.5 %copy-start = (bf16[128,896]{1,0:T(8,128)(2,1)S(1)}, bf16[128,896]{1,0:T(8,128)(2,1)}, u32[]{:S(2)}) copy-start(bf16[128,896]{1,0:T(8,128)(2,1)} %get-tuple-element.19.refs_0_) | copy-start | bytes 688132
  192.4 34.8 %slice-start = ((s8[7340032]{0:T(1024)(128)(4,1)}), s8[4194304]{0:T(1024)(128)(4,1)S(1)}, s32[]{:S(2)}) async-start(s8[7340032]{0:T(1024)(128)(4,1)} %bitcast.46), calls=%async_computation | async-start | bytes 8388608
  215.0 12.3 %slice-start.1 = ((s8[7340032]{0:T(1024)(128)(4,1)}), s8[3145728]{0:T(1024)(128)(4,1)S(1)}, s32[]{:S(2)}) async-start(s8[7340032]{0:T(1024)(128)(4,1)} %bitcast.46), calls=%async_computation.1 | async-start | bytes 6291456
  218.2 40.4 %collective-permute-start.26 = (f32[2]{0:T(128)S(1)}, f32[2]{0:T(128)S(1)}, u32[]{:S(2)}, u32[]{:S(2)}) collective-permute-start(f32[2]{0:T(128)S(1)} %pad_maximum_fusion.2), channel_id=1, source_target_pairs={{0,1},{1,0},{2,3},{3,2},{4,5},{5,4},{6,7},{7,6},{8,9},{9,8},{10,11... | collective-permute-start | bytes 32 | tf_op jit(solution)/shard_map/ppermute | solution.py:27
  224.5 22.3 %collective-permute-start.30 = (bf16[1024,448]{0,1:T(8,128)(2,1)S(1)}, bf16[1024,448]{0,1:T(8,128)(2,1)S(1)}, u32[]{:S(2)}, u32[]{:S(2)}) collective-permute-start(bf16[1024,448]{0,1:T(8,128)(2,1)S(1)} %get-tuple-element.40), channel_id=1, source_target_pairs={{0,4},{4,8},{8,12},{12,0},{1,5},{5,9},{9,13},{13,1},{2,6},{6,10},{... | collective-permute-start | bytes 2752520 | tf_op jit(solution)/shard_map/ppermute | solution.py:22
  224.6 22.8 %collective-permute-start.32 = (bf16[1024,448]{0,1:T(8,128)(2,1)S(1)}, bf16[1024,448]{0,1:T(8,128)(2,1)S(1)}, u32[]{:S(2)}, u32[]{:S(2)}) collective-permute-start(bf16[1024,448]{0,1:T(8,128)(2,1)S(1)} %get-tuple-element.41), channel_id=1, source_target_pairs={{0,12},{4,0},{8,4},{12,8},{1,13},{5,1},{9,5},{13,9},{2,14},{6,2},{... | collective-permute-start | bytes 2752520 | tf_op jit(solution)/shard_map/ppermute | solution.py:22
  247.3 64.6 %collective-permute-start.31 = (bf16[2048,448]{0,1:T(8,128)(2,1)S(1)}, bf16[2048,448]{0,1:T(8,128)(2,1)S(1)}, u32[]{:S(2)}, u32[]{:S(2)}) collective-permute-start(bf16[2048,448]{0,1:T(8,128)(2,1)S(1)} %add_convert_fusion.1), channel_id=1, source_target_pairs={{0,4},{4,8},{8,12},{12,0},{1,5},{5,9},{9,13},{13,1},{2,6},{6,10},{... | collective-permute-start | bytes 5505032 | tf_op jit(solution)/shard_map/ppermute | solution.py:22
  248.6 63.3 %collective-permute-start.33 = (bf16[2048,448]{0,1:T(8,128)(2,1)S(1)}, bf16[2048,448]{0,1:T(8,128)(2,1)S(1)}, u32[]{:S(2)}, u32[]{:S(2)}) collective-permute-start(bf16[2048,448]{0,1:T(8,128)(2,1)S(1)} %add_convert_fusion), channel_id=1, source_target_pairs={{0,12},{4,0},{8,4},{12,8},{1,13},{5,1},{9,5},{13,9},{2,14},{6,2},{... | collective-permute-start | bytes 5505032 | tf_op jit(solution)/shard_map/ppermute | solution.py:22
  251.4 51.6 %collective-permute-start.23 = (bf16[128,2048]{1,0:T(8,128)(2,1)S(1)}, bf16[128,2048]{1,0:T(8,128)(2,1)S(1)}, u32[]{:S(2)}, u32[]{:S(2)}) collective-permute-start(bf16[128,2048]{1,0:T(8,128)(2,1)S(1)} %get-tuple-element.37), channel_id=1, source_target_pairs={{0,3},{1,0},{2,1},{3,2},{4,7},{5,4},{6,5},{7,6},{8,11},{9,8},{10,9... | collective-permute-start | bytes 1572872 | tf_op jit(solution)/shard_map/ppermute | solution.py:22
  258.6 44.5 %collective-permute-start.24 = (bf16[128,2048]{1,0:T(8,128)(2,1)S(1)}, bf16[128,2048]{1,0:T(8,128)(2,1)S(1)}, u32[]{:S(2)}, u32[]{:S(2)}) collective-permute-start(bf16[128,2048]{1,0:T(8,128)(2,1)S(1)} %get-tuple-element.39), channel_id=1, source_target_pairs={{0,2},{1,3},{2,0},{3,1},{4,6},{5,7},{6,4},{7,5},{8,10},{9,11},{10,... | collective-permute-start | bytes 1572872 | tf_op jit(solution)/shard_map/ppermute | solution.py:22
  258.6 31.9 %collective-permute-start.27 = (f32[2]{0:T(128)S(1)}, f32[2]{0:T(128)S(1)}, u32[]{:S(2)}, u32[]{:S(2)}) collective-permute-start(f32[2]{0:T(128)S(1)} %fusion.28), channel_id=1, source_target_pairs={{0,2},{1,3},{2,0},{3,1},{4,6},{5,7},{6,4},{7,5},{8,10},{9,11},{10,... | collective-permute-start | bytes 32 | tf_op jit(solution)/shard_map/ppermute | solution.py:27
  290.6 2.4 collective-permute-start.28
  293.1 3.9 %collective-permute-start.29 = (f32[2]{0:T(128)S(1)}, f32[2]{0:T(128)S(1)}, u32[]{:S(2)}, u32[]{:S(2)}) collective-permute-start(f32[2]{0:T(128)S(1)} %add.84), channel_id=1, source_target_pairs={{0,8},{4,12},{8,0},{12,4},{1,9},{5,13},{9,1},{13,5},{2,10},{6,14},... | collective-permute-start | bytes 32 | tf_op jit(solution)/shard_map/ppermute | solution.py:27
  297.0 13.7 %collective-permute-start.25 = (bf16[128,2048]{1,0:T(8,128)(2,1)S(1)}, bf16[128,2048]{1,0:T(8,128)(2,1)S(1)}, u32[]{:S(2)}, u32[]{:S(2)}) collective-permute-start(bf16[128,2048]{1,0:T(8,128)(2,1)S(1)} %get-tuple-element.38), channel_id=1, source_target_pairs={{0,1},{1,2},{2,3},{3,0},{4,5},{5,6},{6,7},{7,4},{8,9},{9,10},{10,1... | collective-permute-start | bytes 1572872 | tf_op jit(solution)/shard_map/ppermute | solution.py:22
